TPU v7x, 32 devices: a whole 2x2x4 slice. The times are simulated.
32 devices in a mesh: wide: 8 (over y, x, core), narrow: 4 (over z).
Axes of the slice: x: 2, y: 2, z: 4, core: 2. Of those that a mesh axis runs over, the one named last changes fastest.
Arguments:
- tokens: bfloat16 [64, 512, 512], P(('wide', 'narrow')), may hold values from -6 to 6
- seg_ids: int32 [64, 512], P(('wide', 'narrow')), may hold values from 0 to 7, as said below
- positives: int32 [256], replicated, may hold values from 0 to 63
- norm1_gain: bfloat16 [512], replicated, may hold values from 0.5 to 1.5
- w_query: bfloat16 [512, 512], replicated, may hold values from -0.0625 to 0.0625
- w_key: bfloat16 [512, 512], replicated, may hold values from -0.25 to 0.25
- w_value: bfloat16 [512, 512], replicated, may hold values from -0.25 to 0.25
- w_attn_out: bfloat16 [512, 512], replicated, may hold values from -1 to 1
- rel_bias: bfloat16 [32, 8], replicated, may hold values from -4 to 4
- norm2_gain: bfloat16 [512], replicated, may hold values from 0.5 to 1.5
- w_in: bfloat16 [512, 2048], replicated, may hold values from -0.25 to 0.25
- w_ffn_out: bfloat16 [2048, 512], replicated, may hold values from -0.1875 to 0.1875
- w_proj: bfloat16 [512, 512], replicated, may hold values from -0.25 to 0.25
Outputs:
- loss: float32 [], replicated
- tokens_grad: bfloat16 [64, 512, 512], P(('wide', 'narrow'))
- norm1_gain_grad: float32 [512], replicated
- w_query_grad: float32 [512, 512], replicated
- w_key_grad: float32 [512, 512], replicated
- w_value_grad: float32 [512, 512], replicated
- w_attn_out_grad: float32 [512, 512], replicated
- rel_bias_grad: float32 [32, 8], replicated
- norm2_gain_grad: float32 [512], replicated
- w_in_grad: float32 [512, 2048], replicated
- w_ffn_out_grad: float32 [2048, 512], replicated
- w_proj_grad: float32 [512, 512], replicated
Inputs may be any that keep to these rules, and one draw needn't show every extreme that they name: `seg_ids`: each row of the first half holds 8 queries of 64 tokens, numbered 0 to 7 in order. Each row of the second half holds passage 0 and then passage 1, each of 64 to 448 tokens; the first such row has a passage 0 of exactly 448 tokens. `positives`: passages are numbered by row of the second half and then by their number within the row.
All inputs are finite; a program needn't handle non-finite values.
Results may differ from a plain program's by a relative error of at most 0.04.
The roundings to bfloat16 on the way count: a program that leaves them out, or rounds other values in their place, can miss the bound.
Values may be sent and summed in bfloat16 or wider, within the bound.
No kernel may reach another device: no remote copies, remote signals or barrier semaphores. Data moves between devices by JAX's collectives and lax.ppermute only.
A program may use at most 192 MiB of HBM per device.

v0:
```python
import jax
import jax.numpy as jnp
import numpy as np
from jax import lax
from jax.sharding import PartitionSpec as P

NB = 32
MAXD = 128
QLEN = 64
PPR = 2


EPS_NORM = 1e-06
LOGIT_SCALE = 50.0
MASKED = -1e30
HIGHEST = lax.Precision.HIGHEST
F32 = jnp.float32
BF16 = jnp.bfloat16


def bucket_offsets(length):
    offset = np.arange(-(length - 1), length)
    half_count = NB // 2
    exact_span = half_count // 2
    distance = -offset
    bucket = (distance < 0).astype(np.int64) * half_count
    distance = np.abs(distance)
    far_bucket = exact_span + (
        np.log(np.maximum(distance, 1) / exact_span)
        / np.log(MAXD / exact_span)
        * (half_count - exact_span)
    ).astype(np.int64)
    far_bucket = np.minimum(far_bucket, half_count - 1)
    bucket = bucket + np.where(distance < exact_span, distance, far_bucket)
    return bucket.astype(np.int32)


def toeplitz_rows(values, length):
    lead_shape = values.shape[:-1]
    tiled_values = jnp.tile(values, (1,) * len(lead_shape) + (length + 1,))
    start_at = length - 1
    window = tiled_values[..., start_at : start_at + length * (2 * length - 2)]
    return window.reshape(lead_shape + (length, 2 * length - 2))[..., :length]


def contract(left, right, left_dim, right_dim):
    return lax.dot_general(
        left, right, (((left_dim,), (right_dim,)), ((), ())), preferred_element_type=F32
    )


def rms_scale(values):
    return lax.rsqrt(jnp.mean(values * values, axis=-1, keepdims=True) + EPS_NORM)


def norm_back(grad_normed, inputs, scale, gain):
    scaled = grad_normed * gain
    return scale * scaled - inputs * scale**3 * jnp.mean(inputs * scaled, axis=-1, keepdims=True)


def score_block(queries, keys_rows, bias_full, same_seg):
    scores = jnp.einsum("ihd,jhd->hij", queries, keys_rows, preferred_element_type=F32) + bias_full
    return jnp.where(same_seg[None], scores, MASKED)


def local(
    tokens,
    seg_ids,
    positives,
    norm1_gain,
    w_query,
    w_key,
    w_value,
    w_attn_out,
    rel_bias,
    norm2_gain,
    w_in,
    w_ffn_out,
    w_proj,
):
    row_count, length, model_width = tokens.shape
    bucket_count, head_count = rel_bias.shape
    head_size = model_width // head_count
    slot_count = length // QLEN
    linear = lax.axis_index("wide") * lax.axis_size("narrow") + lax.axis_index("narrow")
    is_query = lax.axis_index("wide") < lax.axis_size("wide") // 2
    query_flag = is_query.astype(F32)
    gain_one = norm1_gain.astype(F32)
    gain_two = norm2_gain.astype(F32)
    offset_table = jnp.asarray(bucket_offsets(length))
    bucket_ids = jnp.arange(bucket_count, dtype=jnp.int32)
    offset_onehot = (offset_table[:, None] == bucket_ids[None, :]).astype(F32)
    offset_bias = jnp.dot(offset_onehot, rel_bias.astype(F32), precision=HIGHEST).T
    bias_full = toeplitz_rows(offset_bias, length)
    slot_ids = jnp.arange(slot_count, dtype=jnp.int32)
    stored = []
    embedded_rows = []
    for row_index in range(row_count):
        row_input = tokens[row_index].astype(F32)
        seg_row = seg_ids[row_index]
        scale_one = rms_scale(row_input)
        normed_one = (row_input * scale_one * gain_one).astype(BF16)
        queries = (
            jnp.dot(normed_one, w_query, preferred_element_type=F32)
            .astype(BF16)
            .reshape(length, head_count, head_size)
        )
        keys_rows = (
            jnp.dot(normed_one, w_key, preferred_element_type=F32)
            .astype(BF16)
            .reshape(length, head_count, head_size)
        )
        values_rows = (
            jnp.dot(normed_one, w_value, preferred_element_type=F32)
            .astype(BF16)
            .reshape(length, head_count, head_size)
        )
        same_seg = seg_row[:, None] == seg_row[None, :]
        scores = score_block(queries, keys_rows, bias_full, same_seg)
        row_top = jnp.max(scores, axis=-1, keepdims=True)
        exp_scores = jnp.exp(scores - row_top)
        row_total = jnp.sum(exp_scores, axis=-1, keepdims=True)
        attn_probs = exp_scores / row_total
        log_total = row_top + jnp.log(row_total)
        attn_mixed = jnp.einsum(
            "hij,jhd->ihd", attn_probs.astype(BF16), values_rows, preferred_element_type=F32
        )
        attn_mixed = attn_mixed.reshape(length, model_width).astype(BF16)
        hidden = row_input + jnp.dot(attn_mixed, w_attn_out, preferred_element_type=F32)
        scale_two = rms_scale(hidden)
        normed_two = (hidden * scale_two * gain_two).astype(BF16)
        ffn_inner = jnp.dot(normed_two, w_in, preferred_element_type=F32)
        active = jnp.where(ffn_inner > 0, ffn_inner, 0.0).astype(BF16)
        output = hidden + jnp.dot(active, w_ffn_out, preferred_element_type=F32)
        slot_mask = (seg_row[None, :] == slot_ids[:, None]).astype(F32)
        counts = jnp.maximum(jnp.sum(slot_mask, axis=-1, keepdims=True), 1.0)
        pooled = (jnp.dot(slot_mask, output, precision=HIGHEST) / counts).astype(BF16)
        projected = jnp.dot(pooled, w_proj, preferred_element_type=F32)
        inv_norm = lax.rsqrt(jnp.sum(projected * projected, axis=-1, keepdims=True) + EPS_NORM)
        embedded_rows.append((projected * inv_norm).astype(BF16))
        stored.append(
            (
                row_input,
                same_seg,
                scale_one,
                normed_one,
                queries,
                keys_rows,
                values_rows,
                log_total,
                attn_mixed,
                hidden,
                scale_two,
                normed_two,
                ffn_inner,
                active,
                slot_mask,
                counts,
                pooled,
                projected,
                inv_norm,
            )
        )
    emb_local = jnp.concatenate(embedded_rows, axis=0)
    own_count = row_count * slot_count
    gathered = lax.all_gather(emb_local, ("wide", "narrow"), axis=0, tiled=True)
    half_rows = gathered.shape[0] // (2 * slot_count)
    proj_width = gathered.shape[1]
    passage_all = (
        gathered[half_rows * slot_count :]
        .reshape(half_rows, slot_count, proj_width)[:, :PPR]
        .reshape(half_rows * PPR, proj_width)
    )
    passage_count = half_rows * PPR
    query_start = linear * own_count
    passage_ids = jnp.arange(passage_count, dtype=jnp.int32)
    targets = lax.dynamic_slice_in_dim(positives, query_start, own_count)
    logits = LOGIT_SCALE * contract(emb_local, passage_all, 1, 1)
    row_top = jnp.max(logits, axis=-1, keepdims=True)
    loss_log_total = row_top + jnp.log(jnp.sum(jnp.exp(logits - row_top), axis=-1, keepdims=True))
    pos_hits = (targets[:, None] == passage_ids[None, :]).astype(F32)
    per_query = loss_log_total[:, 0] - jnp.sum(logits * pos_hits, axis=-1)
    weights = (jnp.exp(logits - loss_log_total) - pos_hits).astype(BF16)
    per_query, weights = (per_query, weights)
    loss_part = query_flag * jnp.sum(per_query)
    query_grad = LOGIT_SCALE * jnp.dot(weights, passage_all, preferred_element_type=F32)
    passage_part = LOGIT_SCALE * query_flag * contract(weights, emb_local, 0, 0)
    operand = jnp.concatenate([jnp.zeros_like(passage_part), passage_part], axis=0)
    received = lax.psum_scatter(operand, ("wide", "narrow"), scatter_dimension=0, tiled=True)
    passage_slots = jnp.concatenate(
        [
            received.reshape(row_count, PPR, proj_width),
            jnp.zeros((row_count, slot_count - PPR, proj_width), F32),
        ],
        axis=1,
    ).reshape(own_count, proj_width)
    emb_grad = jnp.where(is_query, query_grad, passage_slots)
    grad_proj = jnp.zeros(w_proj.shape, F32)
    grad_ffn_out = jnp.zeros(w_ffn_out.shape, F32)
    grad_in = jnp.zeros(w_in.shape, F32)
    grad_gain_two = jnp.zeros((model_width,), F32)
    hidden_grads = []
    for row_index in range(row_count):
        (
            row_input,
            same_seg,
            scale_one,
            normed_one,
            queries,
            keys_rows,
            values_rows,
            log_total,
            attn_mixed,
            hidden,
            scale_two,
            normed_two,
            ffn_inner,
            active,
            slot_mask,
            counts,
            pooled,
            projected,
            inv_norm,
        ) = stored[row_index]
        emb_row_grad = emb_grad[row_index * slot_count : (row_index + 1) * slot_count]
        proj_grad = inv_norm * emb_row_grad - projected * inv_norm**3 * jnp.sum(
            emb_row_grad * projected, axis=-1, keepdims=True
        )
        proj_low = proj_grad.astype(BF16)
        grad_proj = grad_proj + contract(pooled, proj_low, 0, 0)
        pooled_grad = contract(proj_low, w_proj, 1, 1)
        out_grad = lax.dot_general(
            slot_mask, pooled_grad / counts, (((0,), (0,)), ((), ())), precision=HIGHEST
        )
        ffn_out_low = out_grad.astype(BF16)
        grad_ffn_out = grad_ffn_out + contract(active, ffn_out_low, 0, 0)
        active_grad = contract(ffn_out_low, w_ffn_out, 1, 1)
        inner_grad = jnp.where(ffn_inner > 0, active_grad, 0.0).astype(BF16)
        grad_in = grad_in + contract(normed_two, inner_grad, 0, 0)
        normed_two_grad = contract(inner_grad, w_in, 1, 1)
        grad_gain_two = grad_gain_two + jnp.sum(normed_two_grad * hidden * scale_two, axis=0)
        hidden_grads.append(out_grad + norm_back(normed_two_grad, hidden, scale_two, gain_two))
    grad_query = jnp.zeros(w_query.shape, F32)
    grad_key = jnp.zeros(w_key.shape, F32)
    grad_value = jnp.zeros(w_value.shape, F32)
    grad_attn_out = jnp.zeros(w_attn_out.shape, F32)
    score_grad_sum = jnp.zeros((head_count, length, length), F32)
    grad_gain_one = jnp.zeros((model_width,), F32)
    token_grads = []
    for row_index in range(row_count):
        (
            row_input,
            same_seg,
            scale_one,
            normed_one,
            queries,
            keys_rows,
            values_rows,
            log_total,
            attn_mixed,
            hidden,
            scale_two,
            normed_two,
            ffn_inner,
            active,
            slot_mask,
            counts,
            pooled,
            projected,
            inv_norm,
        ) = stored[row_index]
        hidden_grad = hidden_grads[row_index]
        attn_low = hidden_grad.astype(BF16)
        grad_attn_out = grad_attn_out + contract(attn_mixed, attn_low, 0, 0)
        mixed_grad = (
            contract(attn_low, w_attn_out, 1, 1).astype(BF16).reshape(length, head_count, head_size)
        )
        attn_probs = jnp.exp(score_block(queries, keys_rows, bias_full, same_seg) - log_total)
        values_grad = (
            jnp.einsum(
                "hij,ihd->jhd", attn_probs.astype(BF16), mixed_grad, preferred_element_type=F32
            )
            .astype(BF16)
            .reshape(length, model_width)
        )
        probs_grad = jnp.einsum("ihd,jhd->hij", mixed_grad, values_rows, preferred_element_type=F32)
        score_grad = (
            attn_probs * (probs_grad - jnp.sum(attn_probs * probs_grad, axis=-1, keepdims=True))
        ).astype(BF16)
        queries_grad = (
            jnp.einsum("hij,jhd->ihd", score_grad, keys_rows, preferred_element_type=F32)
            .astype(BF16)
            .reshape(length, model_width)
        )
        keys_grad = (
            jnp.einsum("hij,ihd->jhd", score_grad, queries, preferred_element_type=F32)
            .astype(BF16)
            .reshape(length, model_width)
        )
        score_grad_sum = score_grad_sum + score_grad.astype(F32)
        grad_query = grad_query + contract(normed_one, queries_grad, 0, 0)
        grad_key = grad_key + contract(normed_one, keys_grad, 0, 0)
        grad_value = grad_value + contract(normed_one, values_grad, 0, 0)
        normed_one_grad = (
            contract(queries_grad, w_query, 1, 1)
            + contract(keys_grad, w_key, 1, 1)
            + contract(values_grad, w_value, 1, 1)
        )
        grad_gain_one = grad_gain_one + jnp.sum(normed_one_grad * row_input * scale_one, axis=0)
        token_grads.append(
            (hidden_grad + norm_back(normed_one_grad, row_input, scale_one, gain_one)).astype(BF16)
        )
    pair_bucket = toeplitz_rows(offset_table[None, :], length)[0]
    pair_onehot = (bucket_ids[:, None] == pair_bucket.reshape(1, length * length)).astype(F32)
    grad_bias = lax.dot_general(
        score_grad_sum.reshape(head_count, length * length),
        pair_onehot,
        (((1,), (1,)), ((), ())),
        precision=HIGHEST,
    )
    sum_query, sum_key, sum_value, sum_attn_out, sum_in, sum_ffn_out, sum_proj = (
        lax.psum_scatter(
            grad_query.reshape(-1), ("wide", "narrow"), scatter_dimension=0, tiled=True
        ),
        lax.psum_scatter(grad_key.reshape(-1), ("wide", "narrow"), scatter_dimension=0, tiled=True),
        lax.psum_scatter(
            grad_value.reshape(-1), ("wide", "narrow"), scatter_dimension=0, tiled=True
        ),
        lax.psum_scatter(
            grad_attn_out.reshape(-1), ("wide", "narrow"), scatter_dimension=0, tiled=True
        ),
        lax.psum_scatter(grad_in.reshape(-1), ("wide", "narrow"), scatter_dimension=0, tiled=True),
        lax.psum_scatter(
            grad_ffn_out.reshape(-1), ("wide", "narrow"), scatter_dimension=0, tiled=True
        ),
        lax.psum_scatter(
            grad_proj.reshape(-1), ("wide", "narrow"), scatter_dimension=0, tiled=True
        ),
    )
    total_query, total_key, total_value, total_attn_out, total_in, total_ffn_out, total_proj = (
        lax.all_gather(
            sum_query.astype(jnp.bfloat16), ("wide", "narrow"), axis=0, tiled=True
        ).astype(sum_query.dtype),
        lax.all_gather(sum_key.astype(jnp.bfloat16), ("wide", "narrow"), axis=0, tiled=True).astype(
            sum_key.dtype
        ),
        lax.all_gather(
            sum_value.astype(jnp.bfloat16), ("wide", "narrow"), axis=0, tiled=True
        ).astype(sum_value.dtype),
        lax.all_gather(
            sum_attn_out.astype(jnp.bfloat16), ("wide", "narrow"), axis=0, tiled=True
        ).astype(sum_attn_out.dtype),
        lax.all_gather(sum_in.astype(jnp.bfloat16), ("wide", "narrow"), axis=0, tiled=True).astype(
            sum_in.dtype
        ),
        lax.all_gather(
            sum_ffn_out.astype(jnp.bfloat16), ("wide", "narrow"), axis=0, tiled=True
        ).astype(sum_ffn_out.dtype),
        lax.all_gather(
            sum_proj.astype(jnp.bfloat16), ("wide", "narrow"), axis=0, tiled=True
        ).astype(sum_proj.dtype),
    )
    loss_total, total_gain_one, total_gain_two, total_bias = lax.psum(
        (loss_part, grad_gain_one, grad_gain_two, grad_bias), ("wide", "narrow")
    )
    tokens_grad = jnp.stack(token_grads, axis=0)
    return (
        loss_total,
        tokens_grad,
        total_gain_one,
        total_query.reshape(w_query.shape),
        total_key.reshape(w_key.shape),
        total_value.reshape(w_value.shape),
        total_attn_out.reshape(w_attn_out.shape),
        total_bias.T,
        total_gain_two,
        total_in.reshape(w_in.shape),
        total_ffn_out.reshape(w_ffn_out.shape),
        total_proj.reshape(w_proj.shape),
    )


def solution(mesh):
    in_specs = (
        P(("wide", "narrow"), None, None),
        P(("wide", "narrow"), None),
        P(),
        P(),
        P(),
        P(),
        P(),
        P(),
        P(),
        P(),
        P(),
        P(),
        P(),
    )
    out_specs = (
        P(),
        P(("wide", "narrow"), None, None),
        P(),
        P(),
        P(),
        P(),
        P(),
        P(),
        P(),
        P(),
        P(),
        P(),
    )
    return jax.shard_map(local, mesh=mesh, in_specs=in_specs, out_specs=out_specs, check_vma=False)
```

profile of v0, /device:TPU:0, one launch (start us, length us, event | category | flops | bytes accessed | tf_op | source)
XLA Modules:
  0.0 1305.2 jit_solution(8156129899407925416)
XLA Ops:
  33.7 211.6 %while.1 = (u32[]{:T(128)}, f32[8,513,1023]{2,1,0:T(8,128)}, f32[4198392]{0:T(1024)}, u32[]{}, u32[]{}, /*index=5*/u32[]{}, u32[]{}) while((u32[]{:T(128)}, f32[8,513,1023]{2,1,0:T(8,128)}, f32[4198392]{0:T(1024)}, u32[]{}, u32[]{}, /*index=5*/u32[]{}, u32[]{}) %tuple.60), condition=%wide.cond, body=%wide.body.sunk | while | flops 9 | bytes 12595357
  41.4 19.0 %dynamic-update-slice.2 = f32[4198392]{0:T(1024)} dynamic-update-slice(f32[4198392]{0:T(1024)} %get-tuple-element.177, f32[524799]{0:T(1024)} %reshape.518, u32[]{:T(128)S(6)} %add.320) | dynamic-update-slice | bytes 4198396
  67.8 19.0 %dynamic-update-slice.2 = f32[4198392]{0:T(1024)} dynamic-update-slice(f32[4198392]{0:T(1024)} %get-tuple-element.177, f32[524799]{0:T(1024)} %reshape.518, u32[]{:T(128)S(6)} %add.320) | dynamic-update-slice | bytes 4198396
  94.2 19.0 %dynamic-update-slice.2 = f32[4198392]{0:T(1024)} dynamic-update-slice(f32[4198392]{0:T(1024)} %get-tuple-element.177, f32[524799]{0:T(1024)} %reshape.518, u32[]{:T(128)S(6)} %add.320) | dynamic-update-slice | bytes 4198396
  120.6 19.0 %dynamic-update-slice.2 = f32[4198392]{0:T(1024)} dynamic-update-slice(f32[4198392]{0:T(1024)} %get-tuple-element.177, f32[524799]{0:T(1024)} %reshape.518, u32[]{:T(128)S(6)} %add.320) | dynamic-update-slice | bytes 4198396
  147.0 19.0 %dynamic-update-slice.2 = f32[4198392]{0:T(1024)} dynamic-update-slice(f32[4198392]{0:T(1024)} %get-tuple-element.177, f32[524799]{0:T(1024)} %reshape.518, u32[]{:T(128)S(6)} %add.320) | dynamic-update-slice | bytes 4198396
  173.5 19.1 %dynamic-update-slice.2 = f32[4198392]{0:T(1024)} dynamic-update-slice(f32[4198392]{0:T(1024)} %get-tuple-element.177, f32[524799]{0:T(1024)} %reshape.518, u32[]{:T(128)S(6)} %add.320) | dynamic-update-slice | bytes 4198396
  200.0 19.1 %dynamic-update-slice.2 = f32[4198392]{0:T(1024)} dynamic-update-slice(f32[4198392]{0:T(1024)} %get-tuple-element.177, f32[524799]{0:T(1024)} %reshape.518, u32[]{:T(128)S(6)} %add.320) | dynamic-update-slice | bytes 4198396
  226.5 18.9 %dynamic-update-slice.2 = f32[4198392]{0:T(1024)} dynamic-update-slice(f32[4198392]{0:T(1024)} %get-tuple-element.177, f32[524799]{0:T(1024)} %reshape.518, u32[]{:T(128)S(6)} %add.320) | dynamic-update-slice | bytes 4198396
  245.3 20.6 %tile.18 = f32[8,524799]{1,0:T(8,128)} reshape(f32[4198392]{0:T(1024)} %get-tuple-element.64) | data formatting | bytes 33587136 | tf_op jit(solution)/shard_map/tile | solution.py:40
  265.9 12.9 slice.48
  278.8 13.9 %reshape.515 = f32[4186112]{0:T(1024)} reshape(f32[8,523264]{1,0:T(8,128)} %slice.48) | data formatting | bytes 33488896
  292.7 18.2 %reshape.451 = f32[8,512,1022]{2,1,0:T(8,128)} reshape(f32[4186112]{0:T(1024)} %reshape.515) | data formatting | bytes 33488896 | tf_op jit(solution)/shard_map/reshape | solution.py:43
  357.7 73.9 %all_gather.24 = bf16[512,512]{1,0:T(8,128)(2,1)S(1)} all-gather(bf16[16,512]{1,0:T(8,128)(2,1)S(1)} %pad_maximum_fusion.1), channel_id=1, replica_groups=mesh['wide'=8,'narrow'=4] {'wide','narrow'}, dimensions={0}, use_global_device_ids=true | all-gather | bytes 540672 | tf_op jit(solution)/shard_map/all_gather | solution.py:166
  441.9 24.4 %slice_reduce_fusion = s32[523264]{0:T(1024)} fusion(s32[1,524799]{1,0:T(1,128)} %tile.20), kind=kLoop, calls=%fused_computation.36 | loop fusion | bytes 4186112 | tf_op jit(solution)/shard_map/slice | solution.py:42
  474.0 83.0 %all-reduce.14.cloned.1.call-done = f32[128,512]{1,0:T(8,128)} async-done(((f32[128,512]{1,0:T(8,128)}), f32[128,512]{1,0:T(8,128)}) %all-reduce.14.cloned.1.call-update) | async-done | bytes 262160
  608.8 18.5 %convert_add_fusion = (f32[8,512,512]{1,2,0:T(8,128)}, bf16[8,512,512]{1,2,0:T(8,128)(2,1)}, bf16[8,512,512]{1,2,0:T(8,128)(2,1)}) fusion(f32[8,512,512]{1,2,0:T(8,128)} %get-tuple-element.141, f32[8,512]{1,0:T(8,128)S(1)} %get-tuple-element.140, f32[8,512,512]{1,2,0:T(8,128)} %copy-done.2, f32[8,512]{1,0:T(8,128)S(1)} %get-tuple-element.147, ...), kind=kLoop, calls=%fused_computation.3 | loop fusion | flops 23068672 | bytes 50397184 | tf_op jit(solution)/shard_map/add | solution.py:300
  678.5 16.1 %fusion = f32[32,8]{0,1:T(8,128)S(1)} fusion(f32[8,262144]{1,0:T(8,128)S(1)} %bitcast.251, s32[262144]{0:T(1024)S(1)} %bitcast.285), kind=kOutput, calls=%fused_computation.1 | convolution fusion | flops 813694976 | bytes 9438208 | tf_op jit(solution)/shard_map/dot_general | solution.py:315
  696.4 230.0 %all-reduce.15 = (bf16[262144]{0:T(1024)(128)(2,1)}, bf16[262144]{0:T(1024)(128)(2,1)}, bf16[262144]{0:T(1024)(128)(2,1)}, bf16[262144]{0:T(1024)(128)(2,1)}, bf...) all-reduce(f32[262144]{0:T(1024)} %bitcast.272, ...), channel_id=3, replica_groups=mesh['wide'=8,'narrow'=4] {'wide','narrow'}, use_global_device_ids=true, to_apply=%region_29.30.clone | all-reduce | flops 3409153 | bytes 20457480
  936.6 70.3 %all_gather.25 = bf16[262144]{0:T(1024)(128)(2,1)S(1)} all-gather(bf16[8192]{0:T(1024)(128)(2,1)S(1)} %dynamic-slice.23), channel_id=1, replica_groups=mesh['wide'=8,'narrow'=4] {'wide','narrow'}, dimensions={0}, use_global_device_ids=true | all-gather | bytes 540672 | tf_op jit(solution)/shard_map/all_gather | solution.py:341
  1008.1 69.5 %all_gather.26 = bf16[262144]{0:T(1024)(128)(2,1)S(1)} all-gather(bf16[8192]{0:T(1024)(128)(2,1)S(1)} %dynamic-slice.22), channel_id=1, replica_groups=mesh['wide'=8,'narrow'=4] {'wide','narrow'}, dimensions={0}, use_global_device_ids=true | all-gather | bytes 540672 | tf_op jit(solution)/shard_map/all_gather | solution.py:344
  1078.9 69.3 %all_gather.27 = bf16[262144]{0:T(1024)(128)(2,1)S(1)} all-gather(bf16[8192]{0:T(1024)(128)(2,1)S(1)} %dynamic-slice.21), channel_id=1, replica_groups=mesh['wide'=8,'narrow'=4] {'wide','narrow'}, dimensions={0}, use_global_device_ids=true | all-gather | bytes 540672 | tf_op jit(solution)/shard_map/all_gather | solution.py:347
  1149.4 68.1 %all_gather.28 = bf16[262144]{0:T(1024)(128)(2,1)S(1)} all-gather(bf16[8192]{0:T(1024)(128)(2,1)S(1)} %dynamic-slice.20), channel_id=1, replica_groups=mesh['wide'=8,'narrow'=4] {'wide','narrow'}, dimensions={0}, use_global_device_ids=true | all-gather | bytes 540672 | tf_op jit(solution)/shard_map/all_gather | solution.py:350
  1218.8 69.2 %all_gather.31 = bf16[262144]{0:T(1024)(128)(2,1)S(1)} all-gather(bf16[8192]{0:T(1024)(128)(2,1)S(1)} %dynamic-slice.19), channel_id=1, replica_groups=mesh['wide'=8,'narrow'=4] {'wide','narrow'}, dimensions={0}, use_global_device_ids=true | all-gather | bytes 540672 | tf_op jit(solution)/shard_map/all_gather | solution.py:359
  (327 shorter events, 279.4 us)
Async XLA Ops:
  7.2 341.4 %copy-start = (bf16[512,2048]{1,0:T(8,128)(2,1)S(1)}, bf16[512,2048]{1,0:T(8,128)(2,1)}, u32[]{:S(2)}) copy-start(bf16[512,2048]{1,0:T(8,128)(2,1)} %param.24) | copy-start | bytes 6291460
  7.2 549.8 %all-reduce.14.cloned.1.call-start = ((), (), s32[]{:S(2)}) async-start(), calls=%async_computation.2 | async-start | bytes 524288
  10.2 13.9 %copy-start.61 = (f32[512]{0:T(512)}, f32[512]{0:T(512)S(1)}, u32[]{:S(2)}) copy-start(f32[512]{0:T(512)S(1)} %convert_element_type.250) | copy-start | bytes 6148
  13.2 10.8 copy-start.63
  14.5 6.9 copy-start.52
  14.6 8.0 copy-start.54
  15.2 8.8 copy-start.65
  339.3 15.4 %copy-start.11 = (f32[512,512]{0,1:T(8,128)}, f32[512,512]{0,1:T(8,128)S(1)}, u32[]{:S(2)}) copy-start(f32[512,512]{0,1:T(8,128)S(1)} %get-tuple-element.132) | copy-start | bytes 3145732
  354.8 77.3 %copy-start.72 = (s32[256]{0:T(256)S(1)}, s32[256]{0:T(256)}, u32[]{:S(2)}) copy-start(s32[256]{0:T(256)} %param.16) | copy-start | bytes 3076
  433.9 855.3 %all-gather.3.cloned.1.call-start = ((), (), s32[]{:S(2)}) async-start(), calls=%async_computation | async-start | bytes 2162688 | tf_op jit(solution)/shard_map/all_gather | solution.py:353
  564.9 5.9 copy-start.17
  587.7 7.1 slice-start
  594.9 7.3 slice-start.2
  603.6 48.9 %copy-start.27 = (bf16[8,64,512]{2,1,0:T(8,128)(2,1)}, bf16[8,64,512]{2,1,0:T(8,128)(2,1)S(1)}, u32[]{:S(2)}) copy-start(bf16[8,64,512]{2,1,0:T(8,128)(2,1)S(1)} %fusion.35) | copy-start | bytes 1572868
  627.2 6.4 copy-start.8
  627.3 6.4 copy-start.43
  664.2 8.4 copy-start.30
  664.2 8.9 copy-start.29
  678.4 16.2 %copy-start.19 = (f32[512,512]{0,1:T(8,128)}, f32[512,512]{0,1:T(8,128)S(1)}, u32[]{:S(2)}) copy-start(f32[512,512]{0,1:T(8,128)S(1)} %convolution_add_fusion.2) | copy-start | bytes 3145732
  678.5 16.1 %copy-start.33 = (bf16[8,64,512]{2,1,0:T(8,128)(2,1)S(1)}, bf16[8,64,512]{2,1,0:T(8,128)(2,1)}, u32[]{:S(2)}) copy-start(bf16[8,64,512]{2,1,0:T(8,128)(2,1)} %fusion.38) | copy-start | bytes 1572868
  696.4 233.0 %copy-start.67 = (f32[512]{0:T(512)S(1)}, f32[512]{0:T(512)}, u32[]{:S(2)}) copy-start(f32[512]{0:T(512)} %get-tuple-element.109) | copy-start | bytes 6148
  696.4 233.0 %copy-start.68 = (f32[512]{0:T(512)S(1)}, f32[512]{0:T(512)}, u32[]{:S(2)}) copy-start(f32[512]{0:T(512)} %get-tuple-element.107) | copy-start | bytes 6148
  927.8 366.0 %all-gather.5.cloned.1.call-start = ((), (), s32[]{:S(2)}) async-start(), calls=%async_computation.1 | async-start | bytes 2162688 | tf_op jit(solution)/shard_map/all_gather | solution.py:356
  1289.2 9.3 copy-start.1
  (58 other events, 190.2 us)
Sparse Core Ops, SparseCore 0:
  434.1 122.9 all-reduce.13
  928.0 55.0 all-gather.2
  986.0 55.6 all-gather.4
where the time goes:
time: 1320 us; the launch traced here: 1310 us
  blocking collectives  650 us (49%)
  local copies, waits for them, and re-layouts  417 us (32%)
  matrix products  110 us (8%)
  waiting for transfers between devices  83.1 us (6%)
  other arithmetic  28.4 us (2%)
  between operations  15.7 us (1%)
    unnamed x205, local copies, waits for them, and re-layouts  280 us
    unnamed x1, blocking collectives  230 us
    unnamed x4, waiting for transfers between devices  83.1 us
    all_gather x1, blocking collectives, local(): gathered = lax.all_gather(emb_local, ('wide', 'narrow'), axis=0, tiled=True)  73.9 us
    all_gather x1, blocking collectives, local(): lax.all_gather(sum_query.astype(jnp.bfloat16), ('wide', 'narrow'), axis=0...  70.3 us
    all_gather x1, blocking collectives, local(): lax.all_gather(sum_key.astype(jnp.bfloat16), ('wide', 'narrow'), axis=0,...  69.5 us
    all_gather x1, blocking collectives, local(): lax.all_gather(sum_value.astype(jnp.bfloat16), ('wide', 'narrow'), axis=0...  69.3 us
    all_gather x1, blocking collectives, local(): lax.all_gather(sum_proj.astype(jnp.bfloat16), ('wide', 'narrow'), axis=0,...  69.2 us
  transfers between devices with their start and end apart: 3, of which 1 were waited for; matrix products, arithmetic and copies ran while one was open for 5% of the time, Pallas kernels for 0%

commit v1 on v0

v1 whole, which is shorter than its diff:
```python
import functools

import jax
import jax.numpy as jnp
import numpy as np
from jax import lax
from jax.experimental import pallas as pl
from jax.experimental.pallas import tpu as pltpu
from jax.sharding import PartitionSpec as P

NB = 32
MAXD = 128
QLEN = 64
PPR = 2

EPS_NORM = 1e-06
LOGIT_SCALE = 50.0
MASKED = -1e30
HIGHEST = lax.Precision.HIGHEST
F32 = jnp.float32
BF16 = jnp.bfloat16
AXES = ("wide", "narrow")
BLK = 128
VMEM_LIMIT = 60 * 1024 * 1024


def bucket_offsets(length):
    offset = np.arange(-(length - 1), length)
    half_count = NB // 2
    exact_span = half_count // 2
    distance = -offset
    bucket = (distance < 0).astype(np.int64) * half_count
    distance = np.abs(distance)
    far_bucket = exact_span + (
        np.log(np.maximum(distance, 1) / exact_span)
        / np.log(MAXD / exact_span)
        * (half_count - exact_span)
    ).astype(np.int64)
    far_bucket = np.minimum(far_bucket, half_count - 1)
    bucket = bucket + np.where(distance < exact_span, distance, far_bucket)
    return bucket.astype(np.int32)


def dot(left, right, left_dim=1, right_dim=0):
    return lax.dot_general(
        left, right, (((left_dim,), (right_dim,)), ((), ())), preferred_element_type=F32
    )


def split_two(values):
    high = values.astype(BF16)
    return high, (values - high.astype(F32)).astype(BF16)


def rms_scale(values):
    return lax.rsqrt(jnp.mean(values * values, axis=-1, keepdims=True) + EPS_NORM)


def norm_back(grad_normed, inputs, scale, gain):
    scaled = grad_normed * gain
    return scale * scaled - inputs * (
        scale * scale * scale * jnp.mean(inputs * scaled, axis=-1, keepdims=True)
    )


def slot_onehot(seg_row, slot_count):
    length = seg_row.shape[1]
    return seg_row == lax.broadcasted_iota(jnp.int32, (slot_count, length), 0)


def forward_kernel(
    seg_ref, tok_ref, g1_ref, wq_ref, wk_ref, wv_ref, wo_ref, off_ref, g2_ref, win_ref, wout_ref,
    n1_ref, q_ref, k_ref, v_ref, p_ref, o_ref, hid_ref, n2_ref, act_ref, abar_ref, m_ref,
    strip_ref, mask_ref, asum_ref, hsum_ref,
):
    step = pl.program_id(0)
    row_count = pl.num_programs(0)
    length, width = tok_ref.shape[1:]
    heads = p_ref.shape[1]
    head_size = width // heads
    blocks = length // BLK
    slots = abar_ref.shape[0] // m_ref.shape[0] * (length // QLEN)

    @pl.when(step == 0)
    def _():
        for head in range(heads):
            wide = jnp.broadcast_to(off_ref[head : head + 1, :], (BLK, 2 * length))
            rolled = pltpu.roll(wide, 2 * length - BLK + 1, 1, stride=1, stride_axis=0)
            strip_ref[head] = rolled[:, : 2 * length - BLK]

    x = tok_ref[0].astype(F32)
    n1 = (x * rms_scale(x) * g1_ref[...]).astype(BF16)
    n1_ref[0] = n1
    q_ref[0] = dot(n1, wq_ref[...]).astype(BF16)
    k_ref[0] = dot(n1, wk_ref[...]).astype(BF16)
    v_ref[0] = dot(n1, wv_ref[...]).astype(BF16)
    onehot = slot_onehot(seg_ref[0], slots)
    onehot_f = onehot.astype(F32)
    onehot_low = onehot_f.astype(BF16)
    same = dot(onehot_low, onehot_low, 0, 0)
    mask_ref[...] = jnp.where(same > 0.5, 0.0, MASKED)
    low_lane = lax.broadcasted_iota(jnp.int32, (BLK, 2 * head_size), 1) < head_size

    def pair(index, carry):
        lanes = pl.ds(pl.multiple_of(index * 2 * head_size, 2 * head_size), 2 * head_size)
        k_pair = k_ref[0, :, lanes]
        v_pair = v_ref[0, :, lanes]
        for block in range(blocks):
            rows = slice(block * BLK, (block + 1) * BLK)
            q_pair = q_ref[0, rows, lanes]
            mixed = []
            for part in range(2):
                head = index * 2 + part
                keep = low_lane if part == 0 else jnp.logical_not(low_lane)
                q_head = jnp.where(keep, q_pair, jnp.zeros_like(q_pair))
                start = (blocks - 1 - block) * BLK
                scores = dot(q_head, k_pair, 1, 1)
                scores = scores + strip_ref[head, :, start : start + length] + mask_ref[rows, :]
                top = jnp.max(scores, axis=-1, keepdims=True)
                exps = jnp.exp(scores - top)
                total = jnp.sum(exps, axis=-1, keepdims=True)
                probs = (exps * (1.0 / total)).astype(BF16)
                p_ref[0, head, rows, :] = probs
                mixed.append(dot(probs, v_pair))
            o_ref[0, rows, lanes] = jnp.where(low_lane, mixed[0], mixed[1]).astype(BF16)
        return carry

    lax.fori_loop(0, heads // 2, pair, 0)
    hidden = x + dot(o_ref[0], wo_ref[...])
    hid_ref[0] = hidden
    n2 = (hidden * rms_scale(hidden) * g2_ref[...]).astype(BF16)
    n2_ref[0] = n2
    act = jnp.maximum(dot(n2, win_ref[...]), 0.0).astype(BF16)
    act_ref[0] = act
    counts = jnp.maximum(jnp.sum(onehot_f, axis=-1, keepdims=True), 1.0)
    asum = dot(onehot_low, act) / counts
    high, low = split_two(hidden)
    hsum = (dot(onehot_low, high) + dot(onehot_low, low)) / counts
    asum_ref[pl.ds(step * slots, slots), :] = asum
    hsum_ref[pl.ds(step * slots, slots), :] = hsum

    @pl.when(step == row_count - 1)
    def _():
        high, low = split_two(asum_ref[...])
        abar_ref[...] = high
        pooled = hsum_ref[...] + dot(high, wout_ref[...]) + dot(low, wout_ref[...])
        m_ref[...] = pooled.astype(BF16)


def whole(shape):
    return pl.BlockSpec(shape, lambda r: (0,) * len(shape))


def per_row(shape):
    return pl.BlockSpec((1,) + shape, lambda r: (r,) + (0,) * len(shape))


def forward(seg3, tokens, g1, wq, wk, wv, wo, off_bias, g2, win, wout, slots):
    rows, length, width = tokens.shape
    heads = off_bias.shape[0]
    inner = win.shape[1]
    low = lambda *s: jax.ShapeDtypeStruct(s, BF16)
    rlw = (rows, length, width)
    return pl.pallas_call(
        forward_kernel,
        name="forward_rows",
        grid=(rows,),
        in_specs=[per_row((1, length)), per_row((length, width))]
        + [whole(a.shape) for a in (g1, wq, wk, wv, wo, off_bias, g2, win, wout)],
        out_specs=[per_row((length, width))] * 4
        + [per_row((heads, length, length))]
        + [per_row((length, width))] * 3
        + [per_row((length, inner)), whole((rows * slots, inner)), whole((rows * slots, width))],
        out_shape=[low(*rlw)] * 4
        + [low(rows, heads, length, length), low(*rlw), jax.ShapeDtypeStruct(rlw, F32), low(*rlw)]
        + [low(rows, length, inner), low(rows * slots, inner), low(rows * slots, width)],
        scratch_shapes=[
            pltpu.VMEM((heads, BLK, 2 * length - BLK), F32),
            pltpu.VMEM((length, length), F32),
            pltpu.VMEM((rows * slots, inner), F32),
            pltpu.VMEM((rows * slots, width), F32),
        ],
        compiler_params=pltpu.CompilerParams(vmem_limit_bytes=VMEM_LIMIT),
    )(seg3, tokens, g1, wq, wk, wv, wo, off_bias, g2, win, wout)


def contrast(pooled, target_col, w_proj, slots):
    half = pooled.shape[0] // 2
    z = dot(pooled, w_proj)
    inv = lax.rsqrt(jnp.sum(z * z, axis=-1, keepdims=True) + EPS_NORM)
    unit = z * inv
    emb = unit.astype(BF16)
    emb_q, emb_p = emb[:half], emb[half:]
    logits = LOGIT_SCALE * dot(emb_q, emb_p, 1, 1)
    column = lax.broadcasted_iota(jnp.int32, (half, half), 1)
    logits = jnp.where(column % slots < PPR, logits, MASKED)
    hits = column == target_col
    top = jnp.max(logits, axis=-1, keepdims=True)
    exps = jnp.exp(logits - top)
    total = jnp.sum(exps, axis=-1, keepdims=True)
    picked = jnp.sum(jnp.where(hits, logits, 0.0), axis=-1, keepdims=True)
    loss = jnp.sum(top + jnp.log(total) - picked, axis=0, keepdims=True)
    weights = (exps / total - hits.astype(F32)).astype(BF16)
    grad_q = LOGIT_SCALE * dot(weights, emb_p)
    grad_p = LOGIT_SCALE * dot(weights, emb_q, 0, 0)
    grad = jnp.concatenate([grad_q, grad_p], axis=0)
    dz = (inv * (grad - unit * jnp.sum(grad * unit, axis=-1, keepdims=True))).astype(BF16)
    grad_proj = dot(pooled, dz, 0, 0)
    dm = dot(dz, w_proj, 1, 1)
    return loss, grad_proj, dm


def contrast_kernel(pooled_ref, target_ref, wp_ref, loss_ref, gproj_ref, dm_ref, *, slots):
    loss, grad_proj, dm = contrast(pooled_ref[...], target_ref[...], wp_ref[...], slots)
    loss_ref[...] = loss
    gproj_ref[...] = grad_proj
    dm_ref[...] = dm


def contrast_call(pooled, target_col, w_proj, slots):
    count, width = pooled.shape
    if count > 1024:
        return contrast(pooled, target_col, w_proj, slots)
    return pl.pallas_call(
        functools.partial(contrast_kernel, slots=slots),
        name="contrast_all",
        out_shape=[
            jax.ShapeDtypeStruct((1, 1), F32),
            jax.ShapeDtypeStruct(w_proj.shape, F32),
            jax.ShapeDtypeStruct((count, width), F32),
        ],
        compiler_params=pltpu.CompilerParams(vmem_limit_bytes=VMEM_LIMIT),
    )(pooled, target_col, w_proj)


def ffn_back_kernel(
    seg_ref, dm_ref, act_ref, n2_ref, hid_ref, o_ref, g2_ref, win_ref, wout_ref, wo_ref,
    dh_ref, do_ref, big_ref, g2grad_ref,
    win_acc, wo_acc, g2_acc,
):
    step = pl.program_id(0)
    last = pl.num_programs(0) - 1
    length, width = hid_ref.shape[1:]
    slots = dm_ref.shape[1]

    onehot = slot_onehot(seg_ref[0], slots)
    onehot_f = onehot.astype(F32)
    onehot_low = onehot_f.astype(BF16)
    counts = jnp.maximum(jnp.sum(onehot_f, axis=-1, keepdims=True), 1.0)
    dy_slot = dm_ref[0] / counts
    dyb_slot = dy_slot.astype(BF16)
    dact_slot = dot(dyb_slot, wout_ref[...], 1, 1).astype(BF16)
    dact = dot(onehot_low, dact_slot, 0, 0).astype(BF16)
    act = act_ref[0]
    du = jnp.where(act > 0, dact, jnp.zeros_like(dact))
    win_part = dot(n2_ref[0], du, 0, 0)
    dn2 = dot(du, win_ref[...], 1, 1)
    hidden = hid_ref[0]
    scale = rms_scale(hidden)
    g2_part = jnp.sum(dn2 * hidden * scale, axis=0, keepdims=True)
    high, low = split_two(dy_slot)
    dy = dot(onehot_low, high, 0, 0) + dot(onehot_low, low, 0, 0)
    dh = dy + norm_back(dn2, hidden, scale, g2_ref[...])
    dh_ref[0] = dh
    dhb = dh.astype(BF16)
    do_ref[0] = dot(dhb, wo_ref[...], 1, 1).astype(BF16)
    wo_part = dot(o_ref[0], dhb, 0, 0)

    @pl.when(step == 0)
    def _():
        win_acc[...] = win_part
        wo_acc[...] = wo_part
        g2_acc[...] = g2_part

    @pl.when(step > 0)
    def _():
        win_acc[...] += win_part
        wo_acc[...] += wo_part
        g2_acc[...] += g2_part

    @pl.when(step == last)
    def _():
        parts = win_acc.shape[1] // width
        for part in range(parts):
            big_ref[part * width : (part + 1) * width, :] = win_acc[
                :, part * width : (part + 1) * width
            ].astype(BF16)
        big_ref[parts * width :, :] = wo_acc[...].astype(BF16)
        g2grad_ref[...] = g2_acc[...]


def ffn_back(seg3, dm3, act, n2, hidden, mixed, g2, win, wout, wo):
    rows, length, width = hidden.shape
    inner = win.shape[1]
    slots = dm3.shape[1]
    return pl.pallas_call(
        ffn_back_kernel,
        name="ffn_back",
        grid=(rows,),
        in_specs=[per_row((1, length)), per_row((slots, width)), per_row((length, inner))]
        + [per_row((length, width))] * 3
        + [whole(a.shape) for a in (g2, win, wout, wo)],
        out_specs=[per_row((length, width))] * 2
        + [whole((inner + width, width)), whole((1, width))],
        out_shape=[
            jax.ShapeDtypeStruct(hidden.shape, F32),
            jax.ShapeDtypeStruct(hidden.shape, BF16),
            jax.ShapeDtypeStruct((inner + width, width), BF16),
            jax.ShapeDtypeStruct((1, width), F32),
        ],
        scratch_shapes=[
            pltpu.VMEM((width, inner), F32),
            pltpu.VMEM((width, width), F32),
            pltpu.VMEM((1, width), F32),
        ],
        compiler_params=pltpu.CompilerParams(vmem_limit_bytes=VMEM_LIMIT),
    )(seg3, dm3, act, n2, hidden, mixed, g2, win, wout, wo)


def attn_back_kernel(
    tok_ref, n1_ref, q_ref, k_ref, v_ref, p_ref, o_ref, do_ref, dh_ref, g1_ref,
    wq_ref, wk_ref, wv_ref,
    tgrad_ref, qkv_ref, g1grad_ref, band_ref,
    dq_ref, dkt_ref, dvt_ref, acc_ref, wacc_ref, g1_acc,
):
    step = pl.program_id(0)
    last = pl.num_programs(0) - 1
    length, width = dh_ref.shape[1:]
    heads = p_ref.shape[1]
    head_size = width // heads
    blocks = length // BLK
    low_lane = lax.broadcasted_iota(jnp.int32, (length, 2 * head_size), 1) < head_size

    @pl.when(step == 0)
    def _():
        acc_ref[...] = jnp.zeros_like(acc_ref)

    def pair(index, carry):
        lanes = pl.ds(pl.multiple_of(index * 2 * head_size, 2 * head_size), 2 * head_size)
        q_pair = q_ref[0, :, lanes]
        k_pair = k_ref[0, :, lanes]
        v_pair = v_ref[0, :, lanes]
        do_pair = do_ref[0, :, lanes]
        q_turned = q_pair.T
        do_turned = do_pair.T
        product = do_pair.astype(F32) * o_ref[0, :, lanes].astype(F32)
        dq_parts = []
        for part in range(2):
            head = index * 2 + part
            keep = low_lane if part == 0 else jnp.logical_not(low_lane)
            do_head = jnp.where(keep, do_pair, jnp.zeros_like(do_pair))
            delta = jnp.sum(jnp.where(keep, product, 0.0), axis=-1, keepdims=True)
            probs = p_ref[0, head]
            dprobs = dot(do_head, v_pair, 1, 1)
            ds = probs.astype(F32) * (dprobs - delta)
            ds_low = ds.astype(BF16)
            sums = {}
            for i in range(blocks):
                for j in range(blocks):
                    place = max(-2, min(2, j - i)) + 2
                    tile = ds[i * BLK : (i + 1) * BLK, j * BLK : (j + 1) * BLK]
                    sums[place] = tile if place not in sums else sums[place] + tile
            for place, value in sums.items():
                acc_ref[head, :, place * BLK : (place + 1) * BLK] += value
            dq_parts.append(dot(ds_low, k_pair))
            own = slice(part * head_size, (part + 1) * head_size)
            place = pl.ds(pl.multiple_of(head * head_size, head_size), head_size)
            dkt_ref[place, :] = dot(q_turned[own], ds_low).astype(BF16)
            dvt_ref[place, :] = dot(do_turned[own], probs).astype(BF16)
        dq_ref[:, lanes] = jnp.where(low_lane, dq_parts[0], dq_parts[1]).astype(BF16)
        return carry

    lax.fori_loop(0, heads // 2, pair, 0)
    dq = dq_ref[...]
    dk = dkt_ref[...].T
    dv = dvt_ref[...].T
    n1 = n1_ref[0]
    parts = [dot(n1, d, 0, 0) for d in (dq, dk, dv)]
    dn1 = dot(dq, wq_ref[...], 1, 1) + dot(dk, wk_ref[...], 1, 1) + dot(dv, wv_ref[...], 1, 1)
    x = tok_ref[0].astype(F32)
    scale = rms_scale(x)
    g1_part = jnp.sum(dn1 * x * scale, axis=0, keepdims=True)
    tgrad_ref[0] = (dh_ref[0] + norm_back(dn1, x, scale, g1_ref[...])).astype(BF16)

    @pl.when(step == 0)
    def _():
        for index in range(3):
            wacc_ref[index] = parts[index]
        g1_acc[...] = g1_part

    @pl.when(step > 0)
    def _():
        for index in range(3):
            wacc_ref[index] += parts[index]
        g1_acc[...] += g1_part

    @pl.when(step == last)
    def _():
        for index in range(3):
            qkv_ref[index * width : (index + 1) * width, :] = wacc_ref[index].astype(BF16)
        g1grad_ref[...] = g1_acc[...]
        for head in range(heads):
            far_low = jnp.sum(acc_ref[head, :, :BLK], axis=0, keepdims=True)
            far_high = jnp.sum(acc_ref[head, :, 4 * BLK :], axis=0, keepdims=True)
            band = jnp.concatenate(
                [acc_ref[head, :, BLK : 4 * BLK], jnp.zeros((BLK, BLK), F32)], axis=1
            )
            rows = BLK // 2
            while rows >= 1:
                band = band[:rows] + pltpu.roll(band[rows:], 4 * BLK - rows, 1)
                rows //= 2
            band_ref[head : head + 1, : 4 * BLK] = band
            band_ref[head : head + 1, 4 * BLK : 5 * BLK] = far_low
            band_ref[head : head + 1, 5 * BLK :] = far_high


def attn_back(tokens, n1, q, k, v, probs, mixed, do, dh, g1, wq, wk, wv):
    rows, length, width = tokens.shape
    heads = probs.shape[1]
    return pl.pallas_call(
        attn_back_kernel,
        name="attn_back",
        grid=(rows,),
        in_specs=[per_row((length, width))] * 5
        + [per_row((heads, length, length))]
        + [per_row((length, width))] * 3
        + [whole(a.shape) for a in (g1, wq, wk, wv)],
        out_specs=[
            per_row((length, width)),
            whole((3 * width, width)),
            whole((1, width)),
            whole((heads, 6 * BLK)),
        ],
        out_shape=[
            jax.ShapeDtypeStruct(tokens.shape, BF16),
            jax.ShapeDtypeStruct((3 * width, width), BF16),
            jax.ShapeDtypeStruct((1, width), F32),
            jax.ShapeDtypeStruct((heads, 6 * BLK), F32),
        ],
        scratch_shapes=[
            pltpu.VMEM((length, width), BF16),
            pltpu.VMEM((width, length), BF16),
            pltpu.VMEM((width, length), BF16),
            pltpu.VMEM((heads, BLK, 5 * BLK), F32),
            pltpu.VMEM((3, width, width), F32),
            pltpu.VMEM((1, width), F32),
        ],
        compiler_params=pltpu.CompilerParams(vmem_limit_bytes=VMEM_LIMIT),
    )(tokens, n1, q, k, v, probs, mixed, do, dh, g1, wq, wk, wv)


def band_table(length):
    buckets = bucket_offsets(length)
    zero = length - 1
    table = np.zeros((6 * BLK, NB), np.float32)
    for column in range(4 * BLK):
        offset = column - BLK if column < 3 * BLK else column - 5 * BLK
        if -2 * BLK < offset < 2 * BLK and abs(offset) < length:
            table[column, buckets[zero + offset]] = 1.0
    far = buckets[: zero - BLK], buckets[zero + BLK + 1 :]
    assert len(set(far[0])) == 1 and len(set(far[1])) == 1
    table[4 * BLK : 5 * BLK, far[0][0]] = 1.0
    table[5 * BLK :, far[1][0]] = 1.0
    return table


def bit_order(wide, narrow):
    total = wide * narrow
    assert total & (total - 1) == 0 and narrow & (narrow - 1) == 0
    outer = [b for b in (1 << s for s in range(total.bit_length())) if narrow <= b < total]
    inner = [b for b in (1 << s for s in range(total.bit_length())) if b < narrow]
    return outer, inner


def swap(values, bit, total):
    return lax.ppermute(values, AXES, [(i, i ^ bit) for i in range(total)])


def gather_rows(values, bits, linear, total):
    for bit in bits:
        other = swap(values, bit, total)
        high = (linear & bit) != 0
        values = jnp.concatenate(
            [jnp.where(high, other, values), jnp.where(high, values, other)], axis=0
        )
    return values


def reorder(values, bits, shard):
    count = len(bits)
    taken = list(reversed(bits))
    want = sorted(bits, reverse=True)
    shape = values.shape
    split = values.reshape((2,) * count + (shard,) + shape[1:])
    perm = [taken.index(b) for b in want]
    return split.transpose(perm + list(range(count, split.ndim))).reshape(shape)


def scatter_sum(values, small, bits, linear, total):
    rows = values.shape[0]
    for bit in bits:
        rows //= 2
        high = ((linear & bit) != 0).astype(jnp.int32)
        send = lax.dynamic_slice_in_dim(values, (1 - high) * rows, rows)
        if small is not None:
            send = jnp.concatenate([send, small.astype(BF16)], axis=0)
        got = swap(send, bit, total)
        keep = lax.dynamic_slice_in_dim(values, high * rows, rows)
        values = (keep.astype(F32) + got[:rows].astype(F32)).astype(BF16)
        if small is not None:
            small = lax.reduce_precision(small, 8, 7) + got[rows:].astype(F32)
    return values, small


def local(
    tokens, seg_ids, positives, norm1_gain, w_query, w_key, w_value, w_attn_out,
    rel_bias, norm2_gain, w_in, w_ffn_out, w_proj,
):
    rows, length, width = tokens.shape
    heads = rel_bias.shape[1]
    slots = length // QLEN
    inner = w_in.shape[1]
    wide, narrow = lax.axis_size("wide"), lax.axis_size("narrow")
    total = wide * narrow
    linear = lax.axis_index("wide") * narrow + lax.axis_index("narrow")
    outer_bits, inner_bits = bit_order(wide, narrow)
    g1 = norm1_gain.astype(F32).reshape(1, width)
    g2 = norm2_gain.astype(F32).reshape(1, width)
    seg3 = seg_ids.reshape(rows, 1, length)
    buckets = bucket_offsets(length)
    offset_onehot = np.zeros((NB, 2 * length), np.float32)
    offset_onehot[buckets, np.arange(2 * length - 1)] = 1.0
    off_bias = dot(rel_bias, jnp.asarray(offset_onehot, BF16), 0, 0)

    n1, q, k, v, probs, mixed, hidden, n2, act, abar, pooled = forward(
        seg3, tokens, g1, w_query, w_key, w_value, w_attn_out, off_bias, g2, w_in, w_ffn_out, slots
    )
    shard = rows * slots
    order = inner_bits + outer_bits[1:] + outer_bits[:1]
    pooled_all = reorder(gather_rows(pooled, order, linear, total), order, shard)
    target_col = ((positives // PPR) * slots + positives % PPR).reshape(-1, 1)
    loss, grad_proj, dm = contrast_call(pooled_all, target_col, w_proj, slots)
    dm_own = lax.dynamic_slice_in_dim(dm, linear * shard, shard).reshape(rows, slots, width)
    dh, do, big, grad_g2 = ffn_back(
        seg3, dm_own, act, n2, hidden, mixed, g2, w_in, w_ffn_out, w_attn_out
    )
    tokens_grad, qkv, grad_g1, band = attn_back(
        tokens, n1, q, k, v, probs, mixed, do, dh, g1, w_query, w_key, w_value
    )
    grad_bias = jnp.dot(band, jnp.asarray(band_table(length)), precision=HIGHEST)

    abar_all = reorder(gather_rows(abar, order, linear, total), order, shard)
    grad_ffn_out = dot(abar_all, dm.astype(BF16), 0, 0)

    small = jnp.concatenate(
        [
            grad_g1,
            grad_g2,
            jnp.pad(grad_bias.reshape(1, -1), ((0, 0), (0, width - heads * NB))),
            jnp.zeros((5, width), F32),
        ],
        axis=0,
    )
    down = outer_bits + inner_bits
    packed = jnp.concatenate([big, qkv], axis=0)
    part, small = scatter_sum(packed, small, down, linear, total)
    full = gather_rows(part, list(reversed(down)), linear, total)
    grads = full.astype(F32)
    blocks = [grads[i * width : (i + 1) * width] for i in range(inner // width + 4)]
    parts = inner // width
    grad_in = jnp.concatenate(blocks[:parts], axis=1)
    return (
        loss[0, 0],
        tokens_grad,
        small[0],
        blocks[parts + 1],
        blocks[parts + 2],
        blocks[parts + 3],
        blocks[parts],
        small[2, : heads * NB].reshape(heads, NB).T,
        small[1],
        grad_in,
        grad_ffn_out,
        grad_proj,
    )


def solution(mesh):
    rows = P(AXES, None, None)
    in_specs = (rows, P(AXES, None)) + (P(),) * 11
    out_specs = (P(), rows) + (P(),) * 10
    return jax.shard_map(local, mesh=mesh, in_specs=in_specs, out_specs=out_specs, check_vma=False)
```

time: 1320 us -> 252 us (0.19)
  blocking collectives: 650 us -> 0 us
  local copies, waits for them, and re-layouts: 417 us -> 13.5 us
  matrix products: 110 us -> 5.93 us
  Pallas kernels: 0 us -> 82.3 us
  starting transfers between devices: 0.12 us -> 37 us
  between operations: 15.7 us -> 1.07 us
    all_gather x6 -> x0, blocking collectives: 420 us -> none  [the longest x1 73.9 us: local(): gathered = lax.all_gather(emb_local, ('wide', 'narrow'), axis=0, tiled=True)]
    unnamed x205 -> x25, local copies, waits for them, and re-layouts: 280 us -> 4.28 us
    unnamed x1 -> x0, blocking collectives: 230 us -> none
    dot_general x63 -> x3, matrix products: 110 us -> 5.93 us  [the longest x2 4.89 us: dot(): lax.dot_general(left, right, (((left_dim,), (right_dim,)), ((), ())), pre...]
    ppermute x0 -> x20, waiting for transfers between devices: none -> 86.9 us  [swap(): return lax.ppermute(values, AXES, [(i, i ^ bit) for i in range(total)])]
    unnamed x4 -> x0, waiting for transfers between devices: 83.1 us -> none
    pallas_call x0 -> x4, Pallas kernels: none -> 82.3 us  [the longest x1 39.1 us: forward(): pl.pallas_call(forward_kernel, name='forward_rows', grid=(rows,), in_spec...]
    slice x6 -> x3, local copies, waits for them, and re-layouts: 47.9 us -> 3.42 us  [the longest x1 2.81 us: local(): grads[i * width:(i + 1) * width]]
  transfers between devices with their start and end apart: 3 -> 20, of which waited for: 1 -> 16; matrix products, arithmetic and copies ran while one was open for 5% -> 4% of each run, Pallas kernels for 0% -> 0%
where the time goes in v1:
time: 252 us; the launch traced here: 249 us
  waiting for transfers between devices  86.9 us (34%)
  Pallas kernels  82.3 us (33%)
  starting transfers between devices  37 us (15%)
  other arithmetic  22.3 us (9%)
  local copies, waits for them, and re-layouts  13.5 us (5%)
  matrix products  5.93 us (2%)
    ppermute x20, waiting for transfers between devices, swap(): return lax.ppermute(values, AXES, [(i, i ^ bit) for i in range(total)])  86.9 us
    pallas_call x1, Pallas kernels, forward(): pl.pallas_call(forward_kernel, name='forward_rows', grid=(rows,), in_spec...  39.1 us
    ppermute x20, starting transfers between devices, swap(): return lax.ppermute(values, AXES, [(i, i ^ bit) for i in range(total)])  37 us
    pallas_call x1, Pallas kernels, attn_back(): pl.pallas_call(attn_back_kernel, name='attn_back', grid=(rows,), in_specs...  23 us
    pallas_call x1, Pallas kernels, ffn_back(): pl.pallas_call(ffn_back_kernel, name='ffn_back', grid=(rows,), in_specs=[...  15.8 us
    select_n x15, other arithmetic, gather_rows(): jnp.where(high, other, values)  5.17 us
  transfers between devices with their start and end apart: 20, of which 16 were waited for; matrix products, arithmetic and copies ran while one was open for 4% of the time, Pallas kernels for 0%

profile of v1, /device:TPU:0, one launch (start us, length us, event | category | flops | bytes accessed | tf_op | source)
XLA Modules:
  0.0 249.0 jit_solution(11481308746384449017)
XLA Ops:
  6.0 39.1 %forward_rows.1 = (bf16[2,512,512]{2,1,0:T(8,128)(2,1)}, bf16[2,512,512]{2,1,0:T(8,128)(2,1)}, bf16[2,512,512]{2,1,0:T(8,128)(2,1)}, bf16[2,512,512]{2,1,0:T(8,1...) custom-call(s32[2,1,512]{2,1,0:T(1,128)} %reshape.58.seg_ref, ...), custom_call_target="tpu_custom_call" | custom-call | tf_op jit(solution)/shard_map/forward_rows/pallas_call | solution.py:164
  45.2 3.1 %collective-permute-start = (bf16[16,512]{1,0:T(8,128)(2,1)}, bf16[16,512]{1,0:T(8,128)(2,1)S(1)}, u32[]{:S(2)}, u32[]{:S(2)}) collective-permute-start(bf16[16,512]{1,0:T(8,128)(2,1)} %get-tuple-element.34), channel_id=1, source_target_pairs={{0,1},{1,0},{2,3},{3,2},{4,5},{5,4},{6,7},{7,6},{8,9},{9,8},{10,11... | collective-permute-start | bytes 49160 | tf_op jit(solution)/shard_map/ppermute | solution.py:476
  50.9 3.1 %collective-permute-start.1 = (bf16[32,512]{1,0:T(8,128)(2,1)S(1)}, bf16[32,512]{1,0:T(8,128)(2,1)S(1)}, u32[]{:S(2)}, u32[]{:S(2)}) collective-permute-start(bf16[32,512]{1,0:T(8,128)(2,1)S(1)} %pad_maximum_fusion.19), channel_id=1, source_target_pairs={{0,2},{1,3},{2,0},{3,1},{4,6},{5,7},{6,4},{7,5},{8,10},{9,11},{10,... | collective-permute-start | bytes 98312 | tf_op jit(solution)/shard_map/ppermute | solution.py:476
  57.8 2.4 collective-permute-done.2
  62.2 3.1 %collective-permute-done.3 = bf16[128,512]{1,0:T(8,128)(2,1)S(1)} collective-permute-done((bf16[128,512]{1,0:T(8,128)(2,1)S(1)}, bf16[128,512]{1,0:T(8,128)(2,1)S(1)}, u32[]{:S(2)}, u32[]{:S(2)}) %collective-permute-start.3) | collective-permute-done | bytes 131104 | tf_op jit(solution)/shard_map/ppermute | solution.py:476
  68.0 4.4 %contrast_all.1 = (f32[1,1]{1,0:T(1,128)}, f32[512,512]{1,0:T(8,128)}, f32[512,512]{1,0:T(8,128)}) custom-call(bf16[512,512]{1,0:T(8,128)(2,1)} %bitcast.26, s32[256,1]{1,0:T(8,128)} %copy.29.target_ref, bf16[512,512]{1,0:T(8,128)(2,1)} %wp_ref.1), custom_call_target="tpu_custom_call" | custom-call | tf_op jit(solution)/shard_map/contrast_all/pallas_call | solution.py:224
  73.8 15.8 %ffn_back.1 = (f32[2,512,512]{2,1,0:T(8,128)}, bf16[2,512,512]{2,1,0:T(8,128)(2,1)}, bf16[2560,512]{1,0:T(8,128)(2,1)}, f32[1,512]{1,0:T(1,128)}) custom-call(s32[2,1,512]{2,1,0:T(1,128)} %reshape.58.seg_ref, f32[2,8,512]{2,1,0:T(8,128)} %dynamic-slice_bitcast_fusion.dm_ref, bf16[2,512,2048]{2,1,0:T(8,128)(2,1)} %get-tuple-element.43.act_ref, ...), custom_call_target="tpu_custom_call" | custom-call | tf_op jit(solution)/shard_map/ffn_back/pallas_call | solution.py:296
  89.6 23.0 %attn_back.1 = (bf16[2,512,512]{2,1,0:T(8,128)(2,1)}, bf16[1536,512]{1,0:T(8,128)(2,1)}, f32[1,512]{1,0:T(1,128)}, f32[8,768]{1,0:T(8,128)}) custom-call(bf16[2,512,512]{2,1,0:T(8,128)(2,1)} %tok_ref.3, bf16[2,512,512]{2,1,0:T(8,128)(2,1)} %get-tuple-element.36.n1_ref, bf16[2,512,512]{2,1,0:T(8,128)(2,1)} %get-tuple-element.37.q_ref, ...), custom_call_target="tpu_custom_call" | custom-call | tf_op jit(solution)/shard_map/attn_back/pallas_call | solution.py:420
  117.7 4.2 %collective-permute-done.5 = bf16[2056,512]{1,0:T(8,128)(2,1)} collective-permute-done((bf16[2056,512]{1,0:T(8,128)(2,1)S(1)}, bf16[2056,512]{1,0:T(8,128)(2,1)}, u32[]{:S(2)}, u32[]{:S(2)}) %collective-permute-start.5) | collective-permute-done | bytes 2105376 | tf_op jit(solution)/shard_map/ppermute | solution.py:476
  121.9 2.8 %add_convert_fusion = bf16[2048,512]{1,0:T(8,128)(2,1)S(1)} fusion(bf16[2056,512]{1,0:T(8,128)(2,1)} %collective-permute-done.5, bf16[4096,512]{1,0:T(8,128)(2,1)} %copy-done.2, s32[]{:T(128)S(6)} %mul.47), kind=kLoop, calls=%fused_computation.2 | loop fusion | flops 4194304 | bytes 6291460 | tf_op jit(solution)/shard_map/convert_element_type | solution.py:509
  127.5 23.7 %collective-permute-done.6 = bf16[1032,512]{1,0:T(8,128)(2,1)} collective-permute-done((bf16[1032,512]{1,0:T(8,128)(2,1)S(1)}, bf16[1032,512]{1,0:T(8,128)(2,1)}, u32[]{:S(2)}, u32[]{:S(2)}) %collective-permute-start.6) | collective-permute-done | bytes 1056800 | tf_op jit(solution)/shard_map/ppermute | solution.py:476
  155.6 11.6 %collective-permute-done.7 = bf16[520,512]{1,0:T(8,128)(2,1)S(1)} collective-permute-done((bf16[520,512]{1,0:T(8,128)(2,1)S(1)}, bf16[520,512]{1,0:T(8,128)(2,1)S(1)}, u32[]{:S(2)}, u32[]{:S(2)}) %collective-permute-start.7) | collective-permute-done | bytes 532512 | tf_op jit(solution)/shard_map/ppermute | solution.py:476
  170.3 5.6 %collective-permute-done.8 = bf16[264,512]{1,0:T(8,128)(2,1)S(1)} collective-permute-done((bf16[264,512]{1,0:T(8,128)(2,1)S(1)}, bf16[264,512]{1,0:T(8,128)(2,1)S(1)}, u32[]{:S(2)}, u32[]{:S(2)}) %collective-permute-start.8) | collective-permute-done | bytes 270368 | tf_op jit(solution)/shard_map/ppermute | solution.py:476
  176.8 2.8 %collective-permute-start.9 = (bf16[136,512]{1,0:T(8,128)(2,1)S(1)}, bf16[136,512]{1,0:T(8,128)(2,1)S(1)}, u32[]{:S(2)}, u32[]{:S(2)}) collective-permute-start(bf16[136,512]{1,0:T(8,128)(2,1)S(1)} %pad_maximum_fusion.15), channel_id=1, source_target_pairs={{0,2},{1,3},{2,0},{3,1},{4,6},{5,7},{6,4},{7,5},{8,10},{9,11},{10,... | collective-permute-start | bytes 417800 | tf_op jit(solution)/shard_map/ppermute | solution.py:476
  179.6 5.0 %collective-permute-done.9 = bf16[136,512]{1,0:T(8,128)(2,1)S(1)} collective-permute-done((bf16[136,512]{1,0:T(8,128)(2,1)S(1)}, bf16[136,512]{1,0:T(8,128)(2,1)S(1)}, u32[]{:S(2)}, u32[]{:S(2)}) %collective-permute-start.9) | collective-permute-done | bytes 139296 | tf_op jit(solution)/shard_map/ppermute | solution.py:476
  187.8 3.6 %collective-permute-done.10 = bf16[128,512]{1,0:T(8,128)(2,1)S(1)} collective-permute-done((bf16[128,512]{1,0:T(8,128)(2,1)S(1)}, bf16[128,512]{1,0:T(8,128)(2,1)S(1)}, u32[]{:S(2)}, u32[]{:S(2)}) %collective-permute-start.10) | collective-permute-done | bytes 131104 | tf_op jit(solution)/shard_map/ppermute | solution.py:476
  191.4 8.7 %collective-permute-start.11 = (bf16[256,512]{1,0:T(8,128)(2,1)S(1)}, bf16[256,512]{1,0:T(8,128)(2,1)S(1)}, u32[]{:S(2)}, u32[]{:S(2)}) collective-permute-start(bf16[256,512]{1,0:T(8,128)(2,1)S(1)} %pad_maximum_fusion.13), channel_id=1, source_target_pairs={{0,1},{1,0},{2,3},{3,2},{4,5},{5,4},{6,7},{7,6},{8,9},{9,8},{10,11... | collective-permute-start | bytes 786440 | tf_op jit(solution)/shard_map/ppermute | solution.py:476
  201.7 2.7 %collective-permute-done.11 = bf16[256,512]{1,0:T(8,128)(2,1)S(1)} collective-permute-done((bf16[256,512]{1,0:T(8,128)(2,1)S(1)}, bf16[256,512]{1,0:T(8,128)(2,1)S(1)}, u32[]{:S(2)}, u32[]{:S(2)}) %collective-permute-start.11) | collective-permute-done | bytes 262176 | tf_op jit(solution)/shard_map/ppermute | solution.py:476
  208.4 7.2 %collective-permute-done.12 = bf16[512,512]{1,0:T(8,128)(2,1)S(1)} collective-permute-done((bf16[512,512]{1,0:T(8,128)(2,1)S(1)}, bf16[512,512]{1,0:T(8,128)(2,1)S(1)}, u32[]{:S(2)}, u32[]{:S(2)}) %collective-permute-start.12) | collective-permute-done | bytes 524320 | tf_op jit(solution)/shard_map/ppermute | solution.py:476
  217.4 3.8 %collective-permute-done.18 = bf16[128,2048]{1,0:T(8,128)(2,1)S(1)} collective-permute-done((bf16[128,2048]{1,0:T(8,128)(2,1)S(1)}, bf16[128,2048]{1,0:T(8,128)(2,1)S(1)}, u32[]{:S(2)}, u32[]{:S(2)}) %collective-permute-start.18) | collective-permute-done | bytes 524320 | tf_op jit(solution)/shard_map/ppermute | solution.py:476
  221.6 9.1 %collective-permute-done.13 = bf16[1024,512]{1,0:T(8,128)(2,1)S(1)} collective-permute-done((bf16[1024,512]{1,0:T(8,128)(2,1)S(1)}, bf16[1024,512]{1,0:T(8,128)(2,1)S(1)}, u32[]{:S(2)}, u32[]{:S(2)}) %collective-permute-start.13) | collective-permute-done | bytes 1048608 | tf_op jit(solution)/shard_map/ppermute | solution.py:476
  234.7 3.3 %fusion = f32[2048,512]{1,0:T(8,128)} fusion(bf16[512,2048]{1,0:T(8,128)(2,1)S(1)} %bitcast.24, f32[512,512]{1,0:T(8,128)S(1)} %copy-done.5), kind=kOutput, calls=%fused_computation.22 | convolution fusion | flops 1074003968 | bytes 7340032 | tf_op jit(solution)/shard_map/dot_general | solution.py:45
  240.1 2.5 %broadcast_select_fusion.1 = (bf16[2048,512]{1,0:T(8,128)(2,1)S(1)}, bf16[2048,512]{1,0:T(8,128)(2,1)S(1)}) fusion(bf16[2048,512]{1,0:T(8,128)(2,1)} %collective-permute-done.14, pred[]{:T(512)S(6)} %ne.30, bf16[1024,512]{1,0:T(8,128)(2,1)S(1)} %get-tuple-element.69, bf16[1024,512]{1,0:T(8,128)(2,1)S(1)} %get-tuple-element.68), kind=kLoop, calls=%fused_computation.8 | loop fusion | flops 6291456 | bytes 8388609 | tf_op jit(solution)/shard_map/jit(_where)/select_n | solution.py:484
  243.8 2.8 %fusion.10 = (f32[512,512]{1,0:T(8,128)S(1)}, f32[512,512]{1,0:T(8,128)S(1)}, f32[512,512]{1,0:T(8,128)S(1)}, f32[512,512]{1,0:T(8,128)S(1)}, f32[512,512]{1,0:T...) fusion(f32[4096,512]{1,0:T(8,128)S(1)} %maximum_convert_fusion), kind=kLoop, calls=%fused_computation.89 | loop fusion | bytes 16777216 | tf_op jit(solution)/shard_map/slice | solution.py:569
  (116 shorter events, 54.5 us)
Async XLA Ops:
  6.0 59.5 %copy-start.11 = (s32[256]{0:T(256)S(1)}, s32[256]{0:T(256)}, u32[]{:S(2)}) copy-start(s32[256]{0:T(256)} %param.17) | copy-start | bytes 3076
  45.2 5.0 %collective-permute-start = (bf16[16,512]{1,0:T(8,128)(2,1)}, bf16[16,512]{1,0:T(8,128)(2,1)S(1)}, u32[]{:S(2)}, u32[]{:S(2)}) collective-permute-start(bf16[16,512]{1,0:T(8,128)(2,1)} %get-tuple-element.34), channel_id=1, source_target_pairs={{0,1},{1,0},{2,3},{3,2},{4,5},{5,4},{6,7},{7,6},{8,9},{9,8},{10,11... | collective-permute-start | bytes 49160 | tf_op jit(solution)/shard_map/ppermute | solution.py:476
  50.9 5.0 %collective-permute-start.1 = (bf16[32,512]{1,0:T(8,128)(2,1)S(1)}, bf16[32,512]{1,0:T(8,128)(2,1)S(1)}, u32[]{:S(2)}, u32[]{:S(2)}) collective-permute-start(bf16[32,512]{1,0:T(8,128)(2,1)S(1)} %pad_maximum_fusion.19), channel_id=1, source_target_pairs={{0,2},{1,3},{2,0},{3,1},{4,6},{5,7},{6,4},{7,5},{8,10},{9,11},{10,... | collective-permute-start | bytes 98312 | tf_op jit(solution)/shard_map/ppermute | solution.py:476
  55.9 4.3 %collective-permute-start.2 = (bf16[64,512]{1,0:T(8,128)(2,1)S(1)}, bf16[64,512]{1,0:T(8,128)(2,1)S(1)}, u32[]{:S(2)}, u32[]{:S(2)}) collective-permute-start(bf16[64,512]{1,0:T(8,128)(2,1)S(1)} %pad_maximum_fusion.18), channel_id=1, source_target_pairs={{0,8},{1,9},{2,10},{3,11},{4,12},{5,13},{6,14},{7,15},{8,0},{9,1},... | collective-permute-start | bytes 196616 | tf_op jit(solution)/shard_map/ppermute | solution.py:476
  60.3 5.0 %collective-permute-start.3 = (bf16[128,512]{1,0:T(8,128)(2,1)S(1)}, bf16[128,512]{1,0:T(8,128)(2,1)S(1)}, u32[]{:S(2)}, u32[]{:S(2)}) collective-permute-start(bf16[128,512]{1,0:T(8,128)(2,1)S(1)} %pad_maximum_fusion.16), channel_id=1, source_target_pairs={{0,16},{1,17},{2,18},{3,19},{4,20},{5,21},{6,22},{7,23},{8,24},{9,... | collective-permute-start | bytes 393224 | tf_op jit(solution)/shard_map/ppermute | solution.py:476
  65.4 1.6 collective-permute-start.4
  89.6 23.1 %copy-start.7 = (f32[768,32]{1,0:T(8,128)S(1)}, f32[768,32]{1,0:T(8,128)}, u32[]{:S(2)}) copy-start(f32[768,32]{1,0:T(8,128)} %constant.74.clone) | copy-start | bytes 294916
  89.6 24.2 %copy-start.3 = (bf16[2560,512]{1,0:T(8,128)(2,1)S(1)}, bf16[2560,512]{1,0:T(8,128)(2,1)}, u32[]{:S(2)}) copy-start(bf16[2560,512]{1,0:T(8,128)(2,1)} %get-tuple-element.52) | copy-start | bytes 7864324
  117.5 4.4 %collective-permute-start.5 = (bf16[2056,512]{1,0:T(8,128)(2,1)S(1)}, bf16[2056,512]{1,0:T(8,128)(2,1)}, u32[]{:S(2)}, u32[]{:S(2)}) collective-permute-start(bf16[2056,512]{1,0:T(8,128)(2,1)S(1)} %pad_maximum_fusion.1), channel_id=1, source_target_pairs={{0,4},{1,5},{2,6},{3,7},{4,0},{5,1},{6,2},{7,3},{8,12},{9,13},{10,... | collective-permute-start | bytes 6316040 | tf_op jit(solution)/shard_map/ppermute | solution.py:476
  125.6 25.6 %collective-permute-start.6 = (bf16[1032,512]{1,0:T(8,128)(2,1)S(1)}, bf16[1032,512]{1,0:T(8,128)(2,1)}, u32[]{:S(2)}, u32[]{:S(2)}) collective-permute-start(bf16[1032,512]{1,0:T(8,128)(2,1)S(1)} %pad_maximum_fusion.4), channel_id=1, source_target_pairs={{0,8},{1,9},{2,10},{3,11},{4,12},{5,13},{6,14},{7,15},{8,0},{9,1},... | collective-permute-start | bytes 3170312 | tf_op jit(solution)/shard_map/ppermute | solution.py:476
  152.9 17.1 %copy-start.10 = (bf16[16,2048]{1,0:T(8,128)(2,1)S(1)}, bf16[16,2048]{1,0:T(8,128)(2,1)}, u32[]{:S(2)}) copy-start(bf16[16,2048]{1,0:T(8,128)(2,1)} %get-tuple-element.54) | copy-start | bytes 196612
  153.8 13.4 %collective-permute-start.7 = (bf16[520,512]{1,0:T(8,128)(2,1)S(1)}, bf16[520,512]{1,0:T(8,128)(2,1)S(1)}, u32[]{:S(2)}, u32[]{:S(2)}) collective-permute-start(bf16[520,512]{1,0:T(8,128)(2,1)S(1)} %pad_maximum_fusion.7), channel_id=1, source_target_pairs={{0,16},{1,17},{2,18},{3,19},{4,20},{5,21},{6,22},{7,23},{8,24},{9,... | collective-permute-start | bytes 1597448 | tf_op jit(solution)/shard_map/ppermute | solution.py:476
  168.2 7.7 %collective-permute-start.8 = (bf16[264,512]{1,0:T(8,128)(2,1)S(1)}, bf16[264,512]{1,0:T(8,128)(2,1)S(1)}, u32[]{:S(2)}, u32[]{:S(2)}) collective-permute-start(bf16[264,512]{1,0:T(8,128)(2,1)S(1)} %pad_maximum_fusion.11), channel_id=1, source_target_pairs={{0,1},{1,0},{2,3},{3,2},{4,5},{5,4},{6,7},{7,6},{8,9},{9,8},{10,11... | collective-permute-start | bytes 811016 | tf_op jit(solution)/shard_map/ppermute | solution.py:476
  170.0 9.6 %collective-permute-start.15 = (bf16[16,2048]{1,0:T(8,128)(2,1)S(1)}, bf16[16,2048]{1,0:T(8,128)(2,1)S(1)}, u32[]{:S(2)}, u32[]{:S(2)}) collective-permute-start(bf16[16,2048]{1,0:T(8,128)(2,1)S(1)} %copy-done.10), channel_id=1, source_target_pairs={{0,1},{1,0},{2,3},{3,2},{4,5},{5,4},{6,7},{7,6},{8,9},{9,8},{10,11... | collective-permute-start | bytes 196616 | tf_op jit(solution)/shard_map/ppermute | solution.py:476
  176.8 7.8 %collective-permute-start.9 = (bf16[136,512]{1,0:T(8,128)(2,1)S(1)}, bf16[136,512]{1,0:T(8,128)(2,1)S(1)}, u32[]{:S(2)}, u32[]{:S(2)}) collective-permute-start(bf16[136,512]{1,0:T(8,128)(2,1)S(1)} %pad_maximum_fusion.15), channel_id=1, source_target_pairs={{0,2},{1,3},{2,0},{3,1},{4,6},{5,7},{6,4},{7,5},{8,10},{9,11},{10,... | collective-permute-start | bytes 417800 | tf_op jit(solution)/shard_map/ppermute | solution.py:476
  184.7 6.7 %collective-permute-start.10 = (bf16[128,512]{1,0:T(8,128)(2,1)S(1)}, bf16[128,512]{1,0:T(8,128)(2,1)S(1)}, u32[]{:S(2)}, u32[]{:S(2)}) collective-permute-start(bf16[128,512]{1,0:T(8,128)(2,1)S(1)} %add_convert_fusion.4), channel_id=1, source_target_pairs={{0,2},{1,3},{2,0},{3,1},{4,6},{5,7},{6,4},{7,5},{8,10},{9,11},{10,... | collective-permute-start | bytes 393224 | tf_op jit(solution)/shard_map/ppermute | solution.py:476
  186.3 13.8 %collective-permute-start.16 = (bf16[32,2048]{1,0:T(8,128)(2,1)S(1)}, bf16[32,2048]{1,0:T(8,128)(2,1)S(1)}, u32[]{:S(2)}, u32[]{:S(2)}) collective-permute-start(bf16[32,2048]{1,0:T(8,128)(2,1)S(1)} %pad_maximum_fusion.17), channel_id=1, source_target_pairs={{0,2},{1,3},{2,0},{3,1},{4,6},{5,7},{6,4},{7,5},{8,10},{9,11},{10,... | collective-permute-start | bytes 393224 | tf_op jit(solution)/shard_map/ppermute | solution.py:476
  191.4 13.1 %collective-permute-start.11 = (bf16[256,512]{1,0:T(8,128)(2,1)S(1)}, bf16[256,512]{1,0:T(8,128)(2,1)S(1)}, u32[]{:S(2)}, u32[]{:S(2)}) collective-permute-start(bf16[256,512]{1,0:T(8,128)(2,1)S(1)} %pad_maximum_fusion.13), channel_id=1, source_target_pairs={{0,1},{1,0},{2,3},{3,2},{4,5},{5,4},{6,7},{7,6},{8,9},{9,8},{10,11... | collective-permute-start | bytes 786440 | tf_op jit(solution)/shard_map/ppermute | solution.py:476
  200.2 6.4 %collective-permute-start.17 = (bf16[64,2048]{1,0:T(8,128)(2,1)S(1)}, bf16[64,2048]{1,0:T(8,128)(2,1)S(1)}, u32[]{:S(2)}, u32[]{:S(2)}) collective-permute-start(bf16[64,2048]{1,0:T(8,128)(2,1)S(1)} %pad_maximum_fusion.14), channel_id=1, source_target_pairs={{0,8},{1,9},{2,10},{3,11},{4,12},{5,13},{6,14},{7,15},{8,0},{9,1},... | collective-permute-start | bytes 786440 | tf_op jit(solution)/shard_map/ppermute | solution.py:476
  204.6 10.9 %collective-permute-start.12 = (bf16[512,512]{1,0:T(8,128)(2,1)S(1)}, bf16[512,512]{1,0:T(8,128)(2,1)S(1)}, u32[]{:S(2)}, u32[]{:S(2)}) collective-permute-start(bf16[512,512]{1,0:T(8,128)(2,1)S(1)} %pad_maximum_fusion.9), channel_id=1, source_target_pairs={{0,16},{1,17},{2,18},{3,19},{4,20},{5,21},{6,22},{7,23},{8,24},{9,... | collective-permute-start | bytes 1572872 | tf_op jit(solution)/shard_map/ppermute | solution.py:476
  206.8 14.4 %collective-permute-start.18 = (bf16[128,2048]{1,0:T(8,128)(2,1)S(1)}, bf16[128,2048]{1,0:T(8,128)(2,1)S(1)}, u32[]{:S(2)}, u32[]{:S(2)}) collective-permute-start(bf16[128,2048]{1,0:T(8,128)(2,1)S(1)} %pad_maximum_fusion.10), channel_id=1, source_target_pairs={{0,16},{1,17},{2,18},{3,19},{4,20},{5,21},{6,22},{7,23},{8,24},{9,... | collective-permute-start | bytes 1572872 | tf_op jit(solution)/shard_map/ppermute | solution.py:476
  215.8 14.9 %collective-permute-start.13 = (bf16[1024,512]{1,0:T(8,128)(2,1)S(1)}, bf16[1024,512]{1,0:T(8,128)(2,1)S(1)}, u32[]{:S(2)}, u32[]{:S(2)}) collective-permute-start(bf16[1024,512]{1,0:T(8,128)(2,1)S(1)} %pad_maximum_fusion.5), channel_id=1, source_target_pairs={{0,8},{1,9},{2,10},{3,11},{4,12},{5,13},{6,14},{7,15},{8,0},{9,1},... | collective-permute-start | bytes 3145736 | tf_op jit(solution)/shard_map/ppermute | solution.py:476
  221.5 11.1 %collective-permute-start.19 = (bf16[256,2048]{1,0:T(8,128)(2,1)S(1)}, bf16[256,2048]{1,0:T(8,128)(2,1)S(1)}, u32[]{:S(2)}, u32[]{:S(2)}) collective-permute-start(bf16[256,2048]{1,0:T(8,128)(2,1)S(1)} %pad_maximum_fusion.6), channel_id=1, source_target_pairs={{0,4},{1,5},{2,6},{3,7},{4,0},{5,1},{6,2},{7,3},{8,12},{9,13},{10,... | collective-permute-start | bytes 3145736 | tf_op jit(solution)/shard_map/ppermute | solution.py:476
  232.6 7.5 %collective-permute-start.14 = (bf16[2048,512]{1,0:T(8,128)(2,1)}, bf16[2048,512]{1,0:T(8,128)(2,1)}, u32[]{:S(2)}, u32[]{:S(2)}) collective-permute-start(bf16[2048,512]{1,0:T(8,128)(2,1)} %pad_maximum_fusion.2), channel_id=1, source_target_pairs={{0,4},{1,5},{2,6},{3,7},{4,0},{5,1},{6,2},{7,3},{8,12},{9,13},{10,... | collective-permute-start | bytes 6291464 | tf_op jit(solution)/shard_map/ppermute | solution.py:476
  (8 other events, 27.3 us)

commit v2 on v1

v2 whole, which is shorter than its diff:
```python
import functools

import jax
import jax.numpy as jnp
import numpy as np
from jax import lax
from jax.experimental import pallas as pl
from jax.experimental.pallas import tpu as pltpu
from jax.sharding import PartitionSpec as P

NB = 32
MAXD = 128
QLEN = 64
PPR = 2

EPS_NORM = 1e-06
LOGIT_SCALE = 50.0
MASKED = -1e30
HIGHEST = lax.Precision.HIGHEST
F32 = jnp.float32
BF16 = jnp.bfloat16
AXES = ("wide", "narrow")
BLK = 128
VMEM_LIMIT = 60 * 1024 * 1024


def bucket_offsets(length):
    offset = np.arange(-(length - 1), length)
    half_count = NB // 2
    exact_span = half_count // 2
    distance = -offset
    bucket = (distance < 0).astype(np.int64) * half_count
    distance = np.abs(distance)
    far_bucket = exact_span + (
        np.log(np.maximum(distance, 1) / exact_span)
        / np.log(MAXD / exact_span)
        * (half_count - exact_span)
    ).astype(np.int64)
    far_bucket = np.minimum(far_bucket, half_count - 1)
    bucket = bucket + np.where(distance < exact_span, distance, far_bucket)
    return bucket.astype(np.int32)


def dot(left, right, left_dim=1, right_dim=0):
    return lax.dot_general(
        left, right, (((left_dim,), (right_dim,)), ((), ())), preferred_element_type=F32
    )


def split_two(values):
    high = values.astype(BF16)
    return high, (values - high.astype(F32)).astype(BF16)


def rms_scale(values):
    return lax.rsqrt(jnp.mean(values * values, axis=-1, keepdims=True) + EPS_NORM)


def norm_back(grad_normed, inputs, scale, gain):
    scaled = grad_normed * gain
    return scale * scaled - inputs * (
        scale * scale * scale * jnp.mean(inputs * scaled, axis=-1, keepdims=True)
    )


def slot_onehot(seg_row, slot_count):
    length = seg_row.shape[1]
    return seg_row == lax.broadcasted_iota(jnp.int32, (slot_count, length), 0)


def gain_row(ref):
    return ref[...].astype(F32).reshape(1, ref.shape[0])


def forward_kernel(
    seg_ref, tok_ref, g1_ref, wq_ref, wk_ref, wv_ref, wo_ref, rel_ref, hot_ref, g2_ref, win_ref, wout_ref,
    n1_ref, q_ref, k_ref, v_ref, p_ref, o_ref, hid_ref, n2_ref, act_ref, abar_ref, m_ref,
    strip_ref, mask_ref, asum_ref, hsum_ref,
):
    step = pl.program_id(0)
    row_count = pl.num_programs(0)
    length, width = tok_ref.shape[1:]
    heads = p_ref.shape[1]
    head_size = width // heads
    blocks = length // BLK
    slots = abar_ref.shape[0] // m_ref.shape[0] * (length // QLEN)

    @pl.when(step == 0)
    def _():
        off_bias = dot(rel_ref[...], hot_ref[...], 0, 0)
        for head in range(heads):
            wide = jnp.broadcast_to(off_bias[head : head + 1, :], (BLK, 2 * length))
            rolled = pltpu.roll(wide, 2 * length - BLK + 1, 1, stride=1, stride_axis=0)
            strip_ref[head] = rolled[:, : 2 * length - BLK]

    x = tok_ref[0].astype(F32)
    n1 = (x * rms_scale(x) * gain_row(g1_ref)).astype(BF16)
    n1_ref[0] = n1
    q_ref[0] = dot(n1, wq_ref[...]).astype(BF16)
    k_ref[0] = dot(n1, wk_ref[...]).astype(BF16)
    v_ref[0] = dot(n1, wv_ref[...]).astype(BF16)
    onehot = slot_onehot(seg_ref[pl.ds(step, 1), :], slots)
    onehot_f = onehot.astype(F32)
    onehot_low = onehot_f.astype(BF16)
    same = dot(onehot_low, onehot_low, 0, 0)
    mask_ref[...] = jnp.where(same > 0.5, 0.0, MASKED)
    low_lane = lax.broadcasted_iota(jnp.int32, (BLK, 2 * head_size), 1) < head_size

    def pair(index, carry):
        lanes = pl.ds(pl.multiple_of(index * 2 * head_size, 2 * head_size), 2 * head_size)
        k_pair = k_ref[0, :, lanes]
        v_pair = v_ref[0, :, lanes]
        for block in range(blocks):
            rows = slice(block * BLK, (block + 1) * BLK)
            q_pair = q_ref[0, rows, lanes]
            for part in range(2):
                head = index * 2 + part
                keep = low_lane if part == 0 else jnp.logical_not(low_lane)
                q_head = jnp.where(keep, q_pair, jnp.zeros_like(q_pair))
                start = (blocks - 1 - block) * BLK
                scores = dot(q_head, k_pair, 1, 1)
                scores = scores + strip_ref[head, :, start : start + length] + mask_ref[rows, :]
                top = jnp.max(scores, axis=-1, keepdims=True)
                exps = jnp.exp(scores - top)
                total = jnp.sum(exps, axis=-1, keepdims=True)
                p_ref[0, head, rows, :] = (exps * (1.0 / total)).astype(BF16)
        low_all = lax.broadcasted_iota(jnp.int32, (length, 2 * head_size), 1) < head_size
        mixed = [dot(p_ref[0, index * 2 + part], v_pair) for part in range(2)]
        o_ref[0, :, lanes] = jnp.where(low_all, mixed[0], mixed[1]).astype(BF16)
        return carry

    lax.fori_loop(0, heads // 2, pair, 0)
    hidden = x + dot(o_ref[0], wo_ref[...])
    hid_ref[0] = hidden
    n2 = (hidden * rms_scale(hidden) * gain_row(g2_ref)).astype(BF16)
    n2_ref[0] = n2
    act = jnp.maximum(dot(n2, win_ref[...]), 0.0).astype(BF16)
    act_ref[0] = act
    counts = jnp.maximum(jnp.sum(onehot_f, axis=-1, keepdims=True), 1.0)
    asum = dot(onehot_low, act) / counts
    high, low = split_two(hidden)
    hsum = (dot(onehot_low, high) + dot(onehot_low, low)) / counts
    asum_ref[pl.ds(step * slots, slots), :] = asum
    hsum_ref[pl.ds(step * slots, slots), :] = hsum

    @pl.when(step == row_count - 1)
    def _():
        high, low = split_two(asum_ref[...])
        abar_ref[...] = high
        pooled = hsum_ref[...] + dot(high, wout_ref[...]) + dot(low, wout_ref[...])
        m_ref[...] = pooled.astype(BF16)


def whole(shape):
    return pl.BlockSpec(shape, lambda r: (0,) * len(shape))


def per_row(shape):
    return pl.BlockSpec((1,) + shape, lambda r: (r,) + (0,) * len(shape))


def forward(seg, tokens, g1, wq, wk, wv, wo, rel_bias, hot, g2, win, wout, slots):
    rows, length, width = tokens.shape
    heads = rel_bias.shape[1]
    inner = win.shape[1]
    low = lambda *s: jax.ShapeDtypeStruct(s, BF16)
    rlw = (rows, length, width)
    return pl.pallas_call(
        forward_kernel,
        name="forward_rows",
        grid=(rows,),
        in_specs=[whole(seg.shape), per_row((length, width))]
        + [whole(a.shape) for a in (g1, wq, wk, wv, wo, rel_bias, hot, g2, win, wout)],
        out_specs=[per_row((length, width))] * 4
        + [per_row((heads, length, length))]
        + [per_row((length, width))] * 3
        + [per_row((length, inner)), whole((rows * slots, inner)), whole((rows * slots, width))],
        out_shape=[low(*rlw)] * 4
        + [low(rows, heads, length, length), low(*rlw), jax.ShapeDtypeStruct(rlw, F32), low(*rlw)]
        + [low(rows, length, inner), low(rows * slots, inner), low(rows * slots, width)],
        scratch_shapes=[
            pltpu.VMEM((heads, BLK, 2 * length - BLK), F32),
            pltpu.VMEM((length, length), F32),
            pltpu.VMEM((rows * slots, inner), F32),
            pltpu.VMEM((rows * slots, width), F32),
        ],
        compiler_params=pltpu.CompilerParams(vmem_limit_bytes=VMEM_LIMIT),
    )(seg, tokens, g1, wq, wk, wv, wo, rel_bias, hot, g2, win, wout)


def chunk_masks(order):
    count = len(order)
    return [
        sum(bit for place, bit in enumerate(order) if p >> (count - 1 - place) & 1)
        for p in range(1 << count)
    ]


def padded_rows(rows, total):
    return -(-rows // (16 * total)) * 16 * total


def take_chunks(source_ref, keep_ref, send_ref, where, masks):
    total = len(masks)
    chunk = 2 * keep_ref.shape[0] // total
    for p in range(total):
        first = pl.multiple_of((where ^ masks[p]) * chunk, chunk)
        values = source_ref[pl.ds(first, chunk), :].astype(BF16)
        ref, at = (keep_ref, p) if p < total // 2 else (send_ref, p - total // 2)
        ref[at * chunk : (at + 1) * chunk, :] = values


def contrast(pooled, targets, w_proj, slots):
    half = pooled.shape[0] // 2
    z = dot(pooled, w_proj)
    inv = lax.rsqrt(jnp.sum(z * z, axis=-1, keepdims=True) + EPS_NORM)
    unit = z * inv
    emb = unit.astype(BF16)
    emb_q, emb_p = emb[:half], emb[half:]
    logits = LOGIT_SCALE * dot(emb_p, emb_q, 1, 1)
    line = lax.broadcasted_iota(jnp.int32, (half, half), 0)
    logits = jnp.where(line % slots < PPR, logits, MASKED)
    hits = line == (targets // PPR) * slots + targets % PPR
    top = jnp.max(logits, axis=0, keepdims=True)
    exps = jnp.exp(logits - top)
    sums = jnp.sum(exps, axis=0, keepdims=True)
    picked = jnp.sum(jnp.where(hits, logits, 0.0), axis=0, keepdims=True)
    loss = jnp.sum(top + jnp.log(sums) - picked, axis=1, keepdims=True)
    weights = (exps / sums - hits.astype(F32)).astype(BF16)
    grad_q = LOGIT_SCALE * dot(weights, emb_p, 0, 0)
    grad_p = LOGIT_SCALE * dot(weights, emb_q)
    grad = jnp.concatenate([grad_q, grad_p], axis=0)
    dz = (inv * (grad - unit * jnp.sum(grad * unit, axis=-1, keepdims=True))).astype(BF16)
    grad_proj = dot(pooled, dz, 0, 0)
    dm = dot(dz, w_proj, 1, 1)
    return loss, grad_proj, dm


def contrast_kernel(
    where_ref, near_ref, far_ref, target_ref, wp_ref,
    loss_ref, gproj_ref, own_ref, low_ref, pooled_ref, dm_ref, *, slots, masks
):
    total = len(masks)
    chunk = own_ref.shape[0]
    firsts = [pl.multiple_of((where_ref[0] ^ mask) * chunk, chunk) for mask in masks]
    for p in range(total):
        ref, at = (near_ref, p) if p < total // 2 else (far_ref, p - total // 2)
        pooled_ref[pl.ds(firsts[p], chunk), :] = ref[at * chunk : (at + 1) * chunk, :]
    targets = target_ref[...].reshape(1, target_ref.shape[0])
    loss, grad_proj, dm = contrast(pooled_ref[...], targets, wp_ref[...], slots)
    loss_ref[...] = loss
    gproj_ref[...] = grad_proj
    dm_ref[...] = dm
    own_ref[...] = dm_ref[pl.ds(firsts[0], chunk), :]
    low_ref[...] = dm.astype(BF16)


def contrast_call(where, near, far, targets, w_proj, slots, masks):
    count, width = 2 * near.shape[0], near.shape[1]
    total = len(masks)
    chunk = count // total
    if count > 1024:
        both = jnp.concatenate([near, far], axis=0).reshape(total, chunk, width)
        places = where ^ jnp.asarray(np.asarray(masks, np.int32))
        pooled = jnp.zeros_like(both).at[places].set(both).reshape(count, width)
        loss, grad_proj, dm = contrast(pooled, targets.reshape(1, -1), w_proj, slots)
        own = dm.reshape(total, chunk, width)[where[0]]
        return loss, grad_proj, own, dm.astype(BF16)
    vmem = pl.BlockSpec(memory_space=pltpu.VMEM)
    return pl.pallas_call(
        functools.partial(contrast_kernel, slots=slots, masks=masks),
        name="contrast_all",
        in_specs=[pl.BlockSpec(memory_space=pltpu.SMEM)] + [vmem] * 4,
        out_shape=[
            jax.ShapeDtypeStruct((1, 1), F32),
            jax.ShapeDtypeStruct(w_proj.shape, F32),
            jax.ShapeDtypeStruct((chunk, width), F32),
            jax.ShapeDtypeStruct((count, width), BF16),
        ],
        scratch_shapes=[pltpu.VMEM((count, width), BF16), pltpu.VMEM((count, width), F32)],
        compiler_params=pltpu.CompilerParams(vmem_limit_bytes=VMEM_LIMIT),
    )(where, near, far, targets, w_proj)


def ffn_out_kernel(where_ref, near_ref, far_ref, dm_ref, out_ref, all_ref, *, masks):
    total = len(masks)
    chunk = all_ref.shape[0] // total
    for p in range(total):
        ref, at = (near_ref, p) if p < total // 2 else (far_ref, p - total // 2)
        first = pl.multiple_of((where_ref[0] ^ masks[p]) * chunk, chunk)
        all_ref[pl.ds(first, chunk), :] = ref[at * chunk : (at + 1) * chunk, :]
    out_ref[...] = dot(all_ref[...], dm_ref[...], 0, 0)


def ffn_out_grad(where, near, far, dm, masks):
    half, inner = near.shape
    width = dm.shape[1]
    side = pl.BlockSpec((half, width), lambda i: (0, i))
    return pl.pallas_call(
        functools.partial(ffn_out_kernel, masks=masks),
        name="ffn_out_grad",
        grid=(inner // width,),
        in_specs=[pl.BlockSpec(memory_space=pltpu.SMEM), side, side, whole(dm.shape)],
        out_specs=pl.BlockSpec((width, width), lambda i: (i, 0)),
        out_shape=jax.ShapeDtypeStruct((inner, width), F32),
        scratch_shapes=[pltpu.VMEM((2 * half, width), BF16)],
        compiler_params=pltpu.CompilerParams(vmem_limit_bytes=VMEM_LIMIT),
    )(where, near, far, dm)


def ffn_back_kernel(
    where_ref, seg_ref, dm_ref, act_ref, n2_ref, hid_ref, o_ref, g2_ref, win_ref, wout_ref, wo_ref,
    dh_ref, do_ref, keep_ref, send_ref, g2grad_ref,
    acc_ref, g2_acc, *, masks
):
    step = pl.program_id(0)
    last = pl.num_programs(0) - 1
    length, width = hid_ref.shape[1:]
    slots = length // QLEN

    onehot = slot_onehot(seg_ref[pl.ds(step, 1), :], slots)
    onehot_f = onehot.astype(F32)
    onehot_low = onehot_f.astype(BF16)
    counts = jnp.maximum(jnp.sum(onehot_f, axis=-1, keepdims=True), 1.0)
    dy_slot = dm_ref[pl.ds(pl.multiple_of(step * slots, slots), slots), :] / counts
    dyb_slot = dy_slot.astype(BF16)
    dact_slot = dot(dyb_slot, wout_ref[...], 1, 1).astype(BF16)
    dact = dot(onehot_low, dact_slot, 0, 0).astype(BF16)
    act = act_ref[0]
    du = jnp.where(act > 0, dact, jnp.zeros_like(dact))
    win_part = dot(n2_ref[0], du, 0, 0)
    dn2 = dot(du, win_ref[...], 1, 1)
    hidden = hid_ref[0]
    scale = rms_scale(hidden)
    g2_part = jnp.sum(dn2 * hidden * scale, axis=0, keepdims=True)
    high, low = split_two(dy_slot)
    dy = dot(onehot_low, high, 0, 0) + dot(onehot_low, low, 0, 0)
    dh = dy + norm_back(dn2, hidden, scale, gain_row(g2_ref))
    dh_ref[0] = dh
    dhb = dh.astype(BF16)
    do_ref[0] = dot(dhb, wo_ref[...], 1, 1).astype(BF16)
    wo_part = dot(o_ref[0], dhb, 0, 0)

    inner = win_part.shape[1]
    parts = [win_part[:, at : at + width] for at in range(0, inner, width)] + [wo_part]

    @pl.when(step == 0)
    def _():
        for index, part in enumerate(parts):
            acc_ref[index * width : (index + 1) * width, :] = part
        if acc_ref.shape[0] > len(parts) * width:
            acc_ref[len(parts) * width :, :] = jnp.zeros_like(acc_ref[len(parts) * width :, :])
        g2_acc[...] = g2_part

    @pl.when(step > 0)
    def _():
        for index, part in enumerate(parts):
            acc_ref[index * width : (index + 1) * width, :] += part
        g2_acc[...] += g2_part

    @pl.when(step == last)
    def _():
        take_chunks(acc_ref, keep_ref, send_ref, where_ref[0], masks)
        g2grad_ref[...] = g2_acc[...]


def ffn_back(where, seg, dm, act, n2, hidden, mixed, g2, win, wout, wo, masks):
    rows, length, width = hidden.shape
    inner = win.shape[1]
    lines = padded_rows(inner + width, len(masks))
    return pl.pallas_call(
        functools.partial(ffn_back_kernel, masks=masks),
        name="ffn_back",
        grid=(rows,),
        in_specs=[pl.BlockSpec(memory_space=pltpu.SMEM), whole(seg.shape), whole(dm.shape)]
        + [per_row((length, inner))]
        + [per_row((length, width))] * 3
        + [whole(a.shape) for a in (g2, win, wout, wo)],
        out_specs=[per_row((length, width))] * 2
        + [whole((lines // 2, width))] * 2
        + [whole((1, width))],
        out_shape=[
            jax.ShapeDtypeStruct(hidden.shape, F32),
            jax.ShapeDtypeStruct(hidden.shape, BF16),
            jax.ShapeDtypeStruct((lines // 2, width), BF16),
            jax.ShapeDtypeStruct((lines // 2, width), BF16),
            jax.ShapeDtypeStruct((1, width), F32),
        ],
        scratch_shapes=[
            pltpu.VMEM((lines, width), F32),
            pltpu.VMEM((1, width), F32),
        ],
        compiler_params=pltpu.CompilerParams(vmem_limit_bytes=VMEM_LIMIT),
    )(where, seg, dm, act, n2, hidden, mixed, g2, win, wout, wo)


def attn_back_kernel(*refs, group, masks):
    where_ref, n1_ref, q_ref, k_ref, v_ref, p_ref, o_ref, do_ref = refs[:8]
    before_refs = refs[8 : 8 + group]
    tail = refs[8 + group :]
    dqkv_ref, band_ref, grad_refs = tail[0], tail[1], tail[2:-4]
    dkt_ref, dvt_ref, acc_ref, wacc_ref = tail[-4:]
    step = pl.program_id(0)
    last = pl.num_programs(0) - 1
    length, width = n1_ref.shape[1:]
    heads = p_ref.shape[1]
    own_width = q_ref.shape[2]
    head_size = own_width // heads
    blocks = length // BLK
    low_lane = lax.broadcasted_iota(jnp.int32, (length, 2 * head_size), 1) < head_size

    @pl.when(step == 0)
    def _():
        acc_ref[...] = jnp.zeros_like(acc_ref)

    def pair(index, carry):
        lanes = pl.ds(pl.multiple_of(index * 2 * head_size, 2 * head_size), 2 * head_size)
        q_pair = q_ref[0, :, lanes]
        k_pair = k_ref[0, :, lanes]
        v_pair = v_ref[0, :, lanes]
        do_pair = do_ref[0, :, lanes]
        q_turned = q_pair.T
        do_turned = do_pair.T
        product = do_pair.astype(F32) * o_ref[0, :, lanes].astype(F32)
        dq_parts = []
        for part in range(2):
            head = index * 2 + part
            keep = low_lane if part == 0 else jnp.logical_not(low_lane)
            do_head = jnp.where(keep, do_pair, jnp.zeros_like(do_pair))
            delta = jnp.sum(jnp.where(keep, product, 0.0), axis=-1, keepdims=True)
            probs = p_ref[0, head]
            dprobs = dot(do_head, v_pair, 1, 1)
            ds = probs.astype(F32) * (dprobs - delta)
            ds_low = ds.astype(BF16)
            sums = {}
            for i in range(blocks):
                for j in range(blocks):
                    place = max(-2, min(2, j - i)) + 2
                    tile = ds[i * BLK : (i + 1) * BLK, j * BLK : (j + 1) * BLK]
                    sums[place] = tile if place not in sums else sums[place] + tile
            for place, value in sums.items():
                acc_ref[head, :, place * BLK : (place + 1) * BLK] += value
            dq_parts.append(dot(ds_low, k_pair))
            own = slice(part * head_size, (part + 1) * head_size)
            place = pl.ds(pl.multiple_of(head * head_size, head_size), head_size)
            dkt_ref[place, :] = dot(q_turned[own], ds_low).astype(BF16)
            dvt_ref[place, :] = dot(do_turned[own], probs).astype(BF16)
        dqkv_ref[0, 0, :, lanes] = jnp.where(low_lane, dq_parts[0], dq_parts[1]).astype(BF16)
        return carry

    lax.fori_loop(0, heads // 2, pair, 0)
    dq = dqkv_ref[0, 0]
    dk = dkt_ref[...].T
    dv = dvt_ref[...].T
    dqkv_ref[0, 1] = dk
    dqkv_ref[0, 2] = dv
    parts = [dot(n1_ref[0], d, 0, 0) for d in (dq, dk, dv)]

    here = slice(group * own_width, (group + 1) * own_width)
    if len(grad_refs) == 1:
        here = slice(0, own_width)

    @pl.when(step == 0)
    def _():
        for index in range(3):
            wacc_ref[index * width : (index + 1) * width, here] = parts[index]

    @pl.when(step > 0)
    def _():
        for index in range(3):
            wacc_ref[index * width : (index + 1) * width, here] += parts[index]

    @pl.when(step == last)
    def _():
        if len(grad_refs) == 1:
            grad_refs[0][...] = wacc_ref[...].astype(BF16)
        else:
            for index, ref in enumerate(before_refs):
                lanes = slice(index * own_width, (index + 1) * own_width)
                wacc_ref[: 3 * width, lanes] = ref[...].astype(F32)
            if wacc_ref.shape[0] > 3 * width:
                wacc_ref[3 * width :, :] = jnp.zeros_like(wacc_ref[3 * width :, :])
            take_chunks(wacc_ref, grad_refs[0], grad_refs[1], where_ref[0], masks)
        for head in range(heads):
            far_low = jnp.sum(acc_ref[head, :, :BLK], axis=0, keepdims=True)
            far_high = jnp.sum(acc_ref[head, :, 4 * BLK :], axis=0, keepdims=True)
            band = jnp.concatenate(
                [acc_ref[head, :, BLK : 4 * BLK], jnp.zeros((BLK, BLK), F32)], axis=1
            )
            rows = BLK // 2
            while rows >= 1:
                band = band[:rows] + pltpu.roll(band[rows:], 4 * BLK - rows, 1)
                rows //= 2
            band_ref[head : head + 1, : 4 * BLK] = band
            band_ref[head : head + 1, 4 * BLK : 5 * BLK] = far_low
            band_ref[head : head + 1, 5 * BLK :] = far_high


def attn_back(where, n1, q, k, v, probs, mixed, do, before, groups, masks):
    group = len(before)
    rows, length, width = n1.shape
    heads = probs.shape[1] // groups
    own_width = width // groups
    lanes = pl.BlockSpec((1, length, own_width), lambda r: (r, 0, group))
    low = lambda *s: jax.ShapeDtypeStruct(s, BF16)
    if group < groups - 1:
        grads = [low(3 * width, own_width)]
        acc = (3 * width, own_width)
    else:
        lines = padded_rows(3 * width, len(masks))
        grads = [low(lines // 2, width)] * 2
        acc = (lines, width)
    return pl.pallas_call(
        functools.partial(attn_back_kernel, group=group, masks=masks),
        name=f"attn_back_{group}",
        grid=(rows,),
        in_specs=[pl.BlockSpec(memory_space=pltpu.SMEM), per_row((length, width))]
        + [lanes] * 3
        + [pl.BlockSpec((1, heads, length, length), lambda r: (r, group, 0, 0)), lanes, lanes]
        + [whole(g.shape) for g in before],
        out_specs=[per_row((3, length, own_width)), whole((heads, 6 * BLK))]
        + [whole(g.shape) for g in grads],
        out_shape=[
            low(rows, 3, length, own_width),
            jax.ShapeDtypeStruct((heads, 6 * BLK), F32),
        ]
        + grads,
        scratch_shapes=[
            pltpu.VMEM((own_width, length), BF16),
            pltpu.VMEM((own_width, length), BF16),
            pltpu.VMEM((heads, BLK, 5 * BLK), F32),
            pltpu.VMEM(acc, F32),
        ],
        compiler_params=pltpu.CompilerParams(vmem_limit_bytes=VMEM_LIMIT),
    )(where, n1, q, k, v, probs, mixed, do, *before)


def finish_kernel(*refs, groups):
    tok_ref, dh_ref, g1_ref, g2grad_ref, table_ref, wq_ref, wk_ref, wv_ref = refs[:8]
    dqkv_refs, band_refs = refs[8 : 8 + groups], refs[8 + groups : 8 + 2 * groups]
    tgrad_ref, small_out, g1_acc, small_ref = refs[8 + 2 * groups :]
    step = pl.program_id(0)
    last = pl.num_programs(0) - 1
    own_width = dqkv_refs[0].shape[3]
    heads = band_refs[0].shape[0]
    dn1 = None
    for index, weight in enumerate((wq_ref, wk_ref, wv_ref)):
        whole_grad = jnp.concatenate([ref[0, index] for ref in dqkv_refs], axis=1)
        part = dot(whole_grad, weight[...], 1, 1)
        dn1 = part if dn1 is None else dn1 + part
    x = tok_ref[0].astype(F32)
    scale = rms_scale(x)
    g1_part = jnp.sum(dn1 * x * scale, axis=0, keepdims=True)
    tgrad_ref[0] = (dh_ref[0] + norm_back(dn1, x, scale, gain_row(g1_ref))).astype(BF16)

    @pl.when(step == 0)
    def _():
        g1_acc[...] = g1_part

    @pl.when(step > 0)
    def _():
        g1_acc[...] += g1_part

    @pl.when(step == last)
    def _():
        width = small_ref.shape[1]
        small_ref[...] = jnp.zeros_like(small_ref)
        for at in range(width // BLK):
            lanes = slice(at * BLK, (at + 1) * BLK)
            small_ref[at : at + 1, BLK : 2 * BLK] = g1_acc[:, lanes]
            small_ref[at : at + 1, 2 * BLK : 3 * BLK] = g2grad_ref[:, lanes]
        for group in range(groups):
            band = band_refs[group][...]
            high = band.astype(BF16)
            rest = band - high.astype(F32)
            low = rest.astype(BF16)
            least = (rest - low.astype(F32)).astype(BF16)
            table = table_ref[...]
            bias = dot(high, table) + dot(low, table) + dot(least, table)
            small_ref[group * heads : (group + 1) * heads, : bias.shape[1]] = bias
        small_out[...] = small_ref[...].astype(BF16)


def finish(tokens, dh, g1, g2grad, table, wq, wk, wv, dqkvs, bands):
    rows, length, width = tokens.shape
    groups = len(dqkvs)
    lead = groups * bands[0].shape[0]
    return pl.pallas_call(
        functools.partial(finish_kernel, groups=groups),
        name="finish_rows",
        grid=(rows,),
        in_specs=[per_row((length, width))] * 2
        + [whole(a.shape) for a in (g1, g2grad, table, wq, wk, wv)]
        + [per_row(d.shape[1:]) for d in dqkvs]
        + [whole(b.shape) for b in bands],
        out_specs=[per_row((length, width)), whole((lead, width))],
        out_shape=[
            jax.ShapeDtypeStruct(tokens.shape, BF16),
            jax.ShapeDtypeStruct((lead, width), BF16),
        ],
        scratch_shapes=[pltpu.VMEM((1, width), F32), pltpu.VMEM((lead, width), F32)],
        compiler_params=pltpu.CompilerParams(vmem_limit_bytes=VMEM_LIMIT),
    )(tokens, dh, g1, g2grad, table, wq, wk, wv, *dqkvs, *bands)


def band_table(length):
    buckets = bucket_offsets(length)
    zero = length - 1
    table = np.zeros((6 * BLK, NB), np.float32)
    for column in range(4 * BLK):
        offset = column - BLK if column < 3 * BLK else column - 5 * BLK
        if -2 * BLK < offset < 2 * BLK and abs(offset) < length:
            table[column, buckets[zero + offset]] = 1.0
    far = buckets[: zero - BLK], buckets[zero + BLK + 1 :]
    assert len(set(far[0])) == 1 and len(set(far[1])) == 1
    table[4 * BLK : 5 * BLK, far[0][0]] = 1.0
    table[5 * BLK :, far[1][0]] = 1.0
    return table


def unpack_kernel(where_ref, *refs, masks, weights):
    big_refs, qkv_refs = refs[0:2], refs[2:4]
    outs = refs[4:-3]
    big_all, qkv_all, small_all = refs[-3:]
    win_out, wo_out, wq_out, wk_out, wv_out, g1_out, g2_out, bias_out = outs
    total = len(masks)
    width = wo_out.shape[1]
    lead = bias_out.shape[0]
    for p in range(total):
        side, at = (0, p) if p < total // 2 else (1, p - total // 2)
        chunk = 2 * big_refs[0].shape[0] // total
        first = pl.multiple_of((where_ref[0] ^ masks[p]) * chunk, chunk)
        big_all[pl.ds(first, chunk), :] = big_refs[side][at * chunk : (at + 1) * chunk, :].astype(F32)
        rows = 2 * qkv_refs[0].shape[0] // total
        chunk = rows - lead
        first = pl.multiple_of((where_ref[0] ^ masks[p]) * chunk, chunk)
        piece = qkv_refs[side][at * rows : (at + 1) * rows, :].astype(F32)
        qkv_all[pl.ds(first, chunk), :] = piece[:chunk]
        first = pl.multiple_of((where_ref[0] ^ masks[p]) * lead, lead)
        small_all[pl.ds(first, lead), :] = piece[chunk:, : small_all.shape[1]]
    small = small_all[:lead, :]
    for p in range(1, total):
        small = small + small_all[p * lead : (p + 1) * lead, :]
    parts = win_out.shape[1] // width
    for part in range(parts):
        win_out[:, part * width : (part + 1) * width] = big_all[part * width : (part + 1) * width, :]
    wo_out[...] = big_all[parts * width : (parts + 1) * width, :]
    for index, ref in enumerate((wq_out, wk_out, wv_out)):
        ref[...] = qkv_all[index * width : (index + 1) * width, :]
    for at in range(width // BLK):
        lanes = slice(at * BLK, (at + 1) * BLK)
        g1_out[:, lanes] = small[at : at + 1, BLK : 2 * BLK]
        g2_out[:, lanes] = small[at : at + 1, 2 * BLK : 3 * BLK]
    bias_out[...] = small[:, : bias_out.shape[1]]


def unpack(where, big, qkv, inner, width, heads, masks):
    full = lambda *s: jax.ShapeDtypeStruct(s, F32)
    vmem = pl.BlockSpec(memory_space=pltpu.VMEM)
    total = len(masks)
    return pl.pallas_call(
        functools.partial(unpack_kernel, masks=masks, weights=None),
        name="unpack_grads",
        in_specs=[pl.BlockSpec(memory_space=pltpu.SMEM)] + [vmem] * 4,
        out_shape=[full(width, inner)] + [full(width, width)] * 4 + [full(1, width)] * 2 + [full(heads, NB)],
        scratch_shapes=[
            pltpu.VMEM((2 * big[0].shape[0], width), F32),
            pltpu.VMEM((2 * qkv[0].shape[0] - total * heads, width), F32),
            pltpu.VMEM((total * heads, 3 * BLK), F32),
        ],
        compiler_params=pltpu.CompilerParams(vmem_limit_bytes=VMEM_LIMIT),
    )(where, *big, *qkv)


def bit_groups(wide, narrow):
    total = wide * narrow
    assert total & (total - 1) == 0 and narrow & (narrow - 1) == 0
    bits = [1 << s for s in range(total.bit_length() - 1)]
    outer = [b for b in bits if b >= narrow]
    inner = [b for b in bits if b < narrow]
    pairs = lambda items: [items[i : i + 2] for i in range(0, len(items), 2)]
    return [outer[:1]] + pairs(outer[1:]) + pairs(inner)


def group_masks(group):
    return chunk_masks(group)[1:]


def swap(values, mask, total):
    return lax.ppermute(values, AXES, [(i, i ^ mask) for i in range(total)])


def gather_stages(values, groups, total):
    pieces = [values]
    for group in reversed(groups):
        values = pieces[0] if len(pieces) == 1 else jnp.concatenate(pieces, axis=0)
        pieces = [values] + [swap(values, mask, total) for mask in group_masks(group)]
    return pieces


def split_rows(values, count):
    rows = values.shape[0] // count
    return [values[i * rows : (i + 1) * rows] for i in range(count)]


def scatter_stages(keep, send, groups, total):
    blocks = [keep, send]
    for index, group in enumerate(groups):
        got = [swap(b, mask, total) for b, mask in zip(blocks[1:], group_masks(group))]
        count = 1 << len(groups[index + 1]) if index + 1 < len(groups) else 1
        parts = [split_rows(b, count) for b in [blocks[0]] + got]
        blocks = []
        for column in zip(*parts):
            total_part = column[0].astype(F32)
            for other in column[1:]:
                total_part = total_part + other.astype(F32)
            blocks.append(total_part.astype(BF16))
    return blocks[0]


GROUPS = 2


def local(
    tokens, seg_ids, positives, norm1_gain, w_query, w_key, w_value, w_attn_out,
    rel_bias, norm2_gain, w_in, w_ffn_out, w_proj,
):
    rows, length, width = tokens.shape
    heads = rel_bias.shape[1]
    slots = length // QLEN
    inner = w_in.shape[1]
    wide, narrow = lax.axis_size("wide"), lax.axis_size("narrow")
    total = wide * narrow
    linear = lax.axis_index("wide") * narrow + lax.axis_index("narrow")
    where = jnp.full((1,), linear, jnp.int32)
    groups = bit_groups(wide, narrow)
    masks = chunk_masks([b for g in groups for b in g])
    buckets = bucket_offsets(length)
    hot = np.zeros((NB, 2 * length), np.float32)
    hot[buckets, np.arange(2 * length - 1)] = 1.0

    n1, q, k, v, probs, mixed, hidden, n2, act, abar, pooled = forward(
        seg_ids, tokens, norm1_gain, w_query, w_key, w_value, w_attn_out, rel_bias,
        jnp.asarray(hot, BF16), norm2_gain, w_in, w_ffn_out, slots,
    )
    near, far = gather_stages(pooled, groups, total)
    loss, grad_proj, dm_own, dm_low = contrast_call(
        where, near, far, positives, w_proj, slots, masks
    )
    dh, do, big_keep, big_send, grad_g2 = ffn_back(
        where, seg_ids, dm_own, act, n2, hidden, mixed, norm2_gain, w_in, w_ffn_out, w_attn_out,
        masks,
    )
    big = scatter_stages(big_keep, big_send, groups, total)
    big = gather_stages(big, groups, total)
    dqkvs, bands, before = [], [], []
    for _ in range(GROUPS):
        dqkv, band, *grads = attn_back(
            where, n1, q, k, v, probs, mixed, do, before, GROUPS, masks
        )
        dqkvs.append(dqkv)
        bands.append(band)
        before = before + grads[:1]
    tokens_grad, small = finish(
        tokens, dh, norm1_gain, grad_g2, jnp.asarray(band_table(length), BF16),
        w_query, w_key, w_value, dqkvs, bands,
    )
    qkv = scatter_stages(grads[0], grads[1], groups, total)
    qkv = gather_stages(jnp.concatenate([qkv, small], axis=0), groups, total)

    grad_ffn_out = ffn_out_grad(where, *gather_stages(abar, groups, total), dm_low, masks)

    win, wo, wq, wk, wv, grad_g1, grad_g2, grad_bias = unpack(
        where, big, qkv, inner, width, heads, masks
    )
    return (
        loss[0, 0],
        tokens_grad,
        grad_g1[0],
        wq,
        wk,
        wv,
        wo,
        grad_bias.T,
        grad_g2[0],
        win,
        grad_ffn_out,
        grad_proj,
    )


def solution(mesh):
    rows = P(AXES, None, None)
    in_specs = (rows, P(AXES, None)) + (P(),) * 11
    out_specs = (P(), rows) + (P(),) * 10
    return jax.shard_map(local, mesh=mesh, in_specs=in_specs, out_specs=out_specs, check_vma=False)
```

time: 252 us -> 207 us (0.82); the launches traced: 249 us -> 207 us
  waiting for transfers between devices: 86.9 us -> 60.7 us
  other arithmetic: 22.3 us -> 3.22 us
  starting transfers between devices: 37 us -> 44.9 us
  matrix products: 5.93 us -> 0 us
    ppermute x20 -> x42, waiting for transfers between devices: 86.9 us -> 60.7 us  [swap(): return lax.ppermute(values, AXES, [(i, i ^ mask) for i in range(total)])]
    pallas_call x3 -> x7, Pallas kernels: 43.2 us -> 59.5 us  [the longest x2 21.7 us: attn_back(): pl.pallas_call(functools.partial(attn_back_kernel, group=group, masks=mas...]
    pallas_call x1, Pallas kernels: 39.1 us -> 24.9 us  [forward(): pl.pallas_call(forward_kernel, name='forward_rows', grid=(rows,), in_spec...]
    ppermute x20 -> x42, starting transfers between devices: 37 us -> 44.9 us  [swap(): return lax.ppermute(values, AXES, [(i, i ^ mask) for i in range(total)])]
    convert_element_type x11 -> x4, other arithmetic: 9.1 us -> 1.45 us  [scatter_stages(): blocks.append(total_part.astype(BF16))]
    unnamed x25 -> x48, local copies, waits for them, and re-layouts: 4.28 us -> 10.8 us
    dot_general x3 -> x0, matrix products: 5.93 us -> none  [the longest x2 4.89 us: dot(): lax.dot_general(left, right, (((left_dim,), (right_dim,)), ((), ())), pre...]
    select_n x15 -> x0, other arithmetic: 5.17 us -> none  [gather_rows(): jnp.where(high, other, values)]
  transfers between devices with their start and end apart: 20 -> 42, of which waited for: 16 -> 20; matrix products, arithmetic and copies ran while one was open for 4% -> 6% of each run, Pallas kernels for 0% -> 26%
where the time goes in v2:
time: 207 us
  Pallas kernels  84.4 us (41%)
  waiting for transfers between devices  60.7 us (29%)
  starting transfers between devices  44.9 us (22%)
  local copies, waits for them, and re-layouts  12.9 us (6%)
  other arithmetic  3.22 us (2%)
    ppermute x42, waiting for transfers between devices, swap(): return lax.ppermute(values, AXES, [(i, i ^ mask) for i in range(total)])  60.7 us
    ppermute x42, starting transfers between devices, swap(): return lax.ppermute(values, AXES, [(i, i ^ mask) for i in range(total)])  44.9 us
    pallas_call x1, Pallas kernels, forward(): pl.pallas_call(forward_kernel, name='forward_rows', grid=(rows,), in_spec...  24.9 us
    pallas_call x2, Pallas kernels, attn_back(): pl.pallas_call(functools.partial(attn_back_kernel, group=group, masks=mas...  21.7 us
    pallas_call x1, Pallas kernels, ffn_back(): pl.pallas_call(functools.partial(ffn_back_kernel, masks=masks), name='ffn...  15.7 us
    unnamed x48, local copies, waits for them, and re-layouts  10.8 us
    pallas_call x1, Pallas kernels, finish(): pl.pallas_call(functools.partial(finish_kernel, groups=groups), name='fin...  6.56 us
    pallas_call x1, Pallas kernels, unpack(): pl.pallas_call(functools.partial(unpack_kernel, masks=masks, weights=None...  6.12 us
  transfers between devices with their start and end apart: 42, of which 20 were waited for; matrix products, arithmetic and copies ran while one was open for 6% of the time, Pallas kernels for 26%

profile of v2, /device:TPU:0, one launch (start us, length us, event | category | flops | bytes accessed | tf_op | source)
XLA Modules:
  0.0 206.9 jit_solution(14344116199205851840)
XLA Ops:
  2.0 24.9 %forward_rows.1 = (bf16[2,512,512]{2,1,0:T(8,128)(2,1)}, bf16[2,512,512]{2,1,0:T(8,128)(2,1)}, bf16[2,512,512]{2,1,0:T(8,128)(2,1)}, bf16[2,512,512]{2,1,0:T(8,1...) custom-call(s32[2,512]{1,0:T(2,128)} %seg_ref.3, ...), custom_call_target="tpu_custom_call" | custom-call | tf_op jit(solution)/shard_map/forward_rows/pallas_call | solution.py:168
  26.9 4.1 %collective-permute-start = (bf16[16,512]{1,0:T(8,128)(2,1)}, bf16[16,512]{1,0:T(8,128)(2,1)S(1)}, u32[]{:S(2)}, u32[]{:S(2)}) collective-permute-start(bf16[16,512]{1,0:T(8,128)(2,1)} %get-tuple-element.49), channel_id=1, source_target_pairs={{0,2},{1,3},{2,0},{3,1},{4,6},{5,7},{6,4},{7,5},{8,10},{9,11},{10,... | collective-permute-start | bytes 49160 | tf_op jit(solution)/shard_map/ppermute | solution.py:690
  35.0 3.4 %collective-permute-done.2 = bf16[16,512]{1,0:T(8,128)(2,1)S(1)} collective-permute-done((bf16[16,512]{1,0:T(8,128)(2,1)}, bf16[16,512]{1,0:T(8,128)(2,1)S(1)}, u32[]{:S(2)}, u32[]{:S(2)}) %collective-permute-start.2) | collective-permute-done | bytes 16416 | tf_op jit(solution)/shard_map/ppermute | solution.py:690
  44.2 2.4 %collective-permute-done.5 = bf16[64,512]{1,0:T(8,128)(2,1)S(1)} collective-permute-done((bf16[64,512]{1,0:T(8,128)(2,1)S(1)}, bf16[64,512]{1,0:T(8,128)(2,1)S(1)}, u32[]{:S(2)}, u32[]{:S(2)}) %collective-permute-start.5) | collective-permute-done | bytes 65568 | tf_op jit(solution)/shard_map/ppermute | solution.py:690
  47.5 3.6 %collective-permute-start.37 = (bf16[16,2048]{1,0:T(8,128)(2,1)}, bf16[16,2048]{1,0:T(8,128)(2,1)S(1)}, u32[]{:S(2)}, u32[]{:S(2)}) collective-permute-start(bf16[16,2048]{1,0:T(8,128)(2,1)} %get-tuple-element.83), channel_id=1, source_target_pairs={{0,3},{1,2},{2,1},{3,0},{4,7},{5,6},{6,5},{7,4},{8,11},{9,10},{10,... | collective-permute-start | bytes 196616 | tf_op jit(solution)/shard_map/ppermute | solution.py:690
  51.8 4.1 %contrast_all.1 = (f32[1,1]{1,0:T(1,128)}, f32[512,512]{1,0:T(8,128)}, f32[16,512]{1,0:T(8,128)}, bf16[512,512]{1,0:T(8,128)(2,1)}) custom-call(s32[1]{0:T(128)} %bitcast.where_ref.refs_0_, bf16[256,512]{1,0:T(8,128)(2,1)} %copy-done.6, bf16[256,512]{1,0:T(8,128)(2,1)} %copy-done.7, s32[256]{0:T(256)} %target_ref.1, bf16[512,512]{1,0:T(8,128)(2,1)} %wp_ref.1), custom_call_target="tpu_custom_call" | custom-call | tf_op jit(solution)/shard_map/contrast_all/pallas_call | solution.py:270
  55.9 15.7 %ffn_back.1 = (f32[2,512,512]{2,1,0:T(8,128)}, bf16[2,512,512]{2,1,0:T(8,128)(2,1)}, bf16[1280,512]{1,0:T(8,128)(2,1)}, bf16[1280,512]{1,0:T(8,128)(2,1)}, f32[1,512]{1,0:T(1,128)}) custom-call(s32[1]{0:T(128)} %bitcast.where_ref.refs_0_, s32[2,512]{1,0:T(2,128)} %seg_ref.3, f32[16,512]{1,0:T(8,128)} %get-tuple-element.51.dm_ref, ...), custom_call_target="tpu_custom_call" | custom-call | tf_op jit(solution)/shard_map/ffn_back/pallas_call | solution.py:371
  71.6 10.3 %attn_back_0.1 = (bf16[2,3,512,256]{3,2,1,0:T(8,128)(2,1)}, f32[4,768]{1,0:T(4,128)}, bf16[1536,256]{1,0:T(8,128)(2,1)}) custom-call(s32[1]{0:T(128)} %bitcast.where_ref.refs_0_, bf16[2,512,512]{2,1,0:T(8,128)(2,1)} %get-tuple-element.58.refs_1_, bf16[2,512,512]{2,1,0:T(8,128)(2,1)} %get-tuple-element.59.refs_2_, ...), custom_call_target="tpu_custom_call" | custom-call | tf_op jit(solution)/shard_map/attn_back_0/pallas_call | solution.py:513
  81.9 11.4 %attn_back_1.1 = (bf16[2,3,512,256]{3,2,1,0:T(8,128)(2,1)}, f32[4,768]{1,0:T(4,128)}, bf16[768,512]{1,0:T(8,128)(2,1)}, bf16[768,512]{1,0:T(8,128)(2,1)}) custom-call(s32[1]{0:T(128)} %bitcast.where_ref.refs_0_, bf16[2,512,512]{2,1,0:T(8,128)(2,1)} %get-tuple-element.58.refs_1_, bf16[2,512,512]{2,1,0:T(8,128)(2,1)} %get-tuple-element.59.refs_2_, ...), custom_call_target="tpu_custom_call" | custom-call | tf_op jit(solution)/shard_map/attn_back_1/pallas_call | solution.py:513
  100.8 4.2 %collective-permute-done.38 = bf16[64,2048]{1,0:T(8,128)(2,1)S(1)} collective-permute-done((bf16[64,2048]{1,0:T(8,128)(2,1)}, bf16[64,2048]{1,0:T(8,128)(2,1)S(1)}, u32[]{:S(2)}, u32[]{:S(2)}) %collective-permute-start.38) | collective-permute-done | bytes 262176 | tf_op jit(solution)/shard_map/ppermute | solution.py:690
  105.5 6.1 %collective-permute-done.24 = bf16[192,512]{1,0:T(8,128)(2,1)S(1)} collective-permute-done((bf16[192,512]{1,0:T(8,128)(2,1)S(1)}, bf16[192,512]{1,0:T(8,128)(2,1)S(1)}, u32[]{:S(2)}, u32[]{:S(2)}) %collective-permute-start.24) | collective-permute-done | bytes 196640 | tf_op jit(solution)/shard_map/ppermute | solution.py:690
  112.3 2.5 %collective-permute-done.23 = bf16[192,512]{1,0:T(8,128)(2,1)S(1)} collective-permute-done((bf16[192,512]{1,0:T(8,128)(2,1)S(1)}, bf16[192,512]{1,0:T(8,128)(2,1)S(1)}, u32[]{:S(2)}, u32[]{:S(2)}) %collective-permute-start.23) | collective-permute-done | bytes 196640 | tf_op jit(solution)/shard_map/ppermute | solution.py:690
  116.1 4.2 %collective-permute-start.25 = (bf16[48,512]{1,0:T(8,128)(2,1)}, bf16[48,512]{1,0:T(8,128)(2,1)}, u32[]{:S(2)}, u32[]{:S(2)}) collective-permute-start(bf16[48,512]{1,0:T(8,128)(2,1)} %get-tuple-element.101), channel_id=1, source_target_pairs={{0,2},{1,3},{2,0},{3,1},{4,6},{5,7},{6,4},{7,5},{8,10},{9,11},{10,... | collective-permute-start | bytes 147464 | tf_op jit(solution)/shard_map/ppermute | solution.py:690
  120.3 6.6 %finish_rows.1 = (bf16[2,512,512]{2,1,0:T(8,128)(2,1)}, bf16[8,512]{1,0:T(8,128)(2,1)}) custom-call(bf16[2,512,512]{2,1,0:T(8,128)(2,1)} %refs_0_.1, f32[2,512,512]{2,1,0:T(8,128)} %get-tuple-element.56.refs_1_, bf16[512]{0:T(512)(128)(2,1)} %refs_2_.1, f32[1,512]{1,0:T(1,128)} %get-tuple-element.57.refs_3_, bf16[768,32]{1,0:T(8,128)(2,1)} %constant.16.clone.refs_4_, ...), custom_call_target="tpu_custom_call" | custom-call | tf_op jit(solution)/shard_map/finish_rows/pallas_call | solution.py:588
  135.1 5.4 %collective-permute-done.10 = bf16[320,512]{1,0:T(8,128)(2,1)S(1)} collective-permute-done((bf16[320,512]{1,0:T(8,128)(2,1)S(1)}, bf16[320,512]{1,0:T(8,128)(2,1)S(1)}, u32[]{:S(2)}, u32[]{:S(2)}) %collective-permute-start.10) | collective-permute-done | bytes 327712 | tf_op jit(solution)/shard_map/ppermute | solution.py:690
  140.5 2.3 %collective-permute-start.30 = (bf16[56,512]{1,0:T(8,128)(2,1)S(1)}, bf16[56,512]{1,0:T(8,128)(2,1)S(1)}, u32[]{:S(2)}, u32[]{:S(2)}) collective-permute-start(bf16[56,512]{1,0:T(8,128)(2,1)S(1)} %pad_maximum_fusion.1), channel_id=1, source_target_pairs={{0,3},{1,2},{2,1},{3,0},{4,7},{5,6},{6,5},{7,4},{8,11},{9,10},{10,... | collective-permute-start | bytes 172040 | tf_op jit(solution)/shard_map/ppermute | solution.py:690
  145.1 2.4 %collective-permute-start.13 = (bf16[80,512]{1,0:T(8,128)(2,1)S(1)}, bf16[80,512]{1,0:T(8,128)(2,1)S(1)}, u32[]{:S(2)}, u32[]{:S(2)}) collective-permute-start(bf16[80,512]{1,0:T(8,128)(2,1)S(1)} %get-tuple-element.99), channel_id=1, source_target_pairs={{0,3},{1,2},{2,1},{3,0},{4,7},{5,6},{6,5},{7,4},{8,11},{9,10},{10,... | collective-permute-start | bytes 245768 | tf_op jit(solution)/shard_map/ppermute | solution.py:690
  161.0 2.4 %collective-permute-done.14 = bf16[80,512]{1,0:T(8,128)(2,1)S(1)} collective-permute-done((bf16[80,512]{1,0:T(8,128)(2,1)S(1)}, bf16[80,512]{1,0:T(8,128)(2,1)S(1)}, u32[]{:S(2)}, u32[]{:S(2)}) %collective-permute-start.14) | collective-permute-done | bytes 81952 | tf_op jit(solution)/shard_map/ppermute | solution.py:690
  166.3 2.4 %collective-permute-start.19 = (bf16[320,512]{1,0:T(8,128)(2,1)S(1)}, bf16[320,512]{1,0:T(8,128)(2,1)S(1)}, u32[]{:S(2)}, u32[]{:S(2)}) collective-permute-start(bf16[320,512]{1,0:T(8,128)(2,1)S(1)} %pad_maximum_fusion), channel_id=1, source_target_pairs={{0,24},{1,25},{2,26},{3,27},{4,28},{5,29},{6,30},{7,31},{8,16},{9,... | collective-permute-start | bytes 983048 | tf_op jit(solution)/shard_map/ppermute | solution.py:690
  168.7 8.4 %collective-permute-done.17 = bf16[320,512]{1,0:T(8,128)(2,1)S(1)} collective-permute-done((bf16[320,512]{1,0:T(8,128)(2,1)S(1)}, bf16[320,512]{1,0:T(8,128)(2,1)S(1)}, u32[]{:S(2)}, u32[]{:S(2)}) %collective-permute-start.17) | collective-permute-done | bytes 327712 | tf_op jit(solution)/shard_map/ppermute | solution.py:690
  177.6 6.0 %collective-permute-done.19 = bf16[320,512]{1,0:T(8,128)(2,1)S(1)} collective-permute-done((bf16[320,512]{1,0:T(8,128)(2,1)S(1)}, bf16[320,512]{1,0:T(8,128)(2,1)S(1)}, u32[]{:S(2)}, u32[]{:S(2)}) %collective-permute-start.19) | collective-permute-done | bytes 327712 | tf_op jit(solution)/shard_map/ppermute | solution.py:690
  186.1 6.6 %collective-permute-done.33 = bf16[224,512]{1,0:T(8,128)(2,1)S(1)} collective-permute-done((bf16[224,512]{1,0:T(8,128)(2,1)S(1)}, bf16[224,512]{1,0:T(8,128)(2,1)S(1)}, u32[]{:S(2)}, u32[]{:S(2)}) %collective-permute-start.33) | collective-permute-done | bytes 229408 | tf_op jit(solution)/shard_map/ppermute | solution.py:690
  194.5 5.2 %ffn_out_grad.1 = f32[2048,512]{1,0:T(8,128)} custom-call(s32[1]{0:T(128)} %bitcast.where_ref.refs_0_, bf16[256,2048]{1,0:T(8,128)(2,1)} %copy-done.3, bf16[256,2048]{1,0:T(8,128)(2,1)} %copy-done.4, bf16[512,512]{1,0:T(8,128)(2,1)} %get-tuple-element.84.dm_ref), custom_call_target="tpu_custom_call" | custom-call | tf_op jit(solution)/shard_map/ffn_out_grad/pallas_call | solution.py:299
  200.8 6.1 %unpack_grads.1 = (f32[512,2048]{1,0:T(8,128)}, f32[512,512]{1,0:T(8,128)}, f32[512,512]{1,0:T(8,128)}, f32[512,512]{1,0:T(8,128)}, f32[512,512]{1,0:T(8,128)}, ...) custom-call(s32[1]{0:T(128)} %bitcast.where_ref.refs_0_, bf16[1280,512]{1,0:T(8,128)(2,1)} %copy-done, ...), custom_call_target="tpu_custom_call" | custom-call | tf_op jit(solution)/shard_map/unpack_grads/pallas_call | solution.py:661
  (131 shorter events, 55.2 us)
Async XLA Ops:
  46.6 47.5 %collective-permute-start.35 = (bf16[16,2048]{1,0:T(8,128)(2,1)}, bf16[16,2048]{1,0:T(8,128)(2,1)S(1)}, u32[]{:S(2)}, u32[]{:S(2)}) collective-permute-start(bf16[16,2048]{1,0:T(8,128)(2,1)} %get-tuple-element.83), channel_id=1, source_target_pairs={{0,2},{1,3},{2,0},{3,1},{4,6},{5,7},{6,4},{7,5},{8,10},{9,11},{10,... | collective-permute-start | bytes 196616 | tf_op jit(solution)/shard_map/ppermute | solution.py:690
  46.7 48.0 %collective-permute-start.36 = (bf16[16,2048]{1,0:T(8,128)(2,1)}, bf16[16,2048]{1,0:T(8,128)(2,1)S(1)}, u32[]{:S(2)}, u32[]{:S(2)}) collective-permute-start(bf16[16,2048]{1,0:T(8,128)(2,1)} %get-tuple-element.83), channel_id=1, source_target_pairs={{0,1},{1,0},{2,3},{3,2},{4,5},{5,4},{6,7},{7,6},{8,9},{9,8},{10,11... | collective-permute-start | bytes 196616 | tf_op jit(solution)/shard_map/ppermute | solution.py:690
  47.5 48.4 %collective-permute-start.37 = (bf16[16,2048]{1,0:T(8,128)(2,1)}, bf16[16,2048]{1,0:T(8,128)(2,1)S(1)}, u32[]{:S(2)}, u32[]{:S(2)}) collective-permute-start(bf16[16,2048]{1,0:T(8,128)(2,1)} %get-tuple-element.83), channel_id=1, source_target_pairs={{0,3},{1,2},{2,1},{3,0},{4,7},{5,6},{6,5},{7,4},{8,11},{9,10},{10,... | collective-permute-start | bytes 196616 | tf_op jit(solution)/shard_map/ppermute | solution.py:690
  95.4 33.2 %collective-permute-start.7 = (bf16[1280,512]{1,0:T(8,128)(2,1)}, bf16[1280,512]{1,0:T(8,128)(2,1)S(1)}, u32[]{:S(2)}, u32[]{:S(2)}) collective-permute-start(bf16[1280,512]{1,0:T(8,128)(2,1)} %get-tuple-element.71), channel_id=1, source_target_pairs={{0,4},{1,5},{2,6},{3,7},{4,0},{5,1},{6,2},{7,3},{8,12},{9,13},{10,... | collective-permute-start | bytes 3932168 | tf_op jit(solution)/shard_map/ppermute | solution.py:690
  96.5 8.5 %collective-permute-start.38 = (bf16[64,2048]{1,0:T(8,128)(2,1)}, bf16[64,2048]{1,0:T(8,128)(2,1)S(1)}, u32[]{:S(2)}, u32[]{:S(2)}) collective-permute-start(bf16[64,2048]{1,0:T(8,128)(2,1)} %get-tuple-element.104), channel_id=1, source_target_pairs={{0,16},{1,17},{2,18},{3,19},{4,20},{5,21},{6,22},{7,23},{8,24},{9,... | collective-permute-start | bytes 786440 | tf_op jit(solution)/shard_map/ppermute | solution.py:690
  97.0 19.1 %collective-permute-start.39 = (bf16[64,2048]{1,0:T(8,128)(2,1)}, bf16[64,2048]{1,0:T(8,128)(2,1)S(1)}, u32[]{:S(2)}, u32[]{:S(2)}) collective-permute-start(bf16[64,2048]{1,0:T(8,128)(2,1)} %get-tuple-element.104), channel_id=1, source_target_pairs={{0,8},{1,9},{2,10},{3,11},{4,12},{5,13},{6,14},{7,15},{8,0},{9,1},... | collective-permute-start | bytes 786440 | tf_op jit(solution)/shard_map/ppermute | solution.py:690
  98.0 13.6 %collective-permute-start.24 = (bf16[192,512]{1,0:T(8,128)(2,1)S(1)}, bf16[192,512]{1,0:T(8,128)(2,1)S(1)}, u32[]{:S(2)}, u32[]{:S(2)}) collective-permute-start(bf16[192,512]{1,0:T(8,128)(2,1)S(1)} %get-tuple-element.95), channel_id=1, source_target_pairs={{0,24},{1,25},{2,26},{3,27},{4,28},{5,29},{6,30},{7,31},{8,16},{9,... | collective-permute-start | bytes 589832 | tf_op jit(solution)/shard_map/ppermute | solution.py:690
  100.3 14.6 %collective-permute-start.23 = (bf16[192,512]{1,0:T(8,128)(2,1)S(1)}, bf16[192,512]{1,0:T(8,128)(2,1)S(1)}, u32[]{:S(2)}, u32[]{:S(2)}) collective-permute-start(bf16[192,512]{1,0:T(8,128)(2,1)S(1)} %get-tuple-element.96), channel_id=1, source_target_pairs={{0,8},{1,9},{2,10},{3,11},{4,12},{5,13},{6,14},{7,15},{8,0},{9,1},... | collective-permute-start | bytes 589832 | tf_op jit(solution)/shard_map/ppermute | solution.py:690
  105.0 10.1 %collective-permute-start.22 = (bf16[192,512]{1,0:T(8,128)(2,1)S(1)}, bf16[192,512]{1,0:T(8,128)(2,1)S(1)}, u32[]{:S(2)}, u32[]{:S(2)}) collective-permute-start(bf16[192,512]{1,0:T(8,128)(2,1)S(1)} %get-tuple-element.97), channel_id=1, source_target_pairs={{0,16},{1,17},{2,18},{3,19},{4,20},{5,21},{6,22},{7,23},{8,24},{9,... | collective-permute-start | bytes 589832 | tf_op jit(solution)/shard_map/ppermute | solution.py:690
  111.6 72.1 %collective-permute-start.40 = (bf16[64,2048]{1,0:T(8,128)(2,1)}, bf16[64,2048]{1,0:T(8,128)(2,1)S(1)}, u32[]{:S(2)}, u32[]{:S(2)}) collective-permute-start(bf16[64,2048]{1,0:T(8,128)(2,1)} %get-tuple-element.104), channel_id=1, source_target_pairs={{0,24},{1,25},{2,26},{3,27},{4,28},{5,29},{6,30},{7,31},{8,16},{9,... | collective-permute-start | bytes 786440 | tf_op jit(solution)/shard_map/ppermute | solution.py:690
  115.8 11.0 %collective-permute-start.27 = (bf16[48,512]{1,0:T(8,128)(2,1)}, bf16[48,512]{1,0:T(8,128)(2,1)}, u32[]{:S(2)}, u32[]{:S(2)}) collective-permute-start(bf16[48,512]{1,0:T(8,128)(2,1)} %get-tuple-element.102), channel_id=1, source_target_pairs={{0,3},{1,2},{2,1},{3,0},{4,7},{5,6},{6,5},{7,4},{8,11},{9,10},{10,... | collective-permute-start | bytes 147464 | tf_op jit(solution)/shard_map/ppermute | solution.py:690
  116.1 10.8 %collective-permute-start.26 = (bf16[48,512]{1,0:T(8,128)(2,1)}, bf16[48,512]{1,0:T(8,128)(2,1)}, u32[]{:S(2)}, u32[]{:S(2)}) collective-permute-start(bf16[48,512]{1,0:T(8,128)(2,1)} %get-tuple-element.103), channel_id=1, source_target_pairs={{0,1},{1,0},{2,3},{3,2},{4,5},{5,4},{6,7},{7,6},{8,9},{9,8},{10,11... | collective-permute-start | bytes 147464 | tf_op jit(solution)/shard_map/ppermute | solution.py:690
  116.1 10.8 %collective-permute-start.25 = (bf16[48,512]{1,0:T(8,128)(2,1)}, bf16[48,512]{1,0:T(8,128)(2,1)}, u32[]{:S(2)}, u32[]{:S(2)}) collective-permute-start(bf16[48,512]{1,0:T(8,128)(2,1)} %get-tuple-element.101), channel_id=1, source_target_pairs={{0,2},{1,3},{2,0},{3,1},{4,6},{5,7},{6,4},{7,5},{8,10},{9,11},{10,... | collective-permute-start | bytes 147464 | tf_op jit(solution)/shard_map/ppermute | solution.py:690
  128.9 11.5 %collective-permute-start.10 = (bf16[320,512]{1,0:T(8,128)(2,1)S(1)}, bf16[320,512]{1,0:T(8,128)(2,1)S(1)}, u32[]{:S(2)}, u32[]{:S(2)}) collective-permute-start(bf16[320,512]{1,0:T(8,128)(2,1)S(1)} %get-tuple-element.91), channel_id=1, source_target_pairs={{0,24},{1,25},{2,26},{3,27},{4,28},{5,29},{6,30},{7,31},{8,16},{9,... | collective-permute-start | bytes 983048 | tf_op jit(solution)/shard_map/ppermute | solution.py:690
  130.3 13.7 %collective-permute-start.9 = (bf16[320,512]{1,0:T(8,128)(2,1)S(1)}, bf16[320,512]{1,0:T(8,128)(2,1)S(1)}, u32[]{:S(2)}, u32[]{:S(2)}) collective-permute-start(bf16[320,512]{1,0:T(8,128)(2,1)S(1)} %get-tuple-element.92), channel_id=1, source_target_pairs={{0,8},{1,9},{2,10},{3,11},{4,12},{5,13},{6,14},{7,15},{8,0},{9,1},... | collective-permute-start | bytes 983048 | tf_op jit(solution)/shard_map/ppermute | solution.py:690
  131.8 13.2 %collective-permute-start.8 = (bf16[320,512]{1,0:T(8,128)(2,1)S(1)}, bf16[320,512]{1,0:T(8,128)(2,1)S(1)}, u32[]{:S(2)}, u32[]{:S(2)}) collective-permute-start(bf16[320,512]{1,0:T(8,128)(2,1)S(1)} %get-tuple-element.93), channel_id=1, source_target_pairs={{0,16},{1,17},{2,18},{3,19},{4,20},{5,21},{6,22},{7,23},{8,24},{9,... | collective-permute-start | bytes 983048 | tf_op jit(solution)/shard_map/ppermute | solution.py:690
  133.7 14.6 %collective-permute-start.29 = (bf16[56,512]{1,0:T(8,128)(2,1)S(1)}, bf16[56,512]{1,0:T(8,128)(2,1)S(1)}, u32[]{:S(2)}, u32[]{:S(2)}) collective-permute-start(bf16[56,512]{1,0:T(8,128)(2,1)S(1)} %pad_maximum_fusion.1), channel_id=1, source_target_pairs={{0,1},{1,0},{2,3},{3,2},{4,5},{5,4},{6,7},{7,6},{8,9},{9,8},{10,11... | collective-permute-start | bytes 172040 | tf_op jit(solution)/shard_map/ppermute | solution.py:690
  140.5 19.6 %collective-permute-start.30 = (bf16[56,512]{1,0:T(8,128)(2,1)S(1)}, bf16[56,512]{1,0:T(8,128)(2,1)S(1)}, u32[]{:S(2)}, u32[]{:S(2)}) collective-permute-start(bf16[56,512]{1,0:T(8,128)(2,1)S(1)} %pad_maximum_fusion.1), channel_id=1, source_target_pairs={{0,3},{1,2},{2,1},{3,0},{4,7},{5,6},{6,5},{7,4},{8,11},{9,10},{10,... | collective-permute-start | bytes 172040 | tf_op jit(solution)/shard_map/ppermute | solution.py:690
  160.7 24.0 %collective-permute-start.31 = (bf16[224,512]{1,0:T(8,128)(2,1)S(1)}, bf16[224,512]{1,0:T(8,128)(2,1)S(1)}, u32[]{:S(2)}, u32[]{:S(2)}) collective-permute-start(bf16[224,512]{1,0:T(8,128)(2,1)S(1)} %get-tuple-element.112), channel_id=1, source_target_pairs={{0,16},{1,17},{2,18},{3,19},{4,20},{5,21},{6,22},{7,23},{8,24},{9,... | collective-permute-start | bytes 688136 | tf_op jit(solution)/shard_map/ppermute | solution.py:690
  165.2 12.0 %collective-permute-start.17 = (bf16[320,512]{1,0:T(8,128)(2,1)S(1)}, bf16[320,512]{1,0:T(8,128)(2,1)S(1)}, u32[]{:S(2)}, u32[]{:S(2)}) collective-permute-start(bf16[320,512]{1,0:T(8,128)(2,1)S(1)} %pad_maximum_fusion), channel_id=1, source_target_pairs={{0,16},{1,17},{2,18},{3,19},{4,20},{5,21},{6,22},{7,23},{8,24},{9,... | collective-permute-start | bytes 983048 | tf_op jit(solution)/shard_map/ppermute | solution.py:690
  165.3 12.2 %collective-permute-start.18 = (bf16[320,512]{1,0:T(8,128)(2,1)S(1)}, bf16[320,512]{1,0:T(8,128)(2,1)S(1)}, u32[]{:S(2)}, u32[]{:S(2)}) collective-permute-start(bf16[320,512]{1,0:T(8,128)(2,1)S(1)} %pad_maximum_fusion), channel_id=1, source_target_pairs={{0,8},{1,9},{2,10},{3,11},{4,12},{5,13},{6,14},{7,15},{8,0},{9,1},... | collective-permute-start | bytes 983048 | tf_op jit(solution)/shard_map/ppermute | solution.py:690
  166.3 17.3 %collective-permute-start.19 = (bf16[320,512]{1,0:T(8,128)(2,1)S(1)}, bf16[320,512]{1,0:T(8,128)(2,1)S(1)}, u32[]{:S(2)}, u32[]{:S(2)}) collective-permute-start(bf16[320,512]{1,0:T(8,128)(2,1)S(1)} %pad_maximum_fusion), channel_id=1, source_target_pairs={{0,24},{1,25},{2,26},{3,27},{4,28},{5,29},{6,30},{7,31},{8,16},{9,... | collective-permute-start | bytes 983048 | tf_op jit(solution)/shard_map/ppermute | solution.py:690
  183.6 16.1 %collective-permute-start.20 = (bf16[1280,512]{1,0:T(8,128)(2,1)S(1)}, bf16[1280,512]{1,0:T(8,128)(2,1)S(1)}, u32[]{:S(2)}, u32[]{:S(2)}) collective-permute-start(bf16[1280,512]{1,0:T(8,128)(2,1)S(1)} %constant_dynamic-update-slice_fusion.11.refs_0_), channel_id=1, source_target_pairs={{0,4},{1,5},{2,6},{3,7},{4,0},{5,1},{6,2},{7,3},{8,12},{9,13},{10,... | collective-permute-start | bytes 3932168 | tf_op jit(solution)/shard_map/ppermute | solution.py:690
  183.7 9.8 %collective-permute-start.41 = (bf16[256,2048]{1,0:T(8,128)(2,1)S(1)}, bf16[256,2048]{1,0:T(8,128)(2,1)S(1)}, u32[]{:S(2)}, u32[]{:S(2)}) collective-permute-start(bf16[256,2048]{1,0:T(8,128)(2,1)S(1)} %constant_dynamic-update-slice_fusion.35.near_ref), channel_id=1, source_target_pairs={{0,4},{1,5},{2,6},{3,7},{4,0},{5,1},{6,2},{7,3},{8,12},{9,13},{10,... | collective-permute-start | bytes 3145736 | tf_op jit(solution)/shard_map/ppermute | solution.py:690
  (31 other events, 191.9 us)

commit v3 on v2

--- a/solution.py
+++ b/solution.py
@@ -22,6 +22,8 @@
 AXES = ("wide", "narrow")
 BLK = 128
 VMEM_LIMIT = 60 * 1024 * 1024
+VMEM_SHARED = 44 * 1024 * 1024
+VMEM_SMALL = 28 * 1024 * 1024
 
 
 def bucket_offsets(length):
@@ -87,7 +89,7 @@
 
     @pl.when(step == 0)
     def _():
-        off_bias = dot(rel_ref[...], hot_ref[...], 0, 0)
+        off_bias = dot(rel_ref[...], hot_ref[...])
         for head in range(heads):
             wide = jnp.broadcast_to(off_bias[head : head + 1, :], (BLK, 2 * length))
             rolled = pltpu.roll(wide, 2 * length - BLK + 1, 1, stride=1, stride_axis=0)
@@ -161,7 +163,7 @@
 
 def forward(seg, tokens, g1, wq, wk, wv, wo, rel_bias, hot, g2, win, wout, slots):
     rows, length, width = tokens.shape
-    heads = rel_bias.shape[1]
+    heads = rel_bias.shape[0]
     inner = win.shape[1]
     low = lambda *s: jax.ShapeDtypeStruct(s, BF16)
     rlw = (rows, length, width)
@@ -278,7 +280,7 @@
             jax.ShapeDtypeStruct((count, width), BF16),
         ],
         scratch_shapes=[pltpu.VMEM((count, width), BF16), pltpu.VMEM((count, width), F32)],
-        compiler_params=pltpu.CompilerParams(vmem_limit_bytes=VMEM_LIMIT),
+        compiler_params=pltpu.CompilerParams(vmem_limit_bytes=VMEM_SHARED),
     )(where, near, far, targets, w_proj)
 
 
@@ -304,7 +306,7 @@
         out_specs=pl.BlockSpec((width, width), lambda i: (i, 0)),
         out_shape=jax.ShapeDtypeStruct((inner, width), F32),
         scratch_shapes=[pltpu.VMEM((2 * half, width), BF16)],
-        compiler_params=pltpu.CompilerParams(vmem_limit_bytes=VMEM_LIMIT),
+        compiler_params=pltpu.CompilerParams(vmem_limit_bytes=VMEM_SHARED),
     )(where, near, far, dm)
 
 
@@ -390,7 +392,7 @@
             pltpu.VMEM((lines, width), F32),
             pltpu.VMEM((1, width), F32),
         ],
-        compiler_params=pltpu.CompilerParams(vmem_limit_bytes=VMEM_LIMIT),
+        compiler_params=pltpu.CompilerParams(vmem_limit_bytes=VMEM_SHARED),
     )(where, seg, dm, act, n2, hidden, mixed, g2, win, wout, wo)
 
 
@@ -531,7 +533,7 @@
             pltpu.VMEM((heads, BLK, 5 * BLK), F32),
             pltpu.VMEM(acc, F32),
         ],
-        compiler_params=pltpu.CompilerParams(vmem_limit_bytes=VMEM_LIMIT),
+        compiler_params=pltpu.CompilerParams(vmem_limit_bytes=VMEM_SMALL),
     )(where, n1, q, k, v, probs, mixed, do, *before)
 
 
@@ -599,7 +601,7 @@
             jax.ShapeDtypeStruct((lead, width), BF16),
         ],
         scratch_shapes=[pltpu.VMEM((1, width), F32), pltpu.VMEM((lead, width), F32)],
-        compiler_params=pltpu.CompilerParams(vmem_limit_bytes=VMEM_LIMIT),
+        compiler_params=pltpu.CompilerParams(vmem_limit_bytes=VMEM_SMALL),
     )(tokens, dh, g1, g2grad, table, wq, wk, wv, *dqkvs, *bands)
 
 
@@ -618,35 +620,57 @@
     return table
 
 
-def unpack_kernel(where_ref, *refs, masks, weights):
-    big_refs, qkv_refs = refs[0:2], refs[2:4]
-    outs = refs[4:-3]
-    big_all, qkv_all, small_all = refs[-3:]
-    win_out, wo_out, wq_out, wk_out, wv_out, g1_out, g2_out, bias_out = outs
+def unpack_big_kernel(where_ref, near_ref, far_ref, win_out, wo_out, all_ref, *, masks):
     total = len(masks)
     width = wo_out.shape[1]
+    chunk = 2 * near_ref.shape[0] // total
+    for p in range(total):
+        ref, at = (near_ref, p) if p < total // 2 else (far_ref, p - total // 2)
+        first = pl.multiple_of((where_ref[0] ^ masks[p]) * chunk, chunk)
+        all_ref[pl.ds(first, chunk), :] = ref[at * chunk : (at + 1) * chunk, :].astype(F32)
+    parts = win_out.shape[1] // width
+    for part in range(parts):
+        win_out[:, part * width : (part + 1) * width] = all_ref[part * width : (part + 1) * width, :]
+    wo_out[...] = all_ref[parts * width : (parts + 1) * width, :]
+
+
+def unpack_big(where, near, far, inner, width, masks):
+    vmem = pl.BlockSpec(memory_space=pltpu.VMEM)
+    return pl.pallas_call(
+        functools.partial(unpack_big_kernel, masks=masks),
+        name="unpack_ffn",
+        in_specs=[pl.BlockSpec(memory_space=pltpu.SMEM), vmem, vmem],
+        out_shape=[
+            jax.ShapeDtypeStruct((width, inner), F32),
+            jax.ShapeDtypeStruct((width, width), F32),
+        ],
+        scratch_shapes=[pltpu.VMEM((2 * near.shape[0], width), F32)],
+        compiler_params=pltpu.CompilerParams(vmem_limit_bytes=VMEM_SMALL),
+    )(where, near, far)
+
+
+def unpack_qkv_kernel(
+    where_ref, near_ref, far_ref, wq_out, wk_out, wv_out, g1_out, g2_out, bias_out,
+    all_ref, small_all, *, masks
+):
+    total = len(masks)
+    width = wq_out.shape[1]
     lead = bias_out.shape[0]
+    rows = 2 * near_ref.shape[0] // total
+    chunk = rows - lead
     for p in range(total):
-        side, at = (0, p) if p < total // 2 else (1, p - total // 2)
-        chunk = 2 * big_refs[0].shape[0] // total
-        first = pl.multiple_of((where_ref[0] ^ masks[p]) * chunk, chunk)
-        big_all[pl.ds(first, chunk), :] = big_refs[side][at * chunk : (at + 1) * chunk, :].astype(F32)
-        rows = 2 * qkv_refs[0].shape[0] // total
-        chunk = rows - lead
-        first = pl.multiple_of((where_ref[0] ^ masks[p]) * chunk, chunk)
-        piece = qkv_refs[side][at * rows : (at + 1) * rows, :].astype(F32)
-        qkv_all[pl.ds(first, chunk), :] = piece[:chunk]
-        first = pl.multiple_of((where_ref[0] ^ masks[p]) * lead, lead)
-        small_all[pl.ds(first, lead), :] = piece[chunk:, : small_all.shape[1]]
+        ref, at = (near_ref, p) if p < total // 2 else (far_ref, p - total // 2)
+        owner = where_ref[0] ^ masks[p]
+        piece = ref[at * rows : (at + 1) * rows, :].astype(F32)
+        all_ref[pl.ds(pl.multiple_of(owner * chunk, chunk), chunk), :] = piece[:chunk]
+        small_all[pl.ds(pl.multiple_of(owner * lead, lead), lead), :] = piece[
+            chunk:, : small_all.shape[1]
+        ]
     small = small_all[:lead, :]
     for p in range(1, total):
         small = small + small_all[p * lead : (p + 1) * lead, :]
-    parts = win_out.shape[1] // width
-    for part in range(parts):
-        win_out[:, part * width : (part + 1) * width] = big_all[part * width : (part + 1) * width, :]
-    wo_out[...] = big_all[parts * width : (parts + 1) * width, :]
     for index, ref in enumerate((wq_out, wk_out, wv_out)):
-        ref[...] = qkv_all[index * width : (index + 1) * width, :]
+        ref[...] = all_ref[index * width : (index + 1) * width, :]
     for at in range(width // BLK):
         lanes = slice(at * BLK, (at + 1) * BLK)
         g1_out[:, lanes] = small[at : at + 1, BLK : 2 * BLK]
@@ -654,22 +678,21 @@
     bias_out[...] = small[:, : bias_out.shape[1]]
 
 
-def unpack(where, big, qkv, inner, width, heads, masks):
+def unpack_qkv(where, near, far, width, heads, masks):
     full = lambda *s: jax.ShapeDtypeStruct(s, F32)
     vmem = pl.BlockSpec(memory_space=pltpu.VMEM)
     total = len(masks)
     return pl.pallas_call(
-        functools.partial(unpack_kernel, masks=masks, weights=None),
-        name="unpack_grads",
-        in_specs=[pl.BlockSpec(memory_space=pltpu.SMEM)] + [vmem] * 4,
-        out_shape=[full(width, inner)] + [full(width, width)] * 4 + [full(1, width)] * 2 + [full(heads, NB)],
+        functools.partial(unpack_qkv_kernel, masks=masks),
+        name="unpack_attn",
+        in_specs=[pl.BlockSpec(memory_space=pltpu.SMEM), vmem, vmem],
+        out_shape=[full(width, width)] * 3 + [full(1, width)] * 2 + [full(heads, NB)],
         scratch_shapes=[
-            pltpu.VMEM((2 * big[0].shape[0], width), F32),
-            pltpu.VMEM((2 * qkv[0].shape[0] - total * heads, width), F32),
+            pltpu.VMEM((2 * near.shape[0] - total * heads, width), F32),
             pltpu.VMEM((total * heads, 3 * BLK), F32),
         ],
-        compiler_params=pltpu.CompilerParams(vmem_limit_bytes=VMEM_LIMIT),
-    )(where, *big, *qkv)
+        compiler_params=pltpu.CompilerParams(vmem_limit_bytes=VMEM_SMALL),
+    )(where, near, far)
 
 
 def bit_groups(wide, narrow):
@@ -690,12 +713,8 @@
     return lax.ppermute(values, AXES, [(i, i ^ mask) for i in range(total)])
 
 
-def gather_stages(values, groups, total):
-    pieces = [values]
-    for group in reversed(groups):
-        values = pieces[0] if len(pieces) == 1 else jnp.concatenate(pieces, axis=0)
-        pieces = [values] + [swap(values, mask, total) for mask in group_masks(group)]
-    return pieces
+def after(values, *others):
+    return lax.optimization_barrier((values,) + others)[0]
 
 
 def split_rows(values, count):
@@ -703,19 +722,48 @@
     return [values[i * rows : (i + 1) * rows] for i in range(count)]
 
 
-def scatter_stages(keep, send, groups, total):
-    blocks = [keep, send]
-    for index, group in enumerate(groups):
-        got = [swap(b, mask, total) for b, mask in zip(blocks[1:], group_masks(group))]
-        count = 1 << len(groups[index + 1]) if index + 1 < len(groups) else 1
-        parts = [split_rows(b, count) for b in [blocks[0]] + got]
-        blocks = []
-        for column in zip(*parts):
-            total_part = column[0].astype(F32)
-            for other in column[1:]:
-                total_part = total_part + other.astype(F32)
-            blocks.append(total_part.astype(BF16))
-    return blocks[0]
+class Gather:
+    def __init__(self, values, groups, total):
+        self.pieces, self.left, self.total = [values], list(reversed(groups)), total
+
+    def step(self, *hold):
+        if self.left:
+            values = self.pieces[0]
+            if len(self.pieces) > 1:
+                pieces = lax.optimization_barrier(tuple(self.pieces) + hold)[: len(self.pieces)]
+                values = jnp.concatenate(pieces, axis=0)
+            masks = group_masks(self.left.pop(0))
+            self.pieces = [values] + [swap(values, mask, self.total) for mask in masks]
+
+    def rest(self):
+        while self.left:
+            self.step()
+        return self.pieces
+
+
+class Scatter:
+    def __init__(self, blocks, groups, total):
+        self.blocks, self.left, self.total = list(blocks), list(groups), total
+
+    def step(self, *hold):
+        if self.left:
+            masks = group_masks(self.left.pop(0))
+            got = [swap(b, mask, self.total) for b, mask in zip(self.blocks[1:], masks)]
+            if hold:
+                got = list(lax.optimization_barrier(tuple(got) + hold)[: len(got)])
+            count = 1 << len(self.left[0]) if self.left else 1
+            parts = [split_rows(b, count) for b in [self.blocks[0]] + got]
+            self.blocks = []
+            for column in zip(*parts):
+                value = column[0].astype(F32)
+                for other in column[1:]:
+                    value = value + other.astype(F32)
+                self.blocks.append(value.astype(BF16))
+
+    def rest(self):
+        while self.left:
+            self.step()
+        return self.blocks[0]
 
 
 GROUPS = 2
@@ -740,10 +788,15 @@
     hot[buckets, np.arange(2 * length - 1)] = 1.0
 
     n1, q, k, v, probs, mixed, hidden, n2, act, abar, pooled = forward(
-        seg_ids, tokens, norm1_gain, w_query, w_key, w_value, w_attn_out, rel_bias,
+        seg_ids, tokens, norm1_gain, w_query, w_key, w_value, w_attn_out, rel_bias.T,
         jnp.asarray(hot, BF16), norm2_gain, w_in, w_ffn_out, slots,
     )
-    near, far = gather_stages(pooled, groups, total)
+    slot = Gather(pooled, groups, total)
+    slot.step()
+    slot.step()
+    acts = Gather(after(abar, slot.pieces[0]), groups, total)
+    acts.step()
+    near, far = slot.rest()
     loss, grad_proj, dm_own, dm_low = contrast_call(
         where, near, far, positives, w_proj, slots, masks
     )
@@ -751,27 +804,42 @@
         where, seg_ids, dm_own, act, n2, hidden, mixed, norm2_gain, w_in, w_ffn_out, w_attn_out,
         masks,
     )
-    big = scatter_stages(big_keep, big_send, groups, total)
-    big = gather_stages(big, groups, total)
-    dqkvs, bands, before = [], [], []
+    acts.step(do)
+    big = Scatter([big_keep, big_send], groups, total)
+    dqkvs, bands, before, tie = [], [], [], acts.pieces[:1]
     for _ in range(GROUPS):
         dqkv, band, *grads = attn_back(
-            where, n1, q, k, v, probs, mixed, do, before, GROUPS, masks
+            where, n1, q, k, v, probs, mixed, after(do, *tie), before, GROUPS, masks
         )
         dqkvs.append(dqkv)
         bands.append(band)
         before = before + grads[:1]
+        if len(before) == 1:
+            big.step(band)
+            acts.step(band)
+            tie = big.blocks + acts.pieces[:1]
+    qkv = Scatter(grads, groups, total)
     tokens_grad, small = finish(
         tokens, dh, norm1_gain, grad_g2, jnp.asarray(band_table(length), BF16),
         w_query, w_key, w_value, dqkvs, bands,
     )
-    qkv = scatter_stages(grads[0], grads[1], groups, total)
-    qkv = gather_stages(jnp.concatenate([qkv, small], axis=0), groups, total)
-
-    grad_ffn_out = ffn_out_grad(where, *gather_stages(abar, groups, total), dm_low, masks)
-
-    win, wo, wq, wk, wv, grad_g1, grad_g2, grad_bias = unpack(
-        where, big, qkv, inner, width, heads, masks
+    qkv.step(small)
+    big.step(*qkv.blocks)
+    grad_ffn_out = ffn_out_grad(where, *acts.rest(), after(dm_low, *big.blocks), masks)
+    qkv.step(grad_ffn_out)
+    big.step(*qkv.blocks)
+    big_all = Gather(big.rest(), groups, total)
+    big_all.step()
+    qkv.step(big_all.pieces[0])
+    qkv_all = Gather(jnp.concatenate([qkv.rest(), small], axis=0), groups, total)
+    qkv_all.step()
+    big_all.step(qkv_all.pieces[0])
+    qkv_all.step(big_all.pieces[0])
+    big_all.step(qkv_all.pieces[0])
+    win, wo = unpack_big(where, *big_all.rest(), inner, width, masks)
+    qkv_all.step(wo)
+    wq, wk, wv, grad_g1, grad_g2, grad_bias = unpack_qkv(
+        where, *qkv_all.rest(), width, heads, masks
     )
     return (
         loss[0, 0],

time: 207 us -> 171 us (0.83)
  waiting for transfers between devices: 60.7 us -> 42 us
  Pallas kernels: 84.4 us -> 69.1 us
  local copies, waits for them, and re-layouts: 12.9 us -> 5.74 us
  starting transfers between devices: 44.9 us -> 51.8 us
  other arithmetic: 3.22 us -> 0.99 us
    ppermute x42, waiting for transfers between devices: 60.7 us -> 42 us  [swap(): return lax.ppermute(values, AXES, [(i, i ^ mask) for i in range(total)])]
    pallas_call x2, Pallas kernels: 21.7 us -> 14.7 us  [attn_back(): pl.pallas_call(functools.partial(attn_back_kernel, group=group, masks=mas...]
    ppermute x42, starting transfers between devices: 44.9 us -> 51.8 us  [swap(): return lax.ppermute(values, AXES, [(i, i ^ mask) for i in range(total)])]
    unnamed x48 -> x70, local copies, waits for them, and re-layouts: 10.8 us -> 5.65 us
    pallas_call x1, Pallas kernels: 6.56 us -> 3.84 us  [finish(): pl.pallas_call(functools.partial(finish_kernel, groups=groups), name='fin...]
    pallas_call x1 -> x2, Pallas kernels: 6.12 us -> 4.94 us  [the longest x1 2.96 us: unpack_big(): pl.pallas_call(functools.partial(unpack_big_kernel, masks=masks), name='u...]
  transfers between devices with their start and end apart: 42 -> 42, of which waited for: 20 -> 17; matrix products, arithmetic and copies ran while one was open for 6% -> 0% of each run, Pallas kernels for 26% -> 20%
where the time goes in v3:
time: 171 us
  Pallas kernels  69.1 us (40%)
  starting transfers between devices  51.8 us (30%)
  waiting for transfers between devices  42 us (25%)
  local copies, waits for them, and re-layouts  5.74 us (3%)
    ppermute x42, starting transfers between devices, swap(): return lax.ppermute(values, AXES, [(i, i ^ mask) for i in range(total)])  51.8 us
    ppermute x42, waiting for transfers between devices, swap(): return lax.ppermute(values, AXES, [(i, i ^ mask) for i in range(total)])  42 us
    pallas_call x1, Pallas kernels, forward(): pl.pallas_call(forward_kernel, name='forward_rows', grid=(rows,), in_spec...  24.8 us
    pallas_call x2, Pallas kernels, attn_back(): pl.pallas_call(functools.partial(attn_back_kernel, group=group, masks=mas...  14.7 us
    pallas_call x1, Pallas kernels, ffn_back(): pl.pallas_call(functools.partial(ffn_back_kernel, masks=masks), name='ffn...  14.5 us
    unnamed x70, local copies, waits for them, and re-layouts  5.65 us
    pallas_call x1, Pallas kernels, finish(): pl.pallas_call(functools.partial(finish_kernel, groups=groups), name='fin...  3.84 us
    pallas_call x1, Pallas kernels, ffn_out_grad(): pl.pallas_call(functools.partial(ffn_out_kernel, masks=masks), name='ffn_...  3.64 us
  transfers between devices with their start and end apart: 42, of which 17 were waited for; matrix products, arithmetic and copies ran while one was open for 0% of the time, Pallas kernels for 20%

profile of v3, /device:TPU:0, one launch (start us, length us, event | category | flops | bytes accessed | tf_op | source)
XLA Modules:
  0.0 170.8 jit_solution(4115599034183283754)
XLA Ops:
  0.7 24.8 %forward_rows.1 = (bf16[2,512,512]{2,1,0:T(8,128)(2,1)}, bf16[2,512,512]{2,1,0:T(8,128)(2,1)}, bf16[2,512,512]{2,1,0:T(8,128)(2,1)}, bf16[2,512,512]{2,1,0:T(8,1...) custom-call(s32[2,512]{1,0:T(2,128)} %seg_ref.3, ...), custom_call_target="tpu_custom_call" | custom-call | tf_op jit(solution)/shard_map/forward_rows/pallas_call | solution.py:170
  25.5 4.1 %collective-permute-start = (bf16[16,512]{1,0:T(8,128)(2,1)}, bf16[16,512]{1,0:T(8,128)(2,1)S(1)}, u32[]{:S(2)}, u32[]{:S(2)}) collective-permute-start(bf16[16,512]{1,0:T(8,128)(2,1)} %get-tuple-element.100), channel_id=1, source_target_pairs={{0,2},{1,3},{2,0},{3,1},{4,6},{5,7},{6,4},{7,5},{8,10},{9,11},{10,... | collective-permute-start | bytes 49160 | tf_op jit(solution)/shard_map/ppermute | solution.py:713
  33.6 3.4 %collective-permute-done.2 = bf16[16,512]{1,0:T(8,128)(2,1)S(1)} collective-permute-done((bf16[16,512]{1,0:T(8,128)(2,1)}, bf16[16,512]{1,0:T(8,128)(2,1)S(1)}, u32[]{:S(2)}, u32[]{:S(2)}) %collective-permute-start.2) | collective-permute-done | bytes 16416 | tf_op jit(solution)/shard_map/ppermute | solution.py:713
  43.5 2.4 %collective-permute-done.5 = bf16[64,512]{1,0:T(8,128)(2,1)S(1)} collective-permute-done((bf16[64,512]{1,0:T(8,128)(2,1)S(1)}, bf16[64,512]{1,0:T(8,128)(2,1)S(1)}, u32[]{:S(2)}, u32[]{:S(2)}) %collective-permute-start.5) | collective-permute-done | bytes 65568 | tf_op jit(solution)/shard_map/ppermute | solution.py:713
  46.9 3.6 %collective-permute-start.9 = (bf16[16,2048]{1,0:T(8,128)(2,1)}, bf16[16,2048]{1,0:T(8,128)(2,1)S(1)}, u32[]{:S(2)}, u32[]{:S(2)}) collective-permute-start(bf16[16,2048]{1,0:T(8,128)(2,1)} %get-tuple-element.124), channel_id=1, source_target_pairs={{0,3},{1,2},{2,1},{3,0},{4,7},{5,6},{6,5},{7,4},{8,11},{9,10},{10,... | collective-permute-start | bytes 196616 | tf_op jit(solution)/shard_map/ppermute | solution.py:713
  50.5 2.7 %contrast_all.1 = (f32[1,1]{1,0:T(1,128)}, f32[512,512]{1,0:T(8,128)}, f32[16,512]{1,0:T(8,128)S(1)}, bf16[512,512]{1,0:T(8,128)(2,1)S(1)}) custom-call(s32[1]{0:T(128)} %bitcast.where_ref.refs_0_, bf16[256,512]{1,0:T(8,128)(2,1)S(1)} %constant_dynamic-update-slice_fusion.4.near_ref, bf16[256,512]{1,0:T(8,128)(2,1)S(1)} %collective-permute-done.6.far_ref, ...), custom_call_target="tpu_custom_call" | custom-call | tf_op jit(solution)/shard_map/contrast_all/pallas_call | solution.py:272
  55.5 14.5 %ffn_back.1 = (f32[2,512,512]{2,1,0:T(8,128)S(1)}, bf16[2,512,512]{2,1,0:T(8,128)(2,1)S(1)}, bf16[1280,512]{1,0:T(8,128)(2,1)S(1)}, bf16[1280,512]{1,0:T(8,128)(2,1)}, f32[1,512]{1,0:T(1,128)S(1)}) custom-call(s32[1]{0:T(128)} %bitcast.where_ref.refs_0_, s32[2,512]{1,0:T(2,128)S(1)} %copy-done.18, f32[16,512]{1,0:T(8,128)S(1)} %get-tuple-element.109.dm_ref, ...), custom_call_target="tpu_custom_call" | custom-call | tf_op jit(solution)/shard_map/ffn_back/pallas_call | solution.py:373
  75.0 7.2 %attn_back_0.1 = (bf16[2,3,512,256]{3,2,1,0:T(8,128)(2,1)S(1)}, f32[4,768]{1,0:T(4,128)S(1)}, bf16[1536,256]{1,0:T(8,128)(2,1)S(1)}) custom-call(s32[1]{0:T(128)} %bitcast.where_ref.refs_0_, bf16[2,512,512]{2,1,0:T(8,128)(2,1)S(1)} %copy-done.2, bf16[2,512,512]{2,1,0:T(8,128)(2,1)S(1)} %copy-done.3, bf16[2,512,512]{2,1,0:T(8,128)(2,1)S(1)} %copy-done.4, ...), custom_call_target="tpu_custom_call" | custom-call | tf_op jit(solution)/shard_map/attn_back_0/pallas_call | solution.py:515
  82.2 3.5 %collective-permute-done.13 = bf16[64,2048]{1,0:T(8,128)(2,1)S(1)} collective-permute-done((bf16[64,2048]{1,0:T(8,128)(2,1)S(1)}, bf16[64,2048]{1,0:T(8,128)(2,1)S(1)}, u32[]{:S(2)}, u32[]{:S(2)}) %collective-permute-start.13) | collective-permute-done | bytes 262176 | tf_op jit(solution)/shard_map/ppermute | solution.py:713
  87.5 7.5 %attn_back_1.1 = (bf16[2,3,512,256]{3,2,1,0:T(8,128)(2,1)S(1)}, f32[4,768]{1,0:T(4,128)S(1)}, bf16[768,512]{1,0:T(8,128)(2,1)S(1)}, bf16[768,512]{1,0:T(8,128)(2,1)S(1)}) custom-call(s32[1]{0:T(128)} %bitcast.where_ref.refs_0_, bf16[2,512,512]{2,1,0:T(8,128)(2,1)S(1)} %copy-done.2, bf16[2,512,512]{2,1,0:T(8,128)(2,1)S(1)} %copy-done.3, ...), custom_call_target="tpu_custom_call" | custom-call | tf_op jit(solution)/shard_map/attn_back_1/pallas_call | solution.py:515
  99.0 3.8 %finish_rows.1 = (bf16[2,512,512]{2,1,0:T(8,128)(2,1)}, bf16[8,512]{1,0:T(8,128)(2,1)S(1)}) custom-call(bf16[2,512,512]{2,1,0:T(8,128)(2,1)S(1)} %copy-done.8, f32[2,512,512]{2,1,0:T(8,128)S(1)} %copy-done.14, bf16[512]{0:T(512)(128)(2,1)S(1)} %copy-done.20, f32[1,512]{1,0:T(1,128)S(1)} %get-tuple-element.115.refs_3_, bf16[768,32]{1,0:T(8,128)(2,1)S(1)} %copy-done.17, ...), custom_call_target="tpu_custom_call" | custom-call | tf_op jit(solution)/shard_map/finish_rows/pallas_call | solution.py:590
  108.1 6.5 %collective-permute-done.21 = bf16[320,512]{1,0:T(8,128)(2,1)S(1)} collective-permute-done((bf16[320,512]{1,0:T(8,128)(2,1)S(1)}, bf16[320,512]{1,0:T(8,128)(2,1)S(1)}, u32[]{:S(2)}, u32[]{:S(2)}) %collective-permute-start.21) | collective-permute-done | bytes 327712 | tf_op jit(solution)/shard_map/ppermute | solution.py:713
  115.7 3.6 %ffn_out_grad.1 = f32[2048,512]{1,0:T(8,128)} custom-call(s32[1]{0:T(128)} %bitcast.where_ref.refs_0_, bf16[256,2048]{1,0:T(8,128)(2,1)S(1)} %constant_dynamic-update-slice_fusion.12.near_ref, bf16[256,2048]{1,0:T(8,128)(2,1)S(1)} %collective-permute-done.18.far_ref, bf16[512,512]{1,0:T(8,128)(2,1)S(1)} %get-tuple-element.151.dm_ref), custom_call_target="tpu_custom_call" | custom-call | tf_op jit(solution)/shard_map/ffn_out_grad/pallas_call | solution.py:301
  119.3 3.6 %collective-permute-start.27 = (bf16[80,512]{1,0:T(8,128)(2,1)S(1)}, bf16[80,512]{1,0:T(8,128)(2,1)S(1)}, u32[]{:S(2)}, u32[]{:S(2)}) collective-permute-start(bf16[80,512]{1,0:T(8,128)(2,1)S(1)} %get-tuple-element.194), channel_id=1, source_target_pairs={{0,3},{1,2},{2,1},{3,0},{4,7},{5,6},{6,5},{7,4},{8,11},{9,10},{10,... | collective-permute-start | bytes 245768 | tf_op jit(solution)/shard_map/ppermute | solution.py:713
  123.9 3.6 %collective-permute-start.24 = (bf16[48,512]{1,0:T(8,128)(2,1)S(1)}, bf16[48,512]{1,0:T(8,128)(2,1)S(1)}, u32[]{:S(2)}, u32[]{:S(2)}) collective-permute-start(bf16[48,512]{1,0:T(8,128)(2,1)S(1)} %get-tuple-element.199), channel_id=1, source_target_pairs={{0,3},{1,2},{2,1},{3,0},{4,7},{5,6},{6,5},{7,4},{8,11},{9,10},{10,... | collective-permute-start | bytes 147464 | tf_op jit(solution)/shard_map/ppermute | solution.py:713
  127.6 2.3 %collective-permute-start.32 = (bf16[80,512]{1,0:T(8,128)(2,1)S(1)}, bf16[80,512]{1,0:T(8,128)(2,1)S(1)}, u32[]{:S(2)}, u32[]{:S(2)}) collective-permute-start(bf16[80,512]{1,0:T(8,128)(2,1)S(1)} %add_convert_fusion.8), channel_id=1, source_target_pairs={{0,1},{1,0},{2,3},{3,2},{4,5},{5,4},{6,7},{7,6},{8,9},{9,8},{10,11... | collective-permute-start | bytes 245768 | tf_op jit(solution)/shard_map/ppermute | solution.py:713
  132.1 2.5 %collective-permute-start.29 = (bf16[56,512]{1,0:T(8,128)(2,1)S(1)}, bf16[56,512]{1,0:T(8,128)(2,1)S(1)}, u32[]{:S(2)}, u32[]{:S(2)}) collective-permute-start(bf16[56,512]{1,0:T(8,128)(2,1)S(1)} %pad_maximum_fusion), channel_id=1, source_target_pairs={{0,1},{1,0},{2,3},{3,2},{4,5},{5,4},{6,7},{7,6},{8,9},{9,8},{10,11... | collective-permute-start | bytes 172040 | tf_op jit(solution)/shard_map/ppermute | solution.py:713
  135.2 4.5 %collective-permute-start.30 = (bf16[56,512]{1,0:T(8,128)(2,1)S(1)}, bf16[56,512]{1,0:T(8,128)(2,1)S(1)}, u32[]{:S(2)}, u32[]{:S(2)}) collective-permute-start(bf16[56,512]{1,0:T(8,128)(2,1)S(1)} %pad_maximum_fusion), channel_id=1, source_target_pairs={{0,3},{1,2},{2,1},{3,0},{4,7},{5,6},{6,5},{7,4},{8,11},{9,10},{10,... | collective-permute-start | bytes 172040 | tf_op jit(solution)/shard_map/ppermute | solution.py:713
  141.1 2.2 %collective-permute-start.39 = (bf16[320,512]{1,0:T(8,128)(2,1)S(1)}, bf16[320,512]{1,0:T(8,128)(2,1)S(1)}, u32[]{:S(2)}, u32[]{:S(2)}) collective-permute-start(bf16[320,512]{1,0:T(8,128)(2,1)S(1)} %constant_dynamic-update-slice_fusion.16), channel_id=1, source_target_pairs={{0,24},{1,25},{2,26},{3,27},{4,28},{5,29},{6,30},{7,31},{8,16},{9,... | collective-permute-start | bytes 983048 | tf_op jit(solution)/shard_map/ppermute | solution.py:713
  143.4 5.0 %collective-permute-done.37 = bf16[320,512]{1,0:T(8,128)(2,1)S(1)} collective-permute-done((bf16[320,512]{1,0:T(8,128)(2,1)S(1)}, bf16[320,512]{1,0:T(8,128)(2,1)S(1)}, u32[]{:S(2)}, u32[]{:S(2)}) %collective-permute-start.37) | collective-permute-done | bytes 327712 | tf_op jit(solution)/shard_map/ppermute | solution.py:713
  148.4 3.5 %collective-permute-done.39 = bf16[320,512]{1,0:T(8,128)(2,1)S(1)} collective-permute-done((bf16[320,512]{1,0:T(8,128)(2,1)S(1)}, bf16[320,512]{1,0:T(8,128)(2,1)S(1)}, u32[]{:S(2)}, u32[]{:S(2)}) %collective-permute-start.39) | collective-permute-done | bytes 327712 | tf_op jit(solution)/shard_map/ppermute | solution.py:713
  155.7 3.0 %unpack_ffn.1 = (f32[512,2048]{1,0:T(8,128)}, f32[512,512]{1,0:T(8,128)}) custom-call(s32[1]{0:T(128)} %bitcast.where_ref.refs_0_, bf16[1280,512]{1,0:T(8,128)(2,1)S(1)} %constant_dynamic-update-slice_fusion.24.near_ref, bf16[1280,512]{1,0:T(8,128)(2,1)S(1)} %collective-permute-done.40.far_ref), custom_call_target="tpu_custom_call" | custom-call | tf_op jit(solution)/shard_map/unpack_ffn/pallas_call | solution.py:639
  161.2 5.0 %collective-permute-done.36 = bf16[224,512]{1,0:T(8,128)(2,1)S(1)} collective-permute-done((bf16[224,512]{1,0:T(8,128)(2,1)S(1)}, bf16[224,512]{1,0:T(8,128)(2,1)S(1)}, u32[]{:S(2)}, u32[]{:S(2)}) %collective-permute-start.36) | collective-permute-done | bytes 229408 | tf_op jit(solution)/shard_map/ppermute | solution.py:713
  166.4 2.5 %collective-permute-done.41.far_ref = bf16[896,512]{1,0:T(8,128)(2,1)S(1)} collective-permute-done((bf16[896,512]{1,0:T(8,128)(2,1)S(1)}, bf16[896,512]{1,0:T(8,128)(2,1)S(1)}, u32[]{:S(2)}, u32[]{:S(2)}) %collective-permute-start.41) | collective-permute-done | bytes 917536 | tf_op jit(solution)/shard_map/ppermute | solution.py:713
  (154 shorter events, 44.2 us)
Async XLA Ops:
  46.0 24.0 %collective-permute-start.7 = (bf16[16,2048]{1,0:T(8,128)(2,1)}, bf16[16,2048]{1,0:T(8,128)(2,1)S(1)}, u32[]{:S(2)}, u32[]{:S(2)}) collective-permute-start(bf16[16,2048]{1,0:T(8,128)(2,1)} %get-tuple-element.124), channel_id=1, source_target_pairs={{0,2},{1,3},{2,0},{3,1},{4,6},{5,7},{6,4},{7,5},{8,10},{9,11},{10,... | collective-permute-start | bytes 196616 | tf_op jit(solution)/shard_map/ppermute | solution.py:713
  46.1 23.9 %collective-permute-start.8 = (bf16[16,2048]{1,0:T(8,128)(2,1)}, bf16[16,2048]{1,0:T(8,128)(2,1)S(1)}, u32[]{:S(2)}, u32[]{:S(2)}) collective-permute-start(bf16[16,2048]{1,0:T(8,128)(2,1)} %get-tuple-element.124), channel_id=1, source_target_pairs={{0,1},{1,0},{2,3},{3,2},{4,5},{5,4},{6,7},{7,6},{8,9},{9,8},{10,11... | collective-permute-start | bytes 196616 | tf_op jit(solution)/shard_map/ppermute | solution.py:713
  46.9 23.1 %collective-permute-start.9 = (bf16[16,2048]{1,0:T(8,128)(2,1)}, bf16[16,2048]{1,0:T(8,128)(2,1)S(1)}, u32[]{:S(2)}, u32[]{:S(2)}) collective-permute-start(bf16[16,2048]{1,0:T(8,128)(2,1)} %get-tuple-element.124), channel_id=1, source_target_pairs={{0,3},{1,2},{2,1},{3,0},{4,7},{5,6},{6,5},{7,4},{8,11},{9,10},{10,... | collective-permute-start | bytes 196616 | tf_op jit(solution)/shard_map/ppermute | solution.py:713
  70.1 15.8 %collective-permute-start.10 = (bf16[1280,512]{1,0:T(8,128)(2,1)}, bf16[1280,512]{1,0:T(8,128)(2,1)S(1)}, u32[]{:S(2)}, u32[]{:S(2)}) collective-permute-start(bf16[1280,512]{1,0:T(8,128)(2,1)} %get-tuple-element.131), channel_id=1, source_target_pairs={{0,4},{1,5},{2,6},{3,7},{4,0},{5,1},{6,2},{7,3},{8,12},{9,13},{10,... | collective-permute-start | bytes 3932168 | tf_op jit(solution)/shard_map/ppermute | solution.py:713
  70.2 12.0 %collective-permute-start.11 = (bf16[64,2048]{1,0:T(8,128)(2,1)S(1)}, bf16[64,2048]{1,0:T(8,128)(2,1)S(1)}, u32[]{:S(2)}, u32[]{:S(2)}) collective-permute-start(bf16[64,2048]{1,0:T(8,128)(2,1)S(1)} %constant_dynamic-update-slice_fusion.8), channel_id=1, source_target_pairs={{0,16},{1,17},{2,18},{3,19},{4,20},{5,21},{6,22},{7,23},{8,24},{9,... | collective-permute-start | bytes 786440 | tf_op jit(solution)/shard_map/ppermute | solution.py:713
  70.8 11.5 %collective-permute-start.12 = (bf16[64,2048]{1,0:T(8,128)(2,1)S(1)}, bf16[64,2048]{1,0:T(8,128)(2,1)S(1)}, u32[]{:S(2)}, u32[]{:S(2)}) collective-permute-start(bf16[64,2048]{1,0:T(8,128)(2,1)S(1)} %constant_dynamic-update-slice_fusion.8), channel_id=1, source_target_pairs={{0,8},{1,9},{2,10},{3,11},{4,12},{5,13},{6,14},{7,15},{8,0},{9,1},... | collective-permute-start | bytes 786440 | tf_op jit(solution)/shard_map/ppermute | solution.py:713
  71.5 14.2 %collective-permute-start.13 = (bf16[64,2048]{1,0:T(8,128)(2,1)S(1)}, bf16[64,2048]{1,0:T(8,128)(2,1)S(1)}, u32[]{:S(2)}, u32[]{:S(2)}) collective-permute-start(bf16[64,2048]{1,0:T(8,128)(2,1)S(1)} %constant_dynamic-update-slice_fusion.8), channel_id=1, source_target_pairs={{0,24},{1,25},{2,26},{3,27},{4,28},{5,29},{6,30},{7,31},{8,16},{9,... | collective-permute-start | bytes 786440 | tf_op jit(solution)/shard_map/ppermute | solution.py:713
  95.0 19.9 %collective-permute-start.18 = (bf16[256,2048]{1,0:T(8,128)(2,1)S(1)}, bf16[256,2048]{1,0:T(8,128)(2,1)S(1)}, u32[]{:S(2)}, u32[]{:S(2)}) collective-permute-start(bf16[256,2048]{1,0:T(8,128)(2,1)S(1)} %constant_dynamic-update-slice_fusion.12.near_ref), channel_id=1, source_target_pairs={{0,4},{1,5},{2,6},{3,7},{4,0},{5,1},{6,2},{7,3},{8,12},{9,13},{10,... | collective-permute-start | bytes 3145736 | tf_op jit(solution)/shard_map/ppermute | solution.py:713
  95.5 10.1 %collective-permute-start.19 = (bf16[320,512]{1,0:T(8,128)(2,1)S(1)}, bf16[320,512]{1,0:T(8,128)(2,1)S(1)}, u32[]{:S(2)}, u32[]{:S(2)}) collective-permute-start(bf16[320,512]{1,0:T(8,128)(2,1)S(1)} %get-tuple-element.188), channel_id=1, source_target_pairs={{0,16},{1,17},{2,18},{3,19},{4,20},{5,21},{6,22},{7,23},{8,24},{9,... | collective-permute-start | bytes 983048 | tf_op jit(solution)/shard_map/ppermute | solution.py:713
  96.0 10.6 %collective-permute-start.20 = (bf16[320,512]{1,0:T(8,128)(2,1)S(1)}, bf16[320,512]{1,0:T(8,128)(2,1)S(1)}, u32[]{:S(2)}, u32[]{:S(2)}) collective-permute-start(bf16[320,512]{1,0:T(8,128)(2,1)S(1)} %get-tuple-element.187), channel_id=1, source_target_pairs={{0,8},{1,9},{2,10},{3,11},{4,12},{5,13},{6,14},{7,15},{8,0},{9,1},... | collective-permute-start | bytes 983048 | tf_op jit(solution)/shard_map/ppermute | solution.py:713
  96.8 17.8 %collective-permute-start.21 = (bf16[320,512]{1,0:T(8,128)(2,1)S(1)}, bf16[320,512]{1,0:T(8,128)(2,1)S(1)}, u32[]{:S(2)}, u32[]{:S(2)}) collective-permute-start(bf16[320,512]{1,0:T(8,128)(2,1)S(1)} %get-tuple-element.186), channel_id=1, source_target_pairs={{0,24},{1,25},{2,26},{3,27},{4,28},{5,29},{6,30},{7,31},{8,16},{9,... | collective-permute-start | bytes 983048 | tf_op jit(solution)/shard_map/ppermute | solution.py:713
  103.1 16.2 %collective-permute-start.15 = (bf16[192,512]{1,0:T(8,128)(2,1)S(1)}, bf16[192,512]{1,0:T(8,128)(2,1)S(1)}, u32[]{:S(2)}, u32[]{:S(2)}) collective-permute-start(bf16[192,512]{1,0:T(8,128)(2,1)S(1)} %get-tuple-element.192), channel_id=1, source_target_pairs={{0,16},{1,17},{2,18},{3,19},{4,20},{5,21},{6,22},{7,23},{8,24},{9,... | collective-permute-start | bytes 589832 | tf_op jit(solution)/shard_map/ppermute | solution.py:713
  105.6 17.3 %collective-permute-start.16 = (bf16[192,512]{1,0:T(8,128)(2,1)S(1)}, bf16[192,512]{1,0:T(8,128)(2,1)S(1)}, u32[]{:S(2)}, u32[]{:S(2)}) collective-permute-start(bf16[192,512]{1,0:T(8,128)(2,1)S(1)} %get-tuple-element.191), channel_id=1, source_target_pairs={{0,8},{1,9},{2,10},{3,11},{4,12},{5,13},{6,14},{7,15},{8,0},{9,1},... | collective-permute-start | bytes 589832 | tf_op jit(solution)/shard_map/ppermute | solution.py:713
  106.6 16.3 %collective-permute-start.17 = (bf16[192,512]{1,0:T(8,128)(2,1)S(1)}, bf16[192,512]{1,0:T(8,128)(2,1)S(1)}, u32[]{:S(2)}, u32[]{:S(2)}) collective-permute-start(bf16[192,512]{1,0:T(8,128)(2,1)S(1)} %get-tuple-element.190), channel_id=1, source_target_pairs={{0,24},{1,25},{2,26},{3,27},{4,28},{5,29},{6,30},{7,31},{8,16},{9,... | collective-permute-start | bytes 589832 | tf_op jit(solution)/shard_map/ppermute | solution.py:713
  114.8 9.1 %collective-permute-start.25 = (bf16[80,512]{1,0:T(8,128)(2,1)S(1)}, bf16[80,512]{1,0:T(8,128)(2,1)S(1)}, u32[]{:S(2)}, u32[]{:S(2)}) collective-permute-start(bf16[80,512]{1,0:T(8,128)(2,1)S(1)} %get-tuple-element.196), channel_id=1, source_target_pairs={{0,2},{1,3},{2,0},{3,1},{4,6},{5,7},{6,4},{7,5},{8,10},{9,11},{10,... | collective-permute-start | bytes 245768 | tf_op jit(solution)/shard_map/ppermute | solution.py:713
  114.9 12.6 %collective-permute-start.26 = (bf16[80,512]{1,0:T(8,128)(2,1)S(1)}, bf16[80,512]{1,0:T(8,128)(2,1)S(1)}, u32[]{:S(2)}, u32[]{:S(2)}) collective-permute-start(bf16[80,512]{1,0:T(8,128)(2,1)S(1)} %get-tuple-element.195), channel_id=1, source_target_pairs={{0,1},{1,0},{2,3},{3,2},{4,5},{5,4},{6,7},{7,6},{8,9},{9,8},{10,11... | collective-permute-start | bytes 245768 | tf_op jit(solution)/shard_map/ppermute | solution.py:713
  123.1 8.9 %collective-permute-start.23 = (bf16[48,512]{1,0:T(8,128)(2,1)S(1)}, bf16[48,512]{1,0:T(8,128)(2,1)S(1)}, u32[]{:S(2)}, u32[]{:S(2)}) collective-permute-start(bf16[48,512]{1,0:T(8,128)(2,1)S(1)} %get-tuple-element.200), channel_id=1, source_target_pairs={{0,1},{1,0},{2,3},{3,2},{4,5},{5,4},{6,7},{7,6},{8,9},{9,8},{10,11... | collective-permute-start | bytes 147464 | tf_op jit(solution)/shard_map/ppermute | solution.py:713
  127.6 12.1 %collective-permute-start.32 = (bf16[80,512]{1,0:T(8,128)(2,1)S(1)}, bf16[80,512]{1,0:T(8,128)(2,1)S(1)}, u32[]{:S(2)}, u32[]{:S(2)}) collective-permute-start(bf16[80,512]{1,0:T(8,128)(2,1)S(1)} %add_convert_fusion.8), channel_id=1, source_target_pairs={{0,1},{1,0},{2,3},{3,2},{4,5},{5,4},{6,7},{7,6},{8,9},{9,8},{10,11... | collective-permute-start | bytes 245768 | tf_op jit(solution)/shard_map/ppermute | solution.py:713
  129.9 9.7 %collective-permute-start.33 = (bf16[80,512]{1,0:T(8,128)(2,1)S(1)}, bf16[80,512]{1,0:T(8,128)(2,1)S(1)}, u32[]{:S(2)}, u32[]{:S(2)}) collective-permute-start(bf16[80,512]{1,0:T(8,128)(2,1)S(1)} %add_convert_fusion.8), channel_id=1, source_target_pairs={{0,3},{1,2},{2,1},{3,0},{4,7},{5,6},{6,5},{7,4},{8,11},{9,10},{10,... | collective-permute-start | bytes 245768 | tf_op jit(solution)/shard_map/ppermute | solution.py:713
  132.0 9.1 %collective-permute-start.28 = (bf16[56,512]{1,0:T(8,128)(2,1)S(1)}, bf16[56,512]{1,0:T(8,128)(2,1)S(1)}, u32[]{:S(2)}, u32[]{:S(2)}) collective-permute-start(bf16[56,512]{1,0:T(8,128)(2,1)S(1)} %pad_maximum_fusion), channel_id=1, source_target_pairs={{0,2},{1,3},{2,0},{3,1},{4,6},{5,7},{6,4},{7,5},{8,10},{9,11},{10,... | collective-permute-start | bytes 172040 | tf_op jit(solution)/shard_map/ppermute | solution.py:713
  132.1 11.2 %collective-permute-start.29 = (bf16[56,512]{1,0:T(8,128)(2,1)S(1)}, bf16[56,512]{1,0:T(8,128)(2,1)S(1)}, u32[]{:S(2)}, u32[]{:S(2)}) collective-permute-start(bf16[56,512]{1,0:T(8,128)(2,1)S(1)} %pad_maximum_fusion), channel_id=1, source_target_pairs={{0,1},{1,0},{2,3},{3,2},{4,5},{5,4},{6,7},{7,6},{8,9},{9,8},{10,11... | collective-permute-start | bytes 172040 | tf_op jit(solution)/shard_map/ppermute | solution.py:713
  139.8 8.6 %collective-permute-start.37 = (bf16[320,512]{1,0:T(8,128)(2,1)S(1)}, bf16[320,512]{1,0:T(8,128)(2,1)S(1)}, u32[]{:S(2)}, u32[]{:S(2)}) collective-permute-start(bf16[320,512]{1,0:T(8,128)(2,1)S(1)} %constant_dynamic-update-slice_fusion.16), channel_id=1, source_target_pairs={{0,16},{1,17},{2,18},{3,19},{4,20},{5,21},{6,22},{7,23},{8,24},{9,... | collective-permute-start | bytes 983048 | tf_op jit(solution)/shard_map/ppermute | solution.py:713
  141.1 10.8 %collective-permute-start.39 = (bf16[320,512]{1,0:T(8,128)(2,1)S(1)}, bf16[320,512]{1,0:T(8,128)(2,1)S(1)}, u32[]{:S(2)}, u32[]{:S(2)}) collective-permute-start(bf16[320,512]{1,0:T(8,128)(2,1)S(1)} %constant_dynamic-update-slice_fusion.16), channel_id=1, source_target_pairs={{0,24},{1,25},{2,26},{3,27},{4,28},{5,29},{6,30},{7,31},{8,16},{9,... | collective-permute-start | bytes 983048 | tf_op jit(solution)/shard_map/ppermute | solution.py:713
  153.4 12.8 %collective-permute-start.36 = (bf16[224,512]{1,0:T(8,128)(2,1)S(1)}, bf16[224,512]{1,0:T(8,128)(2,1)S(1)}, u32[]{:S(2)}, u32[]{:S(2)}) collective-permute-start(bf16[224,512]{1,0:T(8,128)(2,1)S(1)} %constant_dynamic-update-slice_fusion.20), channel_id=1, source_target_pairs={{0,24},{1,25},{2,26},{3,27},{4,28},{5,29},{6,30},{7,31},{8,16},{9,... | collective-permute-start | bytes 688136 | tf_op jit(solution)/shard_map/ppermute | solution.py:713
  (41 other events, 482.6 us)

commit v4 on v3

--- a/solution.py
+++ b/solution.py
@@ -75,20 +75,42 @@
 
 
 def forward_kernel(
-    seg_ref, tok_ref, g1_ref, wq_ref, wk_ref, wv_ref, wo_ref, rel_ref, hot_ref, g2_ref, win_ref, wout_ref,
-    n1_ref, q_ref, k_ref, v_ref, p_ref, o_ref, hid_ref, n2_ref, act_ref, abar_ref, m_ref,
-    strip_ref, mask_ref, asum_ref, hsum_ref,
+    seg_ref, tok_ref, g1_ref, wq_ref, wk_ref, wv_ref, rel_ref, hot_ref, g2_ref,
+    wo_hbm, win_hbm, wout_hbm,
+    n1_out, q_out, k_out, v_out, p_out, o_out, hid_out, n2_out, act_out, abar_ref, m_ref,
+    strip_ref, mask_ref, asum_ref, hsum_ref, wo_ref, win_ref, wout_ref,
+    n1_ref, q_ref, k_ref, v_ref, p_ref, o_ref, hid_ref, n2_ref, act_ref, in_sem, out_sem, p_sem,
 ):
     step = pl.program_id(0)
     row_count = pl.num_programs(0)
     length, width = tok_ref.shape[1:]
-    heads = p_ref.shape[1]
+    heads = p_ref.shape[0]
     head_size = width // heads
     blocks = length // BLK
-    slots = abar_ref.shape[0] // m_ref.shape[0] * (length // QLEN)
+    slots = length // QLEN
+
+    def fetch(index, source, target):
+        return pltpu.make_async_copy(source, target, in_sem.at[index])
+
+    fetches = [fetch(0, wo_hbm, wo_ref), fetch(1, win_hbm, win_ref), fetch(2, wout_hbm, wout_ref)]
+    singles = [
+        pltpu.make_async_copy(source, target.at[step], out_sem.at[index])
+        for index, (source, target) in enumerate(
+            [
+                (n1_ref, n1_out), (q_ref, q_out), (k_ref, k_out), (v_ref, v_out),
+                (o_ref, o_out), (hid_ref, hid_out), (n2_ref, n2_out), (act_ref, act_out),
+            ]
+        )
+    ]
+
+    def put_pair(index):
+        two = pl.ds(index * 2, 2)
+        return pltpu.make_async_copy(p_ref.at[two], p_out.at[step, two], p_sem.at[index])
 
     @pl.when(step == 0)
     def _():
+        for copy in fetches:
+            copy.start()
         off_bias = dot(rel_ref[...], hot_ref[...])
         for head in range(heads):
             wide = jnp.broadcast_to(off_bias[head : head + 1, :], (BLK, 2 * length))
@@ -97,24 +119,27 @@
 
     x = tok_ref[0].astype(F32)
     n1 = (x * rms_scale(x) * gain_row(g1_ref)).astype(BF16)
-    n1_ref[0] = n1
-    q_ref[0] = dot(n1, wq_ref[...]).astype(BF16)
-    k_ref[0] = dot(n1, wk_ref[...]).astype(BF16)
-    v_ref[0] = dot(n1, wv_ref[...]).astype(BF16)
+    n1_ref[...] = n1
+    q_ref[...] = dot(n1, wq_ref[...]).astype(BF16)
+    k_ref[...] = dot(n1, wk_ref[...]).astype(BF16)
+    v_ref[...] = dot(n1, wv_ref[...]).astype(BF16)
+    for copy in singles[:4]:
+        copy.start()
     onehot = slot_onehot(seg_ref[pl.ds(step, 1), :], slots)
     onehot_f = onehot.astype(F32)
     onehot_low = onehot_f.astype(BF16)
     same = dot(onehot_low, onehot_low, 0, 0)
     mask_ref[...] = jnp.where(same > 0.5, 0.0, MASKED)
     low_lane = lax.broadcasted_iota(jnp.int32, (BLK, 2 * head_size), 1) < head_size
+    low_all = lax.broadcasted_iota(jnp.int32, (length, 2 * head_size), 1) < head_size
 
     def pair(index, carry):
         lanes = pl.ds(pl.multiple_of(index * 2 * head_size, 2 * head_size), 2 * head_size)
-        k_pair = k_ref[0, :, lanes]
-        v_pair = v_ref[0, :, lanes]
+        k_pair = k_ref[:, lanes]
+        v_pair = v_ref[:, lanes]
         for block in range(blocks):
             rows = slice(block * BLK, (block + 1) * BLK)
-            q_pair = q_ref[0, rows, lanes]
+            q_pair = q_ref[rows, lanes]
             for part in range(2):
                 head = index * 2 + part
                 keep = low_lane if part == 0 else jnp.logical_not(low_lane)
@@ -125,19 +150,29 @@
                 top = jnp.max(scores, axis=-1, keepdims=True)
                 exps = jnp.exp(scores - top)
                 total = jnp.sum(exps, axis=-1, keepdims=True)
-                p_ref[0, head, rows, :] = (exps * (1.0 / total)).astype(BF16)
-        low_all = lax.broadcasted_iota(jnp.int32, (length, 2 * head_size), 1) < head_size
-        mixed = [dot(p_ref[0, index * 2 + part], v_pair) for part in range(2)]
-        o_ref[0, :, lanes] = jnp.where(low_all, mixed[0], mixed[1]).astype(BF16)
+                p_ref[head, rows, :] = (exps * (1.0 / total)).astype(BF16)
+        put_pair(index).start()
+        mixed = [dot(p_ref[index * 2 + part], v_pair) for part in range(2)]
+        o_ref[:, lanes] = jnp.where(low_all, mixed[0], mixed[1]).astype(BF16)
         return carry
 
     lax.fori_loop(0, heads // 2, pair, 0)
-    hidden = x + dot(o_ref[0], wo_ref[...])
-    hid_ref[0] = hidden
+    singles[4].start()
+
+    @pl.when(step == 0)
+    def _():
+        for copy in fetches:
+            copy.wait()
+
+    hidden = x + dot(o_ref[...], wo_ref[...])
+    hid_ref[...] = hidden
     n2 = (hidden * rms_scale(hidden) * gain_row(g2_ref)).astype(BF16)
-    n2_ref[0] = n2
+    n2_ref[...] = n2
+    singles[5].start()
+    singles[6].start()
     act = jnp.maximum(dot(n2, win_ref[...]), 0.0).astype(BF16)
-    act_ref[0] = act
+    act_ref[...] = act
+    singles[7].start()
     counts = jnp.maximum(jnp.sum(onehot_f, axis=-1, keepdims=True), 1.0)
     asum = dot(onehot_low, act) / counts
     high, low = split_two(hidden)
@@ -152,6 +187,11 @@
         pooled = hsum_ref[...] + dot(high, wout_ref[...]) + dot(low, wout_ref[...])
         m_ref[...] = pooled.astype(BF16)
 
+    for copy in singles:
+        copy.wait()
+    for index in range(heads // 2):
+        put_pair(index).wait()
+
 
 def whole(shape):
     return pl.BlockSpec(shape, lambda r: (0,) * len(shape))
@@ -167,16 +207,15 @@
     inner = win.shape[1]
     low = lambda *s: jax.ShapeDtypeStruct(s, BF16)
     rlw = (rows, length, width)
+    away = pl.BlockSpec(memory_space=pl.ANY)
     return pl.pallas_call(
         forward_kernel,
         name="forward_rows",
         grid=(rows,),
         in_specs=[whole(seg.shape), per_row((length, width))]
-        + [whole(a.shape) for a in (g1, wq, wk, wv, wo, rel_bias, hot, g2, win, wout)],
-        out_specs=[per_row((length, width))] * 4
-        + [per_row((heads, length, length))]
-        + [per_row((length, width))] * 3
-        + [per_row((length, inner)), whole((rows * slots, inner)), whole((rows * slots, width))],
+        + [whole(a.shape) for a in (g1, wq, wk, wv, rel_bias, hot, g2)]
+        + [away] * 3,
+        out_specs=[away] * 9 + [whole((rows * slots, inner)), whole((rows * slots, width))],
         out_shape=[low(*rlw)] * 4
         + [low(rows, heads, length, length), low(*rlw), jax.ShapeDtypeStruct(rlw, F32), low(*rlw)]
         + [low(rows, length, inner), low(rows * slots, inner), low(rows * slots, width)],
@@ -185,9 +224,23 @@
             pltpu.VMEM((length, length), F32),
             pltpu.VMEM((rows * slots, inner), F32),
             pltpu.VMEM((rows * slots, width), F32),
+            pltpu.VMEM(wo.shape, BF16),
+            pltpu.VMEM(win.shape, BF16),
+            pltpu.VMEM(wout.shape, BF16),
+        ]
+        + [pltpu.VMEM((length, width), BF16)] * 4
+        + [
+            pltpu.VMEM((heads, length, length), BF16),
+            pltpu.VMEM((length, width), BF16),
+            pltpu.VMEM((length, width), F32),
+            pltpu.VMEM((length, width), BF16),
+            pltpu.VMEM((length, inner), BF16),
+            pltpu.SemaphoreType.DMA((3,)),
+            pltpu.SemaphoreType.DMA((8,)),
+            pltpu.SemaphoreType.DMA((heads // 2,)),
         ],
         compiler_params=pltpu.CompilerParams(vmem_limit_bytes=VMEM_LIMIT),
-    )(seg, tokens, g1, wq, wk, wv, wo, rel_bias, hot, g2, win, wout)
+    )(seg, tokens, g1, wq, wk, wv, rel_bias, hot, g2, wo, win, wout)
 
 
 def chunk_masks(order):
@@ -313,7 +366,7 @@
 def ffn_back_kernel(
     where_ref, seg_ref, dm_ref, act_ref, n2_ref, hid_ref, o_ref, g2_ref, win_ref, wout_ref, wo_ref,
     dh_ref, do_ref, keep_ref, send_ref, g2grad_ref,
-    acc_ref, g2_acc, *, masks
+    acc_ref, du_all, dhb_all, g2_acc, *, masks
 ):
     step = pl.program_id(0)
     last = pl.num_programs(0) - 1
@@ -330,7 +383,8 @@
     dact = dot(onehot_low, dact_slot, 0, 0).astype(BF16)
     act = act_ref[0]
     du = jnp.where(act > 0, dact, jnp.zeros_like(dact))
-    win_part = dot(n2_ref[0], du, 0, 0)
+    here = pl.ds(pl.multiple_of(step * length, length), length)
+    du_all[here, :] = du
     dn2 = dot(du, win_ref[...], 1, 1)
     hidden = hid_ref[0]
     scale = rms_scale(hidden)
@@ -340,28 +394,27 @@
     dh = dy + norm_back(dn2, hidden, scale, gain_row(g2_ref))
     dh_ref[0] = dh
     dhb = dh.astype(BF16)
+    dhb_all[here, :] = dhb
     do_ref[0] = dot(dhb, wo_ref[...], 1, 1).astype(BF16)
-    wo_part = dot(o_ref[0], dhb, 0, 0)
-
-    inner = win_part.shape[1]
-    parts = [win_part[:, at : at + width] for at in range(0, inner, width)] + [wo_part]
 
     @pl.when(step == 0)
     def _():
-        for index, part in enumerate(parts):
-            acc_ref[index * width : (index + 1) * width, :] = part
-        if acc_ref.shape[0] > len(parts) * width:
-            acc_ref[len(parts) * width :, :] = jnp.zeros_like(acc_ref[len(parts) * width :, :])
         g2_acc[...] = g2_part
 
     @pl.when(step > 0)
     def _():
-        for index, part in enumerate(parts):
-            acc_ref[index * width : (index + 1) * width, :] += part
         g2_acc[...] += g2_part
 
     @pl.when(step == last)
     def _():
+        rows, inner = n2_ref.shape[0], du_all.shape[1]
+        turned = n2_ref[...].reshape(rows * length, width).T
+        for at in range(0, inner, width):
+            acc_ref[at : at + width, :] = dot(turned, du_all[:, at : at + width]).astype(BF16)
+        turned = o_ref[...].reshape(rows * length, width).T
+        acc_ref[inner : inner + width, :] = dot(turned, dhb_all[...]).astype(BF16)
+        if acc_ref.shape[0] > inner + width:
+            acc_ref[inner + width :, :] = jnp.zeros_like(acc_ref[inner + width :, :])
         take_chunks(acc_ref, keep_ref, send_ref, where_ref[0], masks)
         g2grad_ref[...] = g2_acc[...]
 
@@ -375,8 +428,7 @@
         name="ffn_back",
         grid=(rows,),
         in_specs=[pl.BlockSpec(memory_space=pltpu.SMEM), whole(seg.shape), whole(dm.shape)]
-        + [per_row((length, inner))]
-        + [per_row((length, width))] * 3
+        + [per_row((length, inner)), whole(n2.shape), per_row((length, width)), whole(mixed.shape)]
         + [whole(a.shape) for a in (g2, win, wout, wo)],
         out_specs=[per_row((length, width))] * 2
         + [whole((lines // 2, width))] * 2
@@ -389,7 +441,9 @@
             jax.ShapeDtypeStruct((1, width), F32),
         ],
         scratch_shapes=[
-            pltpu.VMEM((lines, width), F32),
+            pltpu.VMEM((lines, width), BF16),
+            pltpu.VMEM((rows * length, inner), BF16),
+            pltpu.VMEM((rows * length, width), BF16),
             pltpu.VMEM((1, width), F32),
         ],
         compiler_params=pltpu.CompilerParams(vmem_limit_bytes=VMEM_SHARED),
@@ -794,8 +848,9 @@
     slot = Gather(pooled, groups, total)
     slot.step()
     slot.step()
-    acts = Gather(after(abar, slot.pieces[0]), groups, total)
+    acts = Gather(abar, groups, total)
     acts.step()
+    slot.step(*acts.pieces)
     near, far = slot.rest()
     loss, grad_proj, dm_own, dm_low = contrast_call(
         where, near, far, positives, w_proj, slots, masks
@@ -818,14 +873,14 @@
             big.step(band)
             acts.step(band)
             tie = big.blocks + acts.pieces[:1]
-    qkv = Scatter(grads, groups, total)
     tokens_grad, small = finish(
         tokens, dh, norm1_gain, grad_g2, jnp.asarray(band_table(length), BF16),
         w_query, w_key, w_value, dqkvs, bands,
     )
-    qkv.step(small)
-    big.step(*qkv.blocks)
-    grad_ffn_out = ffn_out_grad(where, *acts.rest(), after(dm_low, *big.blocks), masks)
+    big.step(small)
+    qkv = Scatter([grads[0], after(grads[1], *big.blocks)], groups, total)
+    qkv.step()
+    grad_ffn_out = ffn_out_grad(where, *acts.rest(), after(dm_low, *qkv.blocks), masks)
     qkv.step(grad_ffn_out)
     big.step(*qkv.blocks)
     big_all = Gather(big.rest(), groups, total)

time: 171 us -> 162 us (0.947)
  Pallas kernels: 69.1 us -> 65.2 us
  waiting for transfers between devices: 42 us -> 39 us
    ppermute x42, waiting for transfers between devices: 42 us -> 39 us  [swap(): return lax.ppermute(values, AXES, [(i, i ^ mask) for i in range(total)])]
    pallas_call x1, Pallas kernels: 24.8 us -> 21.9 us  [forward(): pl.pallas_call(forward_kernel, name='forward_rows', grid=(rows,), in_spec...]
  transfers between devices with their start and end apart: 42 -> 42, of which waited for: 17 -> 18; matrix products, arithmetic and copies ran while one was open for 0% -> 1% of each run, Pallas kernels for 20% -> 16%
where the time goes in v4:
time: 162 us; the launch traced here: 161 us
  Pallas kernels  65.2 us (40%)
  starting transfers between devices  50.2 us (31%)
  waiting for transfers between devices  39 us (24%)
  local copies, waits for them, and re-layouts  4.65 us (3%)
    ppermute x42, starting transfers between devices, swap(): return lax.ppermute(values, AXES, [(i, i ^ mask) for i in range(total)])  50.2 us
    ppermute x42, waiting for transfers between devices, swap(): return lax.ppermute(values, AXES, [(i, i ^ mask) for i in range(total)])  39 us
    pallas_call x1, Pallas kernels, forward(): pl.pallas_call(forward_kernel, name='forward_rows', grid=(rows,), in_spec...  21.9 us
    pallas_call x2, Pallas kernels, attn_back(): pl.pallas_call(functools.partial(attn_back_kernel, group=group, masks=mas...  14.7 us
    pallas_call x1, Pallas kernels, ffn_back(): pl.pallas_call(functools.partial(ffn_back_kernel, masks=masks), name='ffn...  13.6 us
    unnamed x70, local copies, waits for them, and re-layouts  4.56 us
    pallas_call x1, Pallas kernels, finish(): pl.pallas_call(functools.partial(finish_kernel, groups=groups), name='fin...  3.84 us
    pallas_call x1, Pallas kernels, ffn_out_grad(): pl.pallas_call(functools.partial(ffn_out_kernel, masks=masks), name='ffn_...  3.65 us
  transfers between devices with their start and end apart: 42, of which 18 were waited for; matrix products, arithmetic and copies ran while one was open for 1% of the time, Pallas kernels for 16%

profile of v4, /device:TPU:0, one launch (start us, length us, event | category | flops | bytes accessed | tf_op | source)
XLA Modules:
  0.0 161.3 jit_solution(11537090660834970141)
XLA Ops:
  0.7 21.9 %forward_rows.1 = (bf16[2,512,512]{2,1,0:T(8,128)(2,1)}, bf16[2,512,512]{2,1,0:T(8,128)(2,1)}, bf16[2,512,512]{2,1,0:T(8,128)(2,1)}, bf16[2,512,512]{2,1,0:T(8,1...) custom-call(s32[2,512]{1,0:T(2,128)} %seg_ref.3, ...), custom_call_target="tpu_custom_call" | custom-call | tf_op jit(solution)/shard_map/forward_rows/pallas_call | solution.py:211
  22.6 5.1 %collective-permute-start.2 = (bf16[16,512]{1,0:T(8,128)(2,1)}, bf16[16,512]{1,0:T(8,128)(2,1)S(1)}, u32[]{:S(2)}, u32[]{:S(2)}) collective-permute-start(bf16[16,512]{1,0:T(8,128)(2,1)} %get-tuple-element.99), channel_id=1, source_target_pairs={{0,3},{1,2},{2,1},{3,0},{4,7},{5,6},{6,5},{7,4},{8,11},{9,10},{10,... | collective-permute-start | bytes 49160 | tf_op jit(solution)/shard_map/ppermute | solution.py:767
  28.4 3.7 %collective-permute-start.8 = (bf16[16,2048]{1,0:T(8,128)(2,1)}, bf16[16,2048]{1,0:T(8,128)(2,1)S(1)}, u32[]{:S(2)}, u32[]{:S(2)}) collective-permute-start(bf16[16,2048]{1,0:T(8,128)(2,1)} %get-tuple-element.122), channel_id=1, source_target_pairs={{0,3},{1,2},{2,1},{3,0},{4,7},{5,6},{6,5},{7,4},{8,11},{9,10},{10,... | collective-permute-start | bytes 196616 | tf_op jit(solution)/shard_map/ppermute | solution.py:767
  34.0 2.5 %collective-permute-start.5 = (bf16[64,512]{1,0:T(8,128)(2,1)S(1)}, bf16[64,512]{1,0:T(8,128)(2,1)S(1)}, u32[]{:S(2)}, u32[]{:S(2)}) collective-permute-start(bf16[64,512]{1,0:T(8,128)(2,1)S(1)} %constant_dynamic-update-slice_fusion), channel_id=1, source_target_pairs={{0,24},{1,25},{2,26},{3,27},{4,28},{5,29},{6,30},{7,31},{8,16},{9,... | collective-permute-start | bytes 196616 | tf_op jit(solution)/shard_map/ppermute | solution.py:767
  42.9 2.7 %contrast_all.1 = (f32[1,1]{1,0:T(1,128)}, f32[512,512]{1,0:T(8,128)}, f32[16,512]{1,0:T(8,128)S(1)}, bf16[512,512]{1,0:T(8,128)(2,1)S(1)}) custom-call(s32[1]{0:T(128)} %bitcast.where_ref.refs_0_, bf16[256,512]{1,0:T(8,128)(2,1)S(1)} %constant_dynamic-update-slice_fusion.4.near_ref, bf16[256,512]{1,0:T(8,128)(2,1)S(1)} %collective-permute-done.9.far_ref, ...), custom_call_target="tpu_custom_call" | custom-call | tf_op jit(solution)/shard_map/contrast_all/pallas_call | solution.py:325
  47.9 13.6 %ffn_back.1 = (f32[2,512,512]{2,1,0:T(8,128)S(1)}, bf16[2,512,512]{2,1,0:T(8,128)(2,1)S(1)}, bf16[1280,512]{1,0:T(8,128)(2,1)S(1)}, bf16[1280,512]{1,0:T(8,128)(2,1)}, f32[1,512]{1,0:T(1,128)S(1)}) custom-call(s32[1]{0:T(128)} %bitcast.where_ref.refs_0_, s32[2,512]{1,0:T(2,128)S(1)} %copy-done.18, f32[16,512]{1,0:T(8,128)S(1)} %get-tuple-element.109.dm_ref, ...), custom_call_target="tpu_custom_call" | custom-call | tf_op jit(solution)/shard_map/ffn_back/pallas_call | solution.py:426
  66.5 7.2 %attn_back_0.1 = (bf16[2,3,512,256]{3,2,1,0:T(8,128)(2,1)S(1)}, f32[4,768]{1,0:T(4,128)S(1)}, bf16[1536,256]{1,0:T(8,128)(2,1)S(1)}) custom-call(s32[1]{0:T(128)} %bitcast.where_ref.refs_0_, bf16[2,512,512]{2,1,0:T(8,128)(2,1)S(1)} %copy-done.2, bf16[2,512,512]{2,1,0:T(8,128)(2,1)S(1)} %copy-done.3, bf16[2,512,512]{2,1,0:T(8,128)(2,1)S(1)} %copy-done.4, ...), custom_call_target="tpu_custom_call" | custom-call | tf_op jit(solution)/shard_map/attn_back_0/pallas_call | solution.py:569
  73.8 2.2 %collective-permute-done.12 = bf16[64,2048]{1,0:T(8,128)(2,1)S(1)} collective-permute-done((bf16[64,2048]{1,0:T(8,128)(2,1)S(1)}, bf16[64,2048]{1,0:T(8,128)(2,1)S(1)}, u32[]{:S(2)}, u32[]{:S(2)}) %collective-permute-start.12) | collective-permute-done | bytes 262176 | tf_op jit(solution)/shard_map/ppermute | solution.py:767
  81.1 7.5 %attn_back_1.1 = (bf16[2,3,512,256]{3,2,1,0:T(8,128)(2,1)S(1)}, f32[4,768]{1,0:T(4,128)S(1)}, bf16[768,512]{1,0:T(8,128)(2,1)S(1)}, bf16[768,512]{1,0:T(8,128)(2,1)S(1)}) custom-call(s32[1]{0:T(128)} %bitcast.where_ref.refs_0_, bf16[2,512,512]{2,1,0:T(8,128)(2,1)S(1)} %copy-done.2, bf16[2,512,512]{2,1,0:T(8,128)(2,1)S(1)} %copy-done.3, ...), custom_call_target="tpu_custom_call" | custom-call | tf_op jit(solution)/shard_map/attn_back_1/pallas_call | solution.py:569
  88.7 3.8 %finish_rows.1 = (bf16[2,512,512]{2,1,0:T(8,128)(2,1)}, bf16[8,512]{1,0:T(8,128)(2,1)S(1)}) custom-call(bf16[2,512,512]{2,1,0:T(8,128)(2,1)S(1)} %copy-done.8, f32[2,512,512]{2,1,0:T(8,128)S(1)} %copy-done.14, bf16[512]{0:T(512)(128)(2,1)S(1)} %copy-done.20, f32[1,512]{1,0:T(1,128)S(1)} %get-tuple-element.115.refs_3_, bf16[768,32]{1,0:T(8,128)(2,1)S(1)} %copy-done.17, ...), custom_call_target="tpu_custom_call" | custom-call | tf_op jit(solution)/shard_map/finish_rows/pallas_call | solution.py:644
  101.3 3.3 %collective-permute-start.27 = (bf16[80,512]{1,0:T(8,128)(2,1)S(1)}, bf16[80,512]{1,0:T(8,128)(2,1)S(1)}, u32[]{:S(2)}, u32[]{:S(2)}) collective-permute-start(bf16[80,512]{1,0:T(8,128)(2,1)S(1)} %get-tuple-element.192), channel_id=1, source_target_pairs={{0,3},{1,2},{2,1},{3,0},{4,7},{5,6},{6,5},{7,4},{8,11},{9,10},{10,... | collective-permute-start | bytes 245768 | tf_op jit(solution)/shard_map/ppermute | solution.py:767
  104.6 3.6 %ffn_out_grad.1 = f32[2048,512]{1,0:T(8,128)} custom-call(s32[1]{0:T(128)} %bitcast.where_ref.refs_0_, bf16[256,2048]{1,0:T(8,128)(2,1)S(1)} %constant_dynamic-update-slice_fusion.12.near_ref, bf16[256,2048]{1,0:T(8,128)(2,1)S(1)} %collective-permute-done.21.far_ref, bf16[512,512]{1,0:T(8,128)(2,1)S(1)} %get-tuple-element.149.dm_ref), custom_call_target="tpu_custom_call" | custom-call | tf_op jit(solution)/shard_map/ffn_out_grad/pallas_call | solution.py:354
  110.0 3.4 %collective-permute-start.24 = (bf16[48,512]{1,0:T(8,128)(2,1)S(1)}, bf16[48,512]{1,0:T(8,128)(2,1)S(1)}, u32[]{:S(2)}, u32[]{:S(2)}) collective-permute-start(bf16[48,512]{1,0:T(8,128)(2,1)S(1)} %get-tuple-element.197), channel_id=1, source_target_pairs={{0,3},{1,2},{2,1},{3,0},{4,7},{5,6},{6,5},{7,4},{8,11},{9,10},{10,... | collective-permute-start | bytes 147464 | tf_op jit(solution)/shard_map/ppermute | solution.py:767
  114.5 3.4 %collective-permute-start.33 = (bf16[80,512]{1,0:T(8,128)(2,1)S(1)}, bf16[80,512]{1,0:T(8,128)(2,1)S(1)}, u32[]{:S(2)}, u32[]{:S(2)}) collective-permute-start(bf16[80,512]{1,0:T(8,128)(2,1)S(1)} %add_convert_fusion.8), channel_id=1, source_target_pairs={{0,3},{1,2},{2,1},{3,0},{4,7},{5,6},{6,5},{7,4},{8,11},{9,10},{10,... | collective-permute-start | bytes 245768 | tf_op jit(solution)/shard_map/ppermute | solution.py:767
  119.0 3.0 %collective-permute-done.22 = bf16[48,512]{1,0:T(8,128)(2,1)S(1)} collective-permute-done((bf16[48,512]{1,0:T(8,128)(2,1)S(1)}, bf16[48,512]{1,0:T(8,128)(2,1)S(1)}, u32[]{:S(2)}, u32[]{:S(2)}) %collective-permute-start.22) | collective-permute-done | bytes 49184 | tf_op jit(solution)/shard_map/ppermute | solution.py:767
  122.4 4.1 %collective-permute-start.28 = (bf16[56,512]{1,0:T(8,128)(2,1)S(1)}, bf16[56,512]{1,0:T(8,128)(2,1)S(1)}, u32[]{:S(2)}, u32[]{:S(2)}) collective-permute-start(bf16[56,512]{1,0:T(8,128)(2,1)S(1)} %pad_maximum_fusion), channel_id=1, source_target_pairs={{0,2},{1,3},{2,0},{3,1},{4,6},{5,7},{6,4},{7,5},{8,10},{9,11},{10,... | collective-permute-start | bytes 172040 | tf_op jit(solution)/shard_map/ppermute | solution.py:767
  126.5 2.3 %collective-permute-done.31 = bf16[80,512]{1,0:T(8,128)(2,1)S(1)} collective-permute-done((bf16[80,512]{1,0:T(8,128)(2,1)S(1)}, bf16[80,512]{1,0:T(8,128)(2,1)S(1)}, u32[]{:S(2)}, u32[]{:S(2)}) %collective-permute-start.31) | collective-permute-done | bytes 81952 | tf_op jit(solution)/shard_map/ppermute | solution.py:767
  132.5 6.8 %collective-permute-done.39 = bf16[320,512]{1,0:T(8,128)(2,1)S(1)} collective-permute-done((bf16[320,512]{1,0:T(8,128)(2,1)S(1)}, bf16[320,512]{1,0:T(8,128)(2,1)S(1)}, u32[]{:S(2)}, u32[]{:S(2)}) %collective-permute-start.39) | collective-permute-done | bytes 327712 | tf_op jit(solution)/shard_map/ppermute | solution.py:767
  139.3 3.4 %collective-permute-done.38 = bf16[320,512]{1,0:T(8,128)(2,1)S(1)} collective-permute-done((bf16[320,512]{1,0:T(8,128)(2,1)S(1)}, bf16[320,512]{1,0:T(8,128)(2,1)S(1)}, u32[]{:S(2)}, u32[]{:S(2)}) %collective-permute-start.38) | collective-permute-done | bytes 327712 | tf_op jit(solution)/shard_map/ppermute | solution.py:767
  146.4 3.0 %unpack_ffn.1 = (f32[512,2048]{1,0:T(8,128)}, f32[512,512]{1,0:T(8,128)}) custom-call(s32[1]{0:T(128)} %bitcast.where_ref.refs_0_, bf16[1280,512]{1,0:T(8,128)(2,1)S(1)} %constant_dynamic-update-slice_fusion.24.near_ref, bf16[1280,512]{1,0:T(8,128)(2,1)S(1)} %collective-permute-done.40.far_ref), custom_call_target="tpu_custom_call" | custom-call | tf_op jit(solution)/shard_map/unpack_ffn/pallas_call | solution.py:693
  149.4 3.0 %collective-permute-done.36 = bf16[224,512]{1,0:T(8,128)(2,1)S(1)} collective-permute-done((bf16[224,512]{1,0:T(8,128)(2,1)S(1)}, bf16[224,512]{1,0:T(8,128)(2,1)S(1)}, u32[]{:S(2)}, u32[]{:S(2)}) %collective-permute-start.36) | collective-permute-done | bytes 229408 | tf_op jit(solution)/shard_map/ppermute | solution.py:767
  152.3 4.3 %collective-permute-done.35 = bf16[224,512]{1,0:T(8,128)(2,1)S(1)} collective-permute-done((bf16[224,512]{1,0:T(8,128)(2,1)S(1)}, bf16[224,512]{1,0:T(8,128)(2,1)S(1)}, u32[]{:S(2)}, u32[]{:S(2)}) %collective-permute-start.35) | collective-permute-done | bytes 229408 | tf_op jit(solution)/shard_map/ppermute | solution.py:767
  156.9 2.5 %collective-permute-done.41.far_ref = bf16[896,512]{1,0:T(8,128)(2,1)S(1)} collective-permute-done((bf16[896,512]{1,0:T(8,128)(2,1)S(1)}, bf16[896,512]{1,0:T(8,128)(2,1)S(1)}, u32[]{:S(2)}, u32[]{:S(2)}) %collective-permute-start.41) | collective-permute-done | bytes 917536 | tf_op jit(solution)/shard_map/ppermute | solution.py:767
  159.3 2.0 %unpack_attn.1 = (f32[512,512]{1,0:T(8,128)}, f32[512,512]{1,0:T(8,128)}, f32[512,512]{1,0:T(8,128)}, f32[1,512]{1,0:T(1,128)}, f32[1,512]{1,0:T(1,128)}, /*index=5*/f32[8,32]{1,0:T(8,128)}) custom-call(s32[1]{0:T(128)} %bitcast.where_ref.refs_0_, bf16[896,512]{1,0:T(8,128)(2,1)S(1)} %constant_dynamic-update-slice_fusion.28.near_ref, ...), custom_call_target="tpu_custom_call" | custom-call | tf_op jit(solution)/shard_map/unpack_attn/pallas_call | solution.py:739
  (154 shorter events, 41.9 us)
Async XLA Ops:
  22.6 9.5 %collective-permute-start.2 = (bf16[16,512]{1,0:T(8,128)(2,1)}, bf16[16,512]{1,0:T(8,128)(2,1)S(1)}, u32[]{:S(2)}, u32[]{:S(2)}) collective-permute-start(bf16[16,512]{1,0:T(8,128)(2,1)} %get-tuple-element.99), channel_id=1, source_target_pairs={{0,3},{1,2},{2,1},{3,0},{4,7},{5,6},{6,5},{7,4},{8,11},{9,10},{10,... | collective-permute-start | bytes 49160 | tf_op jit(solution)/shard_map/ppermute | solution.py:767
  61.5 15.5 %collective-permute-start.10 = (bf16[1280,512]{1,0:T(8,128)(2,1)}, bf16[1280,512]{1,0:T(8,128)(2,1)S(1)}, u32[]{:S(2)}, u32[]{:S(2)}) collective-permute-start(bf16[1280,512]{1,0:T(8,128)(2,1)} %get-tuple-element.129), channel_id=1, source_target_pairs={{0,4},{1,5},{2,6},{3,7},{4,0},{5,1},{6,2},{7,3},{8,12},{9,13},{10,... | collective-permute-start | bytes 3932168 | tf_op jit(solution)/shard_map/ppermute | solution.py:767
  61.7 12.0 %collective-permute-start.13 = (bf16[64,2048]{1,0:T(8,128)(2,1)S(1)}, bf16[64,2048]{1,0:T(8,128)(2,1)S(1)}, u32[]{:S(2)}, u32[]{:S(2)}) collective-permute-start(bf16[64,2048]{1,0:T(8,128)(2,1)S(1)} %constant_dynamic-update-slice_fusion.8), channel_id=1, source_target_pairs={{0,24},{1,25},{2,26},{3,27},{4,28},{5,29},{6,30},{7,31},{8,16},{9,... | collective-permute-start | bytes 786440 | tf_op jit(solution)/shard_map/ppermute | solution.py:767
  63.2 12.7 %collective-permute-start.12 = (bf16[64,2048]{1,0:T(8,128)(2,1)S(1)}, bf16[64,2048]{1,0:T(8,128)(2,1)S(1)}, u32[]{:S(2)}, u32[]{:S(2)}) collective-permute-start(bf16[64,2048]{1,0:T(8,128)(2,1)S(1)} %constant_dynamic-update-slice_fusion.8), channel_id=1, source_target_pairs={{0,8},{1,9},{2,10},{3,11},{4,12},{5,13},{6,14},{7,15},{8,0},{9,1},... | collective-permute-start | bytes 786440 | tf_op jit(solution)/shard_map/ppermute | solution.py:767
  63.8 13.1 %collective-permute-start.11 = (bf16[64,2048]{1,0:T(8,128)(2,1)S(1)}, bf16[64,2048]{1,0:T(8,128)(2,1)S(1)}, u32[]{:S(2)}, u32[]{:S(2)}) collective-permute-start(bf16[64,2048]{1,0:T(8,128)(2,1)S(1)} %constant_dynamic-update-slice_fusion.8), channel_id=1, source_target_pairs={{0,16},{1,17},{2,18},{3,19},{4,20},{5,21},{6,22},{7,23},{8,24},{9,... | collective-permute-start | bytes 786440 | tf_op jit(solution)/shard_map/ppermute | solution.py:767
  77.4 15.1 %collective-permute-start.16 = (bf16[320,512]{1,0:T(8,128)(2,1)S(1)}, bf16[320,512]{1,0:T(8,128)(2,1)S(1)}, u32[]{:S(2)}, u32[]{:S(2)}) collective-permute-start(bf16[320,512]{1,0:T(8,128)(2,1)S(1)} %get-tuple-element.184), channel_id=1, source_target_pairs={{0,24},{1,25},{2,26},{3,27},{4,28},{5,29},{6,30},{7,31},{8,16},{9,... | collective-permute-start | bytes 983048 | tf_op jit(solution)/shard_map/ppermute | solution.py:767
  79.0 15.1 %collective-permute-start.15 = (bf16[320,512]{1,0:T(8,128)(2,1)S(1)}, bf16[320,512]{1,0:T(8,128)(2,1)S(1)}, u32[]{:S(2)}, u32[]{:S(2)}) collective-permute-start(bf16[320,512]{1,0:T(8,128)(2,1)S(1)} %get-tuple-element.185), channel_id=1, source_target_pairs={{0,8},{1,9},{2,10},{3,11},{4,12},{5,13},{6,14},{7,15},{8,0},{9,1},... | collective-permute-start | bytes 983048 | tf_op jit(solution)/shard_map/ppermute | solution.py:767
  79.5 15.5 %collective-permute-start.14 = (bf16[320,512]{1,0:T(8,128)(2,1)S(1)}, bf16[320,512]{1,0:T(8,128)(2,1)S(1)}, u32[]{:S(2)}, u32[]{:S(2)}) collective-permute-start(bf16[320,512]{1,0:T(8,128)(2,1)S(1)} %get-tuple-element.186), channel_id=1, source_target_pairs={{0,16},{1,17},{2,18},{3,19},{4,20},{5,21},{6,22},{7,23},{8,24},{9,... | collective-permute-start | bytes 983048 | tf_op jit(solution)/shard_map/ppermute | solution.py:767
  95.3 9.3 %collective-permute-start.21 = (bf16[256,2048]{1,0:T(8,128)(2,1)S(1)}, bf16[256,2048]{1,0:T(8,128)(2,1)S(1)}, u32[]{:S(2)}, u32[]{:S(2)}) collective-permute-start(bf16[256,2048]{1,0:T(8,128)(2,1)S(1)} %constant_dynamic-update-slice_fusion.12.near_ref), channel_id=1, source_target_pairs={{0,4},{1,5},{2,6},{3,7},{4,0},{5,1},{6,2},{7,3},{8,12},{9,13},{10,... | collective-permute-start | bytes 3145736 | tf_op jit(solution)/shard_map/ppermute | solution.py:767
  97.8 10.5 %collective-permute-start.20 = (bf16[192,512]{1,0:T(8,128)(2,1)S(1)}, bf16[192,512]{1,0:T(8,128)(2,1)S(1)}, u32[]{:S(2)}, u32[]{:S(2)}) collective-permute-start(bf16[192,512]{1,0:T(8,128)(2,1)S(1)} %get-tuple-element.188), channel_id=1, source_target_pairs={{0,24},{1,25},{2,26},{3,27},{4,28},{5,29},{6,30},{7,31},{8,16},{9,... | collective-permute-start | bytes 589832 | tf_op jit(solution)/shard_map/ppermute | solution.py:767
  99.4 10.0 %collective-permute-start.19 = (bf16[192,512]{1,0:T(8,128)(2,1)S(1)}, bf16[192,512]{1,0:T(8,128)(2,1)S(1)}, u32[]{:S(2)}, u32[]{:S(2)}) collective-permute-start(bf16[192,512]{1,0:T(8,128)(2,1)S(1)} %get-tuple-element.189), channel_id=1, source_target_pairs={{0,8},{1,9},{2,10},{3,11},{4,12},{5,13},{6,14},{7,15},{8,0},{9,1},... | collective-permute-start | bytes 589832 | tf_op jit(solution)/shard_map/ppermute | solution.py:767
  99.9 10.0 %collective-permute-start.18 = (bf16[192,512]{1,0:T(8,128)(2,1)S(1)}, bf16[192,512]{1,0:T(8,128)(2,1)S(1)}, u32[]{:S(2)}, u32[]{:S(2)}) collective-permute-start(bf16[192,512]{1,0:T(8,128)(2,1)S(1)} %get-tuple-element.190), channel_id=1, source_target_pairs={{0,16},{1,17},{2,18},{3,19},{4,20},{5,21},{6,22},{7,23},{8,24},{9,... | collective-permute-start | bytes 589832 | tf_op jit(solution)/shard_map/ppermute | solution.py:767
  101.3 12.0 %collective-permute-start.27 = (bf16[80,512]{1,0:T(8,128)(2,1)S(1)}, bf16[80,512]{1,0:T(8,128)(2,1)S(1)}, u32[]{:S(2)}, u32[]{:S(2)}) collective-permute-start(bf16[80,512]{1,0:T(8,128)(2,1)S(1)} %get-tuple-element.192), channel_id=1, source_target_pairs={{0,3},{1,2},{2,1},{3,0},{4,7},{5,6},{6,5},{7,4},{8,11},{9,10},{10,... | collective-permute-start | bytes 245768 | tf_op jit(solution)/shard_map/ppermute | solution.py:767
  104.6 9.8 %collective-permute-start.26 = (bf16[80,512]{1,0:T(8,128)(2,1)S(1)}, bf16[80,512]{1,0:T(8,128)(2,1)S(1)}, u32[]{:S(2)}, u32[]{:S(2)}) collective-permute-start(bf16[80,512]{1,0:T(8,128)(2,1)S(1)} %get-tuple-element.193), channel_id=1, source_target_pairs={{0,1},{1,0},{2,3},{3,2},{4,5},{5,4},{6,7},{7,6},{8,9},{9,8},{10,11... | collective-permute-start | bytes 245768 | tf_op jit(solution)/shard_map/ppermute | solution.py:767
  117.9 10.9 %collective-permute-start.31 = (bf16[80,512]{1,0:T(8,128)(2,1)S(1)}, bf16[80,512]{1,0:T(8,128)(2,1)S(1)}, u32[]{:S(2)}, u32[]{:S(2)}) collective-permute-start(bf16[80,512]{1,0:T(8,128)(2,1)S(1)} %add_convert_fusion.8), channel_id=1, source_target_pairs={{0,2},{1,3},{2,0},{3,1},{4,6},{5,7},{6,4},{7,5},{8,10},{9,11},{10,... | collective-permute-start | bytes 245768 | tf_op jit(solution)/shard_map/ppermute | solution.py:767
  122.0 9.0 %collective-permute-start.30 = (bf16[56,512]{1,0:T(8,128)(2,1)S(1)}, bf16[56,512]{1,0:T(8,128)(2,1)S(1)}, u32[]{:S(2)}, u32[]{:S(2)}) collective-permute-start(bf16[56,512]{1,0:T(8,128)(2,1)S(1)} %pad_maximum_fusion), channel_id=1, source_target_pairs={{0,3},{1,2},{2,1},{3,0},{4,7},{5,6},{6,5},{7,4},{8,11},{9,10},{10,... | collective-permute-start | bytes 172040 | tf_op jit(solution)/shard_map/ppermute | solution.py:767
  122.4 10.1 %collective-permute-start.29 = (bf16[56,512]{1,0:T(8,128)(2,1)S(1)}, bf16[56,512]{1,0:T(8,128)(2,1)S(1)}, u32[]{:S(2)}, u32[]{:S(2)}) collective-permute-start(bf16[56,512]{1,0:T(8,128)(2,1)S(1)} %pad_maximum_fusion), channel_id=1, source_target_pairs={{0,1},{1,0},{2,3},{3,2},{4,5},{5,4},{6,7},{7,6},{8,9},{9,8},{10,11... | collective-permute-start | bytes 172040 | tf_op jit(solution)/shard_map/ppermute | solution.py:767
  122.4 10.0 %collective-permute-start.28 = (bf16[56,512]{1,0:T(8,128)(2,1)S(1)}, bf16[56,512]{1,0:T(8,128)(2,1)S(1)}, u32[]{:S(2)}, u32[]{:S(2)}) collective-permute-start(bf16[56,512]{1,0:T(8,128)(2,1)S(1)} %pad_maximum_fusion), channel_id=1, source_target_pairs={{0,2},{1,3},{2,0},{3,1},{4,6},{5,7},{6,4},{7,5},{8,10},{9,11},{10,... | collective-permute-start | bytes 172040 | tf_op jit(solution)/shard_map/ppermute | solution.py:767
  128.9 10.4 %collective-permute-start.39 = (bf16[320,512]{1,0:T(8,128)(2,1)S(1)}, bf16[320,512]{1,0:T(8,128)(2,1)S(1)}, u32[]{:S(2)}, u32[]{:S(2)}) collective-permute-start(bf16[320,512]{1,0:T(8,128)(2,1)S(1)} %constant_dynamic-update-slice_fusion.16), channel_id=1, source_target_pairs={{0,24},{1,25},{2,26},{3,27},{4,28},{5,29},{6,30},{7,31},{8,16},{9,... | collective-permute-start | bytes 983048 | tf_op jit(solution)/shard_map/ppermute | solution.py:767
  130.5 12.2 %collective-permute-start.38 = (bf16[320,512]{1,0:T(8,128)(2,1)S(1)}, bf16[320,512]{1,0:T(8,128)(2,1)S(1)}, u32[]{:S(2)}, u32[]{:S(2)}) collective-permute-start(bf16[320,512]{1,0:T(8,128)(2,1)S(1)} %constant_dynamic-update-slice_fusion.16), channel_id=1, source_target_pairs={{0,8},{1,9},{2,10},{3,11},{4,12},{5,13},{6,14},{7,15},{8,0},{9,1},... | collective-permute-start | bytes 983048 | tf_op jit(solution)/shard_map/ppermute | solution.py:767
  131.0 11.6 %collective-permute-start.37 = (bf16[320,512]{1,0:T(8,128)(2,1)S(1)}, bf16[320,512]{1,0:T(8,128)(2,1)S(1)}, u32[]{:S(2)}, u32[]{:S(2)}) collective-permute-start(bf16[320,512]{1,0:T(8,128)(2,1)S(1)} %constant_dynamic-update-slice_fusion.16), channel_id=1, source_target_pairs={{0,16},{1,17},{2,18},{3,19},{4,20},{5,21},{6,22},{7,23},{8,24},{9,... | collective-permute-start | bytes 983048 | tf_op jit(solution)/shard_map/ppermute | solution.py:767
  142.9 9.5 %collective-permute-start.36 = (bf16[224,512]{1,0:T(8,128)(2,1)S(1)}, bf16[224,512]{1,0:T(8,128)(2,1)S(1)}, u32[]{:S(2)}, u32[]{:S(2)}) collective-permute-start(bf16[224,512]{1,0:T(8,128)(2,1)S(1)} %constant_dynamic-update-slice_fusion.20), channel_id=1, source_target_pairs={{0,24},{1,25},{2,26},{3,27},{4,28},{5,29},{6,30},{7,31},{8,16},{9,... | collective-permute-start | bytes 688136 | tf_op jit(solution)/shard_map/ppermute | solution.py:767
  144.5 12.2 %collective-permute-start.35 = (bf16[224,512]{1,0:T(8,128)(2,1)S(1)}, bf16[224,512]{1,0:T(8,128)(2,1)S(1)}, u32[]{:S(2)}, u32[]{:S(2)}) collective-permute-start(bf16[224,512]{1,0:T(8,128)(2,1)S(1)} %constant_dynamic-update-slice_fusion.20), channel_id=1, source_target_pairs={{0,8},{1,9},{2,10},{3,11},{4,12},{5,13},{6,14},{7,15},{8,0},{9,1},... | collective-permute-start | bytes 688136 | tf_op jit(solution)/shard_map/ppermute | solution.py:767
  145.8 10.9 %collective-permute-start.34 = (bf16[224,512]{1,0:T(8,128)(2,1)S(1)}, bf16[224,512]{1,0:T(8,128)(2,1)S(1)}, u32[]{:S(2)}, u32[]{:S(2)}) collective-permute-start(bf16[224,512]{1,0:T(8,128)(2,1)S(1)} %constant_dynamic-update-slice_fusion.20), channel_id=1, source_target_pairs={{0,16},{1,17},{2,18},{3,19},{4,20},{5,21},{6,22},{7,23},{8,24},{9,... | collective-permute-start | bytes 688136 | tf_op jit(solution)/shard_map/ppermute | solution.py:767
  (41 other events, 411.8 us)

commit v5 on v4

--- a/solution.py
+++ b/solution.py
@@ -79,7 +79,7 @@
     wo_hbm, win_hbm, wout_hbm,
     n1_out, q_out, k_out, v_out, p_out, o_out, hid_out, n2_out, act_out, abar_ref, m_ref,
     strip_ref, mask_ref, asum_ref, hsum_ref, wo_ref, win_ref, wout_ref,
-    n1_ref, q_ref, k_ref, v_ref, p_ref, o_ref, hid_ref, n2_ref, act_ref, in_sem, out_sem, p_sem,
+    n1_ref, q_ref, k_ref, v_ref, p_ref, o_ref, hid_ref, n2_ref, act_ref, in_sem, out_sem, late_sem, p_sem,
 ):
     step = pl.program_id(0)
     row_count = pl.num_programs(0)
@@ -98,10 +98,15 @@
         for index, (source, target) in enumerate(
             [
                 (n1_ref, n1_out), (q_ref, q_out), (k_ref, k_out), (v_ref, v_out),
-                (o_ref, o_out), (hid_ref, hid_out), (n2_ref, n2_out), (act_ref, act_out),
             ]
         )
     ]
+
+    def put_late(index, row):
+        source, target = (
+            (o_ref, o_out), (hid_ref, hid_out), (n2_ref, n2_out), (act_ref, act_out)
+        )[index]
+        return pltpu.make_async_copy(source.at[row], target.at[row], late_sem.at[index, row])
 
     def put_pair(index):
         two = pl.ds(index * 2, 2)
@@ -123,7 +128,7 @@
     q_ref[...] = dot(n1, wq_ref[...]).astype(BF16)
     k_ref[...] = dot(n1, wk_ref[...]).astype(BF16)
     v_ref[...] = dot(n1, wv_ref[...]).astype(BF16)
-    for copy in singles[:4]:
+    for copy in singles:
         copy.start()
     onehot = slot_onehot(seg_ref[pl.ds(step, 1), :], slots)
     onehot_f = onehot.astype(F32)
@@ -153,26 +158,26 @@
                 p_ref[head, rows, :] = (exps * (1.0 / total)).astype(BF16)
         put_pair(index).start()
         mixed = [dot(p_ref[index * 2 + part], v_pair) for part in range(2)]
-        o_ref[:, lanes] = jnp.where(low_all, mixed[0], mixed[1]).astype(BF16)
+        o_ref[step, :, lanes] = jnp.where(low_all, mixed[0], mixed[1]).astype(BF16)
         return carry
 
     lax.fori_loop(0, heads // 2, pair, 0)
-    singles[4].start()
+    put_late(0, step).start()
 
     @pl.when(step == 0)
     def _():
         for copy in fetches:
             copy.wait()
 
-    hidden = x + dot(o_ref[...], wo_ref[...])
-    hid_ref[...] = hidden
+    hidden = x + dot(o_ref[step], wo_ref[...])
+    hid_ref[step] = hidden
     n2 = (hidden * rms_scale(hidden) * gain_row(g2_ref)).astype(BF16)
-    n2_ref[...] = n2
-    singles[5].start()
-    singles[6].start()
+    n2_ref[step] = n2
+    put_late(1, step).start()
+    put_late(2, step).start()
     act = jnp.maximum(dot(n2, win_ref[...]), 0.0).astype(BF16)
-    act_ref[...] = act
-    singles[7].start()
+    act_ref[step] = act
+    put_late(3, step).start()
     counts = jnp.maximum(jnp.sum(onehot_f, axis=-1, keepdims=True), 1.0)
     asum = dot(onehot_low, act) / counts
     high, low = split_two(hidden)
@@ -186,6 +191,9 @@
         abar_ref[...] = high
         pooled = hsum_ref[...] + dot(high, wout_ref[...]) + dot(low, wout_ref[...])
         m_ref[...] = pooled.astype(BF16)
+        for row in range(act_ref.shape[0]):
+            for index in range(4):
+                put_late(index, row).wait()
 
     for copy in singles:
         copy.wait()
@@ -231,12 +239,13 @@
         + [pltpu.VMEM((length, width), BF16)] * 4
         + [
             pltpu.VMEM((heads, length, length), BF16),
-            pltpu.VMEM((length, width), BF16),
-            pltpu.VMEM((length, width), F32),
-            pltpu.VMEM((length, width), BF16),
-            pltpu.VMEM((length, inner), BF16),
+            pltpu.VMEM(rlw, BF16),
+            pltpu.VMEM(rlw, F32),
+            pltpu.VMEM(rlw, BF16),
+            pltpu.VMEM((rows, length, inner), BF16),
             pltpu.SemaphoreType.DMA((3,)),
-            pltpu.SemaphoreType.DMA((8,)),
+            pltpu.SemaphoreType.DMA((4,)),
+            pltpu.SemaphoreType.DMA((4, rows)),
             pltpu.SemaphoreType.DMA((heads // 2,)),
         ],
         compiler_params=pltpu.CompilerParams(vmem_limit_bytes=VMEM_LIMIT),
@@ -880,16 +889,16 @@
     big.step(small)
     qkv = Scatter([grads[0], after(grads[1], *big.blocks)], groups, total)
     qkv.step()
-    grad_ffn_out = ffn_out_grad(where, *acts.rest(), after(dm_low, *qkv.blocks), masks)
-    qkv.step(grad_ffn_out)
     big.step(*qkv.blocks)
     big_all = Gather(big.rest(), groups, total)
     big_all.step()
     qkv.step(big_all.pieces[0])
+    big_all.step(*qkv.blocks)
+    qkv.step(big_all.pieces[0])
     qkv_all = Gather(jnp.concatenate([qkv.rest(), small], axis=0), groups, total)
     qkv_all.step()
-    big_all.step(qkv_all.pieces[0])
-    qkv_all.step(big_all.pieces[0])
+    grad_ffn_out = ffn_out_grad(where, *acts.rest(), after(dm_low, qkv_all.pieces[0]), masks)
+    qkv_all.step(grad_ffn_out)
     big_all.step(qkv_all.pieces[0])
     win, wo = unpack_big(where, *big_all.rest(), inner, width, masks)
     qkv_all.step(wo)

time: 162 us -> 159 us (0.981)
  waiting for transfers between devices: 39 us -> 36 us
    ppermute x42, waiting for transfers between devices: 39 us -> 36 us  [swap(): return lax.ppermute(values, AXES, [(i, i ^ mask) for i in range(total)])]
  transfers between devices with their start and end apart: 42 -> 42, of which waited for: 18 -> 24; matrix products, arithmetic and copies ran while one was open for 1% -> 1% of each run, Pallas kernels for 16% -> 16%
where the time goes in v5:
time: 159 us
  Pallas kernels  64.3 us (40%)
  starting transfers between devices  51.5 us (32%)
  waiting for transfers between devices  36 us (23%)
  local copies, waits for them, and re-layouts  4.65 us (3%)
    ppermute x42, starting transfers between devices, swap(): return lax.ppermute(values, AXES, [(i, i ^ mask) for i in range(total)])  51.5 us
    ppermute x42, waiting for transfers between devices, swap(): return lax.ppermute(values, AXES, [(i, i ^ mask) for i in range(total)])  36 us
    pallas_call x1, Pallas kernels, forward(): pl.pallas_call(forward_kernel, name='forward_rows', grid=(rows,), in_spec...  21 us
    pallas_call x2, Pallas kernels, attn_back(): pl.pallas_call(functools.partial(attn_back_kernel, group=group, masks=mas...  14.7 us
    pallas_call x1, Pallas kernels, ffn_back(): pl.pallas_call(functools.partial(ffn_back_kernel, masks=masks), name='ffn...  13.6 us
    unnamed x70, local copies, waits for them, and re-layouts  4.56 us
    pallas_call x1, Pallas kernels, finish(): pl.pallas_call(functools.partial(finish_kernel, groups=groups), name='fin...  3.84 us
    pallas_call x1, Pallas kernels, ffn_out_grad(): pl.pallas_call(functools.partial(ffn_out_kernel, masks=masks), name='ffn_...  3.65 us
  transfers between devices with their start and end apart: 42, of which 24 were waited for; matrix products, arithmetic and copies ran while one was open for 1% of the time, Pallas kernels for 16%

profile of v5, /device:TPU:0, one launch (start us, length us, event | category | flops | bytes accessed | tf_op | source)
XLA Modules:
  0.0 158.7 jit_solution(3149858061167273259)
XLA Ops:
  0.7 21.0 %forward_rows.1 = (bf16[2,512,512]{2,1,0:T(8,128)(2,1)}, bf16[2,512,512]{2,1,0:T(8,128)(2,1)}, bf16[2,512,512]{2,1,0:T(8,128)(2,1)}, bf16[2,512,512]{2,1,0:T(8,1...) custom-call(s32[2,512]{1,0:T(2,128)} %seg_ref.3, ...), custom_call_target="tpu_custom_call" | custom-call | tf_op jit(solution)/shard_map/forward_rows/pallas_call | solution.py:219
  21.7 5.2 %collective-permute-start.2 = (bf16[16,512]{1,0:T(8,128)(2,1)}, bf16[16,512]{1,0:T(8,128)(2,1)S(1)}, u32[]{:S(2)}, u32[]{:S(2)}) collective-permute-start(bf16[16,512]{1,0:T(8,128)(2,1)} %get-tuple-element.99), channel_id=1, source_target_pairs={{0,3},{1,2},{2,1},{3,0},{4,7},{5,6},{6,5},{7,4},{8,11},{9,10},{10,... | collective-permute-start | bytes 49160 | tf_op jit(solution)/shard_map/ppermute | solution.py:776
  27.5 3.7 %collective-permute-start.8 = (bf16[16,2048]{1,0:T(8,128)(2,1)}, bf16[16,2048]{1,0:T(8,128)(2,1)S(1)}, u32[]{:S(2)}, u32[]{:S(2)}) collective-permute-start(bf16[16,2048]{1,0:T(8,128)(2,1)} %get-tuple-element.122), channel_id=1, source_target_pairs={{0,3},{1,2},{2,1},{3,0},{4,7},{5,6},{6,5},{7,4},{8,11},{9,10},{10,... | collective-permute-start | bytes 196616 | tf_op jit(solution)/shard_map/ppermute | solution.py:776
  33.0 2.5 %collective-permute-start.5 = (bf16[64,512]{1,0:T(8,128)(2,1)S(1)}, bf16[64,512]{1,0:T(8,128)(2,1)S(1)}, u32[]{:S(2)}, u32[]{:S(2)}) collective-permute-start(bf16[64,512]{1,0:T(8,128)(2,1)S(1)} %constant_dynamic-update-slice_fusion), channel_id=1, source_target_pairs={{0,24},{1,25},{2,26},{3,27},{4,28},{5,29},{6,30},{7,31},{8,16},{9,... | collective-permute-start | bytes 196616 | tf_op jit(solution)/shard_map/ppermute | solution.py:776
  42.0 2.7 %contrast_all.1 = (f32[1,1]{1,0:T(1,128)}, f32[512,512]{1,0:T(8,128)}, f32[16,512]{1,0:T(8,128)S(1)}, bf16[512,512]{1,0:T(8,128)(2,1)S(1)}) custom-call(s32[1]{0:T(128)} %bitcast.where_ref.refs_0_, bf16[256,512]{1,0:T(8,128)(2,1)S(1)} %constant_dynamic-update-slice_fusion.4.near_ref, bf16[256,512]{1,0:T(8,128)(2,1)S(1)} %collective-permute-done.9.far_ref, ...), custom_call_target="tpu_custom_call" | custom-call | tf_op jit(solution)/shard_map/contrast_all/pallas_call | solution.py:334
  47.0 13.6 %ffn_back.1 = (f32[2,512,512]{2,1,0:T(8,128)S(1)}, bf16[2,512,512]{2,1,0:T(8,128)(2,1)S(1)}, bf16[1280,512]{1,0:T(8,128)(2,1)S(1)}, bf16[1280,512]{1,0:T(8,128)(2,1)}, f32[1,512]{1,0:T(1,128)S(1)}) custom-call(s32[1]{0:T(128)} %bitcast.where_ref.refs_0_, s32[2,512]{1,0:T(2,128)S(1)} %copy-done.18, f32[16,512]{1,0:T(8,128)S(1)} %get-tuple-element.109.dm_ref, ...), custom_call_target="tpu_custom_call" | custom-call | tf_op jit(solution)/shard_map/ffn_back/pallas_call | solution.py:435
  65.6 7.2 %attn_back_0.1 = (bf16[2,3,512,256]{3,2,1,0:T(8,128)(2,1)S(1)}, f32[4,768]{1,0:T(4,128)S(1)}, bf16[1536,256]{1,0:T(8,128)(2,1)S(1)}) custom-call(s32[1]{0:T(128)} %bitcast.where_ref.refs_0_, bf16[2,512,512]{2,1,0:T(8,128)(2,1)S(1)} %copy-done.2, bf16[2,512,512]{2,1,0:T(8,128)(2,1)S(1)} %copy-done.3, bf16[2,512,512]{2,1,0:T(8,128)(2,1)S(1)} %copy-done.4, ...), custom_call_target="tpu_custom_call" | custom-call | tf_op jit(solution)/shard_map/attn_back_0/pallas_call | solution.py:578
  72.9 2.2 %collective-permute-done.12 = bf16[64,2048]{1,0:T(8,128)(2,1)S(1)} collective-permute-done((bf16[64,2048]{1,0:T(8,128)(2,1)S(1)}, bf16[64,2048]{1,0:T(8,128)(2,1)S(1)}, u32[]{:S(2)}, u32[]{:S(2)}) %collective-permute-start.12) | collective-permute-done | bytes 262176 | tf_op jit(solution)/shard_map/ppermute | solution.py:776
  80.2 7.5 %attn_back_1.1 = (bf16[2,3,512,256]{3,2,1,0:T(8,128)(2,1)S(1)}, f32[4,768]{1,0:T(4,128)S(1)}, bf16[768,512]{1,0:T(8,128)(2,1)S(1)}, bf16[768,512]{1,0:T(8,128)(2,1)S(1)}) custom-call(s32[1]{0:T(128)} %bitcast.where_ref.refs_0_, bf16[2,512,512]{2,1,0:T(8,128)(2,1)S(1)} %copy-done.2, bf16[2,512,512]{2,1,0:T(8,128)(2,1)S(1)} %copy-done.3, ...), custom_call_target="tpu_custom_call" | custom-call | tf_op jit(solution)/shard_map/attn_back_1/pallas_call | solution.py:578
  87.8 3.8 %finish_rows.1 = (bf16[2,512,512]{2,1,0:T(8,128)(2,1)}, bf16[8,512]{1,0:T(8,128)(2,1)S(1)}) custom-call(bf16[2,512,512]{2,1,0:T(8,128)(2,1)S(1)} %copy-done.8, f32[2,512,512]{2,1,0:T(8,128)S(1)} %copy-done.14, bf16[512]{0:T(512)(128)(2,1)S(1)} %copy-done.20, f32[1,512]{1,0:T(1,128)S(1)} %get-tuple-element.115.refs_3_, bf16[768,32]{1,0:T(8,128)(2,1)S(1)} %copy-done.17, ...), custom_call_target="tpu_custom_call" | custom-call | tf_op jit(solution)/shard_map/finish_rows/pallas_call | solution.py:653
  94.9 3.3 %collective-permute-start.23 = (bf16[80,512]{1,0:T(8,128)(2,1)S(1)}, bf16[80,512]{1,0:T(8,128)(2,1)S(1)}, u32[]{:S(2)}, u32[]{:S(2)}) collective-permute-start(bf16[80,512]{1,0:T(8,128)(2,1)S(1)} %get-tuple-element.192), channel_id=1, source_target_pairs={{0,3},{1,2},{2,1},{3,0},{4,7},{5,6},{6,5},{7,4},{8,11},{9,10},{10,... | collective-permute-start | bytes 245768 | tf_op jit(solution)/shard_map/ppermute | solution.py:776
  105.5 2.5 %collective-permute-start.29 = (bf16[80,512]{1,0:T(8,128)(2,1)S(1)}, bf16[80,512]{1,0:T(8,128)(2,1)S(1)}, u32[]{:S(2)}, u32[]{:S(2)}) collective-permute-start(bf16[80,512]{1,0:T(8,128)(2,1)S(1)} %add_convert_fusion.8), channel_id=1, source_target_pairs={{0,3},{1,2},{2,1},{3,0},{4,7},{5,6},{6,5},{7,4},{8,11},{9,10},{10,... | collective-permute-start | bytes 245768 | tf_op jit(solution)/shard_map/ppermute | solution.py:776
  109.9 2.2 %collective-permute-start.27 = (bf16[80,512]{1,0:T(8,128)(2,1)S(1)}, bf16[80,512]{1,0:T(8,128)(2,1)S(1)}, u32[]{:S(2)}, u32[]{:S(2)}) collective-permute-start(bf16[80,512]{1,0:T(8,128)(2,1)S(1)} %add_convert_fusion.8), channel_id=1, source_target_pairs={{0,2},{1,3},{2,0},{3,1},{4,6},{5,7},{6,4},{7,5},{8,10},{9,11},{10,... | collective-permute-start | bytes 245768 | tf_op jit(solution)/shard_map/ppermute | solution.py:776
  114.2 2.5 %collective-permute-start.24 = (bf16[48,512]{1,0:T(8,128)(2,1)S(1)}, bf16[48,512]{1,0:T(8,128)(2,1)S(1)}, u32[]{:S(2)}, u32[]{:S(2)}) collective-permute-start(bf16[48,512]{1,0:T(8,128)(2,1)S(1)} %get-tuple-element.199), channel_id=1, source_target_pairs={{0,2},{1,3},{2,0},{3,1},{4,6},{5,7},{6,4},{7,5},{8,10},{9,11},{10,... | collective-permute-start | bytes 147464 | tf_op jit(solution)/shard_map/ppermute | solution.py:776
  119.5 3.7 %collective-permute-start.32 = (bf16[56,512]{1,0:T(8,128)(2,1)S(1)}, bf16[56,512]{1,0:T(8,128)(2,1)S(1)}, u32[]{:S(2)}, u32[]{:S(2)}) collective-permute-start(bf16[56,512]{1,0:T(8,128)(2,1)S(1)} %pad_maximum_fusion), channel_id=1, source_target_pairs={{0,3},{1,2},{2,1},{3,0},{4,7},{5,6},{6,5},{7,4},{8,11},{9,10},{10,... | collective-permute-start | bytes 172040 | tf_op jit(solution)/shard_map/ppermute | solution.py:776
  123.9 2.4 %collective-permute-start.39 = (bf16[320,512]{1,0:T(8,128)(2,1)S(1)}, bf16[320,512]{1,0:T(8,128)(2,1)S(1)}, u32[]{:S(2)}, u32[]{:S(2)}) collective-permute-start(bf16[320,512]{1,0:T(8,128)(2,1)S(1)} %constant_dynamic-update-slice_fusion.16), channel_id=1, source_target_pairs={{0,24},{1,25},{2,26},{3,27},{4,28},{5,29},{6,30},{7,31},{8,16},{9,... | collective-permute-start | bytes 983048 | tf_op jit(solution)/shard_map/ppermute | solution.py:776
  126.8 3.6 %ffn_out_grad.1 = f32[2048,512]{1,0:T(8,128)} custom-call(s32[1]{0:T(128)} %bitcast.where_ref.refs_0_, bf16[256,2048]{1,0:T(8,128)(2,1)S(1)} %constant_dynamic-update-slice_fusion.12.near_ref, bf16[256,2048]{1,0:T(8,128)(2,1)S(1)} %collective-permute-done.33.far_ref, bf16[512,512]{1,0:T(8,128)(2,1)S(1)} %get-tuple-element.162.dm_ref), custom_call_target="tpu_custom_call" | custom-call | tf_op jit(solution)/shard_map/ffn_out_grad/pallas_call | solution.py:363
  131.1 4.3 %collective-permute-done.39 = bf16[320,512]{1,0:T(8,128)(2,1)S(1)} collective-permute-done((bf16[320,512]{1,0:T(8,128)(2,1)S(1)}, bf16[320,512]{1,0:T(8,128)(2,1)S(1)}, u32[]{:S(2)}, u32[]{:S(2)}) %collective-permute-start.39) | collective-permute-done | bytes 327712 | tf_op jit(solution)/shard_map/ppermute | solution.py:776
  135.4 4.1 %collective-permute-done.38 = bf16[320,512]{1,0:T(8,128)(2,1)S(1)} collective-permute-done((bf16[320,512]{1,0:T(8,128)(2,1)S(1)}, bf16[320,512]{1,0:T(8,128)(2,1)S(1)}, u32[]{:S(2)}, u32[]{:S(2)}) %collective-permute-start.38) | collective-permute-done | bytes 327712 | tf_op jit(solution)/shard_map/ppermute | solution.py:776
  140.2 2.1 %collective-permute-start.36 = (bf16[224,512]{1,0:T(8,128)(2,1)S(1)}, bf16[224,512]{1,0:T(8,128)(2,1)S(1)}, u32[]{:S(2)}, u32[]{:S(2)}) collective-permute-start(bf16[224,512]{1,0:T(8,128)(2,1)S(1)} %constant_dynamic-update-slice_fusion.20), channel_id=1, source_target_pairs={{0,24},{1,25},{2,26},{3,27},{4,28},{5,29},{6,30},{7,31},{8,16},{9,... | collective-permute-start | bytes 688136 | tf_op jit(solution)/shard_map/ppermute | solution.py:776
  143.8 3.0 %unpack_ffn.1 = (f32[512,2048]{1,0:T(8,128)}, f32[512,512]{1,0:T(8,128)}) custom-call(s32[1]{0:T(128)} %bitcast.where_ref.refs_0_, bf16[1280,512]{1,0:T(8,128)(2,1)S(1)} %constant_dynamic-update-slice_fusion.24.near_ref, bf16[1280,512]{1,0:T(8,128)(2,1)S(1)} %collective-permute-done.40.far_ref), custom_call_target="tpu_custom_call" | custom-call | tf_op jit(solution)/shard_map/unpack_ffn/pallas_call | solution.py:702
  146.7 3.0 %collective-permute-done.36 = bf16[224,512]{1,0:T(8,128)(2,1)S(1)} collective-permute-done((bf16[224,512]{1,0:T(8,128)(2,1)S(1)}, bf16[224,512]{1,0:T(8,128)(2,1)S(1)}, u32[]{:S(2)}, u32[]{:S(2)}) %collective-permute-start.36) | collective-permute-done | bytes 229408 | tf_op jit(solution)/shard_map/ppermute | solution.py:776
  149.7 3.9 %collective-permute-done.35 = bf16[224,512]{1,0:T(8,128)(2,1)S(1)} collective-permute-done((bf16[224,512]{1,0:T(8,128)(2,1)S(1)}, bf16[224,512]{1,0:T(8,128)(2,1)S(1)}, u32[]{:S(2)}, u32[]{:S(2)}) %collective-permute-start.35) | collective-permute-done | bytes 229408 | tf_op jit(solution)/shard_map/ppermute | solution.py:776
  154.2 2.5 %collective-permute-done.41.far_ref = bf16[896,512]{1,0:T(8,128)(2,1)S(1)} collective-permute-done((bf16[896,512]{1,0:T(8,128)(2,1)S(1)}, bf16[896,512]{1,0:T(8,128)(2,1)S(1)}, u32[]{:S(2)}, u32[]{:S(2)}) %collective-permute-start.41) | collective-permute-done | bytes 917536 | tf_op jit(solution)/shard_map/ppermute | solution.py:776
  (154 shorter events, 45.1 us)
Async XLA Ops:
  21.7 9.6 %collective-permute-start.2 = (bf16[16,512]{1,0:T(8,128)(2,1)}, bf16[16,512]{1,0:T(8,128)(2,1)S(1)}, u32[]{:S(2)}, u32[]{:S(2)}) collective-permute-start(bf16[16,512]{1,0:T(8,128)(2,1)} %get-tuple-element.99), channel_id=1, source_target_pairs={{0,3},{1,2},{2,1},{3,0},{4,7},{5,6},{6,5},{7,4},{8,11},{9,10},{10,... | collective-permute-start | bytes 49160 | tf_op jit(solution)/shard_map/ppermute | solution.py:776
  27.5 8.6 %collective-permute-start.8 = (bf16[16,2048]{1,0:T(8,128)(2,1)}, bf16[16,2048]{1,0:T(8,128)(2,1)S(1)}, u32[]{:S(2)}, u32[]{:S(2)}) collective-permute-start(bf16[16,2048]{1,0:T(8,128)(2,1)} %get-tuple-element.122), channel_id=1, source_target_pairs={{0,3},{1,2},{2,1},{3,0},{4,7},{5,6},{6,5},{7,4},{8,11},{9,10},{10,... | collective-permute-start | bytes 196616 | tf_op jit(solution)/shard_map/ppermute | solution.py:776
  60.6 15.5 %collective-permute-start.10 = (bf16[1280,512]{1,0:T(8,128)(2,1)}, bf16[1280,512]{1,0:T(8,128)(2,1)S(1)}, u32[]{:S(2)}, u32[]{:S(2)}) collective-permute-start(bf16[1280,512]{1,0:T(8,128)(2,1)} %get-tuple-element.129), channel_id=1, source_target_pairs={{0,4},{1,5},{2,6},{3,7},{4,0},{5,1},{6,2},{7,3},{8,12},{9,13},{10,... | collective-permute-start | bytes 3932168 | tf_op jit(solution)/shard_map/ppermute | solution.py:776
  60.8 12.0 %collective-permute-start.13 = (bf16[64,2048]{1,0:T(8,128)(2,1)S(1)}, bf16[64,2048]{1,0:T(8,128)(2,1)S(1)}, u32[]{:S(2)}, u32[]{:S(2)}) collective-permute-start(bf16[64,2048]{1,0:T(8,128)(2,1)S(1)} %constant_dynamic-update-slice_fusion.8), channel_id=1, source_target_pairs={{0,24},{1,25},{2,26},{3,27},{4,28},{5,29},{6,30},{7,31},{8,16},{9,... | collective-permute-start | bytes 786440 | tf_op jit(solution)/shard_map/ppermute | solution.py:776
  62.3 12.8 %collective-permute-start.12 = (bf16[64,2048]{1,0:T(8,128)(2,1)S(1)}, bf16[64,2048]{1,0:T(8,128)(2,1)S(1)}, u32[]{:S(2)}, u32[]{:S(2)}) collective-permute-start(bf16[64,2048]{1,0:T(8,128)(2,1)S(1)} %constant_dynamic-update-slice_fusion.8), channel_id=1, source_target_pairs={{0,8},{1,9},{2,10},{3,11},{4,12},{5,13},{6,14},{7,15},{8,0},{9,1},... | collective-permute-start | bytes 786440 | tf_op jit(solution)/shard_map/ppermute | solution.py:776
  62.8 13.1 %collective-permute-start.11 = (bf16[64,2048]{1,0:T(8,128)(2,1)S(1)}, bf16[64,2048]{1,0:T(8,128)(2,1)S(1)}, u32[]{:S(2)}, u32[]{:S(2)}) collective-permute-start(bf16[64,2048]{1,0:T(8,128)(2,1)S(1)} %constant_dynamic-update-slice_fusion.8), channel_id=1, source_target_pairs={{0,16},{1,17},{2,18},{3,19},{4,20},{5,21},{6,22},{7,23},{8,24},{9,... | collective-permute-start | bytes 786440 | tf_op jit(solution)/shard_map/ppermute | solution.py:776
  76.5 15.1 %collective-permute-start.16 = (bf16[320,512]{1,0:T(8,128)(2,1)S(1)}, bf16[320,512]{1,0:T(8,128)(2,1)S(1)}, u32[]{:S(2)}, u32[]{:S(2)}) collective-permute-start(bf16[320,512]{1,0:T(8,128)(2,1)S(1)} %get-tuple-element.184), channel_id=1, source_target_pairs={{0,24},{1,25},{2,26},{3,27},{4,28},{5,29},{6,30},{7,31},{8,16},{9,... | collective-permute-start | bytes 983048 | tf_op jit(solution)/shard_map/ppermute | solution.py:776
  78.1 15.1 %collective-permute-start.15 = (bf16[320,512]{1,0:T(8,128)(2,1)S(1)}, bf16[320,512]{1,0:T(8,128)(2,1)S(1)}, u32[]{:S(2)}, u32[]{:S(2)}) collective-permute-start(bf16[320,512]{1,0:T(8,128)(2,1)S(1)} %get-tuple-element.185), channel_id=1, source_target_pairs={{0,8},{1,9},{2,10},{3,11},{4,12},{5,13},{6,14},{7,15},{8,0},{9,1},... | collective-permute-start | bytes 983048 | tf_op jit(solution)/shard_map/ppermute | solution.py:776
  78.6 15.5 %collective-permute-start.14 = (bf16[320,512]{1,0:T(8,128)(2,1)S(1)}, bf16[320,512]{1,0:T(8,128)(2,1)S(1)}, u32[]{:S(2)}, u32[]{:S(2)}) collective-permute-start(bf16[320,512]{1,0:T(8,128)(2,1)S(1)} %get-tuple-element.186), channel_id=1, source_target_pairs={{0,16},{1,17},{2,18},{3,19},{4,20},{5,21},{6,22},{7,23},{8,24},{9,... | collective-permute-start | bytes 983048 | tf_op jit(solution)/shard_map/ppermute | solution.py:776
  94.4 31.9 %collective-permute-start.33 = (bf16[256,2048]{1,0:T(8,128)(2,1)S(1)}, bf16[256,2048]{1,0:T(8,128)(2,1)S(1)}, u32[]{:S(2)}, u32[]{:S(2)}) collective-permute-start(bf16[256,2048]{1,0:T(8,128)(2,1)S(1)} %constant_dynamic-update-slice_fusion.12.near_ref), channel_id=1, source_target_pairs={{0,4},{1,5},{2,6},{3,7},{4,0},{5,1},{6,2},{7,3},{8,12},{9,13},{10,... | collective-permute-start | bytes 3145736 | tf_op jit(solution)/shard_map/ppermute | solution.py:776
  99.5 8.7 %collective-permute-start.20 = (bf16[192,512]{1,0:T(8,128)(2,1)S(1)}, bf16[192,512]{1,0:T(8,128)(2,1)S(1)}, u32[]{:S(2)}, u32[]{:S(2)}) collective-permute-start(bf16[192,512]{1,0:T(8,128)(2,1)S(1)} %get-tuple-element.188), channel_id=1, source_target_pairs={{0,24},{1,25},{2,26},{3,27},{4,28},{5,29},{6,30},{7,31},{8,16},{9,... | collective-permute-start | bytes 589832 | tf_op jit(solution)/shard_map/ppermute | solution.py:776
  102.0 7.9 %collective-permute-start.19 = (bf16[192,512]{1,0:T(8,128)(2,1)S(1)}, bf16[192,512]{1,0:T(8,128)(2,1)S(1)}, u32[]{:S(2)}, u32[]{:S(2)}) collective-permute-start(bf16[192,512]{1,0:T(8,128)(2,1)S(1)} %get-tuple-element.189), channel_id=1, source_target_pairs={{0,8},{1,9},{2,10},{3,11},{4,12},{5,13},{6,14},{7,15},{8,0},{9,1},... | collective-permute-start | bytes 589832 | tf_op jit(solution)/shard_map/ppermute | solution.py:776
  104.3 7.8 %collective-permute-start.18 = (bf16[192,512]{1,0:T(8,128)(2,1)S(1)}, bf16[192,512]{1,0:T(8,128)(2,1)S(1)}, u32[]{:S(2)}, u32[]{:S(2)}) collective-permute-start(bf16[192,512]{1,0:T(8,128)(2,1)S(1)} %get-tuple-element.190), channel_id=1, source_target_pairs={{0,16},{1,17},{2,18},{3,19},{4,20},{5,21},{6,22},{7,23},{8,24},{9,... | collective-permute-start | bytes 589832 | tf_op jit(solution)/shard_map/ppermute | solution.py:776
  105.5 8.7 %collective-permute-start.29 = (bf16[80,512]{1,0:T(8,128)(2,1)S(1)}, bf16[80,512]{1,0:T(8,128)(2,1)S(1)}, u32[]{:S(2)}, u32[]{:S(2)}) collective-permute-start(bf16[80,512]{1,0:T(8,128)(2,1)S(1)} %add_convert_fusion.8), channel_id=1, source_target_pairs={{0,3},{1,2},{2,1},{3,0},{4,7},{5,6},{6,5},{7,4},{8,11},{9,10},{10,... | collective-permute-start | bytes 245768 | tf_op jit(solution)/shard_map/ppermute | solution.py:776
  109.9 7.3 %collective-permute-start.27 = (bf16[80,512]{1,0:T(8,128)(2,1)S(1)}, bf16[80,512]{1,0:T(8,128)(2,1)S(1)}, u32[]{:S(2)}, u32[]{:S(2)}) collective-permute-start(bf16[80,512]{1,0:T(8,128)(2,1)S(1)} %add_convert_fusion.8), channel_id=1, source_target_pairs={{0,2},{1,3},{2,0},{3,1},{4,6},{5,7},{6,4},{7,5},{8,10},{9,11},{10,... | collective-permute-start | bytes 245768 | tf_op jit(solution)/shard_map/ppermute | solution.py:776
  119.5 11.0 %collective-permute-start.32 = (bf16[56,512]{1,0:T(8,128)(2,1)S(1)}, bf16[56,512]{1,0:T(8,128)(2,1)S(1)}, u32[]{:S(2)}, u32[]{:S(2)}) collective-permute-start(bf16[56,512]{1,0:T(8,128)(2,1)S(1)} %pad_maximum_fusion), channel_id=1, source_target_pairs={{0,3},{1,2},{2,1},{3,0},{4,7},{5,6},{6,5},{7,4},{8,11},{9,10},{10,... | collective-permute-start | bytes 172040 | tf_op jit(solution)/shard_map/ppermute | solution.py:776
  123.2 7.9 %collective-permute-start.31 = (bf16[56,512]{1,0:T(8,128)(2,1)S(1)}, bf16[56,512]{1,0:T(8,128)(2,1)S(1)}, u32[]{:S(2)}, u32[]{:S(2)}) collective-permute-start(bf16[56,512]{1,0:T(8,128)(2,1)S(1)} %pad_maximum_fusion), channel_id=1, source_target_pairs={{0,1},{1,0},{2,3},{3,2},{4,5},{5,4},{6,7},{7,6},{8,9},{9,8},{10,11... | collective-permute-start | bytes 172040 | tf_op jit(solution)/shard_map/ppermute | solution.py:776
  123.2 7.9 %collective-permute-start.30 = (bf16[56,512]{1,0:T(8,128)(2,1)S(1)}, bf16[56,512]{1,0:T(8,128)(2,1)S(1)}, u32[]{:S(2)}, u32[]{:S(2)}) collective-permute-start(bf16[56,512]{1,0:T(8,128)(2,1)S(1)} %pad_maximum_fusion), channel_id=1, source_target_pairs={{0,2},{1,3},{2,0},{3,1},{4,6},{5,7},{6,4},{7,5},{8,10},{9,11},{10,... | collective-permute-start | bytes 172040 | tf_op jit(solution)/shard_map/ppermute | solution.py:776
  123.9 11.5 %collective-permute-start.39 = (bf16[320,512]{1,0:T(8,128)(2,1)S(1)}, bf16[320,512]{1,0:T(8,128)(2,1)S(1)}, u32[]{:S(2)}, u32[]{:S(2)}) collective-permute-start(bf16[320,512]{1,0:T(8,128)(2,1)S(1)} %constant_dynamic-update-slice_fusion.16), channel_id=1, source_target_pairs={{0,24},{1,25},{2,26},{3,27},{4,28},{5,29},{6,30},{7,31},{8,16},{9,... | collective-permute-start | bytes 983048 | tf_op jit(solution)/shard_map/ppermute | solution.py:776
  126.3 13.2 %collective-permute-start.38 = (bf16[320,512]{1,0:T(8,128)(2,1)S(1)}, bf16[320,512]{1,0:T(8,128)(2,1)S(1)}, u32[]{:S(2)}, u32[]{:S(2)}) collective-permute-start(bf16[320,512]{1,0:T(8,128)(2,1)S(1)} %constant_dynamic-update-slice_fusion.16), channel_id=1, source_target_pairs={{0,8},{1,9},{2,10},{3,11},{4,12},{5,13},{6,14},{7,15},{8,0},{9,1},... | collective-permute-start | bytes 983048 | tf_op jit(solution)/shard_map/ppermute | solution.py:776
  130.5 9.6 %collective-permute-start.37 = (bf16[320,512]{1,0:T(8,128)(2,1)S(1)}, bf16[320,512]{1,0:T(8,128)(2,1)S(1)}, u32[]{:S(2)}, u32[]{:S(2)}) collective-permute-start(bf16[320,512]{1,0:T(8,128)(2,1)S(1)} %constant_dynamic-update-slice_fusion.16), channel_id=1, source_target_pairs={{0,16},{1,17},{2,18},{3,19},{4,20},{5,21},{6,22},{7,23},{8,24},{9,... | collective-permute-start | bytes 983048 | tf_op jit(solution)/shard_map/ppermute | solution.py:776
  140.2 9.5 %collective-permute-start.36 = (bf16[224,512]{1,0:T(8,128)(2,1)S(1)}, bf16[224,512]{1,0:T(8,128)(2,1)S(1)}, u32[]{:S(2)}, u32[]{:S(2)}) collective-permute-start(bf16[224,512]{1,0:T(8,128)(2,1)S(1)} %constant_dynamic-update-slice_fusion.20), channel_id=1, source_target_pairs={{0,24},{1,25},{2,26},{3,27},{4,28},{5,29},{6,30},{7,31},{8,16},{9,... | collective-permute-start | bytes 688136 | tf_op jit(solution)/shard_map/ppermute | solution.py:776
  142.4 11.3 %collective-permute-start.35 = (bf16[224,512]{1,0:T(8,128)(2,1)S(1)}, bf16[224,512]{1,0:T(8,128)(2,1)S(1)}, u32[]{:S(2)}, u32[]{:S(2)}) collective-permute-start(bf16[224,512]{1,0:T(8,128)(2,1)S(1)} %constant_dynamic-update-slice_fusion.20), channel_id=1, source_target_pairs={{0,8},{1,9},{2,10},{3,11},{4,12},{5,13},{6,14},{7,15},{8,0},{9,1},... | collective-permute-start | bytes 688136 | tf_op jit(solution)/shard_map/ppermute | solution.py:776
  142.8 11.3 %collective-permute-start.34 = (bf16[224,512]{1,0:T(8,128)(2,1)S(1)}, bf16[224,512]{1,0:T(8,128)(2,1)S(1)}, u32[]{:S(2)}, u32[]{:S(2)}) collective-permute-start(bf16[224,512]{1,0:T(8,128)(2,1)S(1)} %constant_dynamic-update-slice_fusion.20), channel_id=1, source_target_pairs={{0,16},{1,17},{2,18},{3,19},{4,20},{5,21},{6,22},{7,23},{8,24},{9,... | collective-permute-start | bytes 688136 | tf_op jit(solution)/shard_map/ppermute | solution.py:776
  (41 other events, 402.1 us)

commit v6 on v5

--- a/solution.py
+++ b/solution.py
@@ -897,7 +897,7 @@
     qkv.step(big_all.pieces[0])
     qkv_all = Gather(jnp.concatenate([qkv.rest(), small], axis=0), groups, total)
     qkv_all.step()
-    grad_ffn_out = ffn_out_grad(where, *acts.rest(), after(dm_low, qkv_all.pieces[0]), masks)
+    grad_ffn_out = ffn_out_grad(where, *acts.rest(), after(dm_low, *qkv_all.pieces), masks)
     qkv_all.step(grad_ffn_out)
     big_all.step(qkv_all.pieces[0])
     win, wo = unpack_big(where, *big_all.rest(), inner, width, masks)

time: 159 us -> 159 us (level)
  transfers between devices with their start and end apart: 42 -> 42, of which waited for: 24 -> 23; matrix products, arithmetic and copies ran while one was open for 1% -> 1% of each run, Pallas kernels for 16% -> 16%
where the time goes in v6:
time: 159 us; the launch traced here: 158 us
  Pallas kernels  64.3 us (40%)
  starting transfers between devices  52.4 us (33%)
  waiting for transfers between devices  34.7 us (22%)
  local copies, waits for them, and re-layouts  4.65 us (3%)
    ppermute x42, starting transfers between devices, swap(): return lax.ppermute(values, AXES, [(i, i ^ mask) for i in range(total)])  52.4 us
    ppermute x42, waiting for transfers between devices, swap(): return lax.ppermute(values, AXES, [(i, i ^ mask) for i in range(total)])  34.7 us
    pallas_call x1, Pallas kernels, forward(): pl.pallas_call(forward_kernel, name='forward_rows', grid=(rows,), in_spec...  21 us
    pallas_call x2, Pallas kernels, attn_back(): pl.pallas_call(functools.partial(attn_back_kernel, group=group, masks=mas...  14.7 us
    pallas_call x1, Pallas kernels, ffn_back(): pl.pallas_call(functools.partial(ffn_back_kernel, masks=masks), name='ffn...  13.6 us
    unnamed x70, local copies, waits for them, and re-layouts  4.56 us
    pallas_call x1, Pallas kernels, finish(): pl.pallas_call(functools.partial(finish_kernel, groups=groups), name='fin...  3.84 us
    pallas_call x1, Pallas kernels, ffn_out_grad(): pl.pallas_call(functools.partial(ffn_out_kernel, masks=masks), name='ffn_...  3.65 us
  transfers between devices with their start and end apart: 42, of which 23 were waited for; matrix products, arithmetic and copies ran while one was open for 1% of the time, Pallas kernels for 16%

profile of v6, /device:TPU:0, one launch (start us, length us, event | category | flops | bytes accessed | tf_op | source)
XLA Modules:
  0.0 158.2 jit_solution(8679376953768993438)
XLA Ops:
  0.7 21.0 %forward_rows.1 = (bf16[2,512,512]{2,1,0:T(8,128)(2,1)}, bf16[2,512,512]{2,1,0:T(8,128)(2,1)}, bf16[2,512,512]{2,1,0:T(8,128)(2,1)}, bf16[2,512,512]{2,1,0:T(8,1...) custom-call(s32[2,512]{1,0:T(2,128)} %seg_ref.3, ...), custom_call_target="tpu_custom_call" | custom-call | tf_op jit(solution)/shard_map/forward_rows/pallas_call | solution.py:219
  21.7 5.2 %collective-permute-start.2 = (bf16[16,512]{1,0:T(8,128)(2,1)}, bf16[16,512]{1,0:T(8,128)(2,1)S(1)}, u32[]{:S(2)}, u32[]{:S(2)}) collective-permute-start(bf16[16,512]{1,0:T(8,128)(2,1)} %get-tuple-element.99), channel_id=1, source_target_pairs={{0,3},{1,2},{2,1},{3,0},{4,7},{5,6},{6,5},{7,4},{8,11},{9,10},{10,... | collective-permute-start | bytes 49160 | tf_op jit(solution)/shard_map/ppermute | solution.py:776
  27.5 3.7 %collective-permute-start.8 = (bf16[16,2048]{1,0:T(8,128)(2,1)}, bf16[16,2048]{1,0:T(8,128)(2,1)S(1)}, u32[]{:S(2)}, u32[]{:S(2)}) collective-permute-start(bf16[16,2048]{1,0:T(8,128)(2,1)} %get-tuple-element.122), channel_id=1, source_target_pairs={{0,3},{1,2},{2,1},{3,0},{4,7},{5,6},{6,5},{7,4},{8,11},{9,10},{10,... | collective-permute-start | bytes 196616 | tf_op jit(solution)/shard_map/ppermute | solution.py:776
  33.0 2.5 %collective-permute-start.5 = (bf16[64,512]{1,0:T(8,128)(2,1)S(1)}, bf16[64,512]{1,0:T(8,128)(2,1)S(1)}, u32[]{:S(2)}, u32[]{:S(2)}) collective-permute-start(bf16[64,512]{1,0:T(8,128)(2,1)S(1)} %constant_dynamic-update-slice_fusion), channel_id=1, source_target_pairs={{0,24},{1,25},{2,26},{3,27},{4,28},{5,29},{6,30},{7,31},{8,16},{9,... | collective-permute-start | bytes 196616 | tf_op jit(solution)/shard_map/ppermute | solution.py:776
  42.0 2.7 %contrast_all.1 = (f32[1,1]{1,0:T(1,128)}, f32[512,512]{1,0:T(8,128)}, f32[16,512]{1,0:T(8,128)S(1)}, bf16[512,512]{1,0:T(8,128)(2,1)S(1)}) custom-call(s32[1]{0:T(128)} %bitcast.where_ref.refs_0_, bf16[256,512]{1,0:T(8,128)(2,1)S(1)} %constant_dynamic-update-slice_fusion.4.near_ref, bf16[256,512]{1,0:T(8,128)(2,1)S(1)} %collective-permute-done.9.far_ref, ...), custom_call_target="tpu_custom_call" | custom-call | tf_op jit(solution)/shard_map/contrast_all/pallas_call | solution.py:334
  47.0 13.6 %ffn_back.1 = (f32[2,512,512]{2,1,0:T(8,128)S(1)}, bf16[2,512,512]{2,1,0:T(8,128)(2,1)S(1)}, bf16[1280,512]{1,0:T(8,128)(2,1)S(1)}, bf16[1280,512]{1,0:T(8,128)(2,1)}, f32[1,512]{1,0:T(1,128)S(1)}) custom-call(s32[1]{0:T(128)} %bitcast.where_ref.refs_0_, s32[2,512]{1,0:T(2,128)S(1)} %copy-done.18, f32[16,512]{1,0:T(8,128)S(1)} %get-tuple-element.109.dm_ref, ...), custom_call_target="tpu_custom_call" | custom-call | tf_op jit(solution)/shard_map/ffn_back/pallas_call | solution.py:435
  65.6 7.2 %attn_back_0.1 = (bf16[2,3,512,256]{3,2,1,0:T(8,128)(2,1)S(1)}, f32[4,768]{1,0:T(4,128)S(1)}, bf16[1536,256]{1,0:T(8,128)(2,1)S(1)}) custom-call(s32[1]{0:T(128)} %bitcast.where_ref.refs_0_, bf16[2,512,512]{2,1,0:T(8,128)(2,1)S(1)} %copy-done.2, bf16[2,512,512]{2,1,0:T(8,128)(2,1)S(1)} %copy-done.3, bf16[2,512,512]{2,1,0:T(8,128)(2,1)S(1)} %copy-done.4, ...), custom_call_target="tpu_custom_call" | custom-call | tf_op jit(solution)/shard_map/attn_back_0/pallas_call | solution.py:578
  72.9 2.2 %collective-permute-done.12 = bf16[64,2048]{1,0:T(8,128)(2,1)S(1)} collective-permute-done((bf16[64,2048]{1,0:T(8,128)(2,1)S(1)}, bf16[64,2048]{1,0:T(8,128)(2,1)S(1)}, u32[]{:S(2)}, u32[]{:S(2)}) %collective-permute-start.12) | collective-permute-done | bytes 262176 | tf_op jit(solution)/shard_map/ppermute | solution.py:776
  80.2 7.5 %attn_back_1.1 = (bf16[2,3,512,256]{3,2,1,0:T(8,128)(2,1)S(1)}, f32[4,768]{1,0:T(4,128)S(1)}, bf16[768,512]{1,0:T(8,128)(2,1)S(1)}, bf16[768,512]{1,0:T(8,128)(2,1)S(1)}) custom-call(s32[1]{0:T(128)} %bitcast.where_ref.refs_0_, bf16[2,512,512]{2,1,0:T(8,128)(2,1)S(1)} %copy-done.2, bf16[2,512,512]{2,1,0:T(8,128)(2,1)S(1)} %copy-done.3, ...), custom_call_target="tpu_custom_call" | custom-call | tf_op jit(solution)/shard_map/attn_back_1/pallas_call | solution.py:578
  87.8 3.8 %finish_rows.1 = (bf16[2,512,512]{2,1,0:T(8,128)(2,1)}, bf16[8,512]{1,0:T(8,128)(2,1)S(1)}) custom-call(bf16[2,512,512]{2,1,0:T(8,128)(2,1)S(1)} %copy-done.8, f32[2,512,512]{2,1,0:T(8,128)S(1)} %copy-done.14, bf16[512]{0:T(512)(128)(2,1)S(1)} %copy-done.20, f32[1,512]{1,0:T(1,128)S(1)} %get-tuple-element.115.refs_3_, bf16[768,32]{1,0:T(8,128)(2,1)S(1)} %copy-done.17, ...), custom_call_target="tpu_custom_call" | custom-call | tf_op jit(solution)/shard_map/finish_rows/pallas_call | solution.py:653
  94.9 3.3 %collective-permute-start.23 = (bf16[80,512]{1,0:T(8,128)(2,1)S(1)}, bf16[80,512]{1,0:T(8,128)(2,1)S(1)}, u32[]{:S(2)}, u32[]{:S(2)}) collective-permute-start(bf16[80,512]{1,0:T(8,128)(2,1)S(1)} %get-tuple-element.192), channel_id=1, source_target_pairs={{0,3},{1,2},{2,1},{3,0},{4,7},{5,6},{6,5},{7,4},{8,11},{9,10},{10,... | collective-permute-start | bytes 245768 | tf_op jit(solution)/shard_map/ppermute | solution.py:776
  105.5 2.5 %collective-permute-start.29 = (bf16[80,512]{1,0:T(8,128)(2,1)S(1)}, bf16[80,512]{1,0:T(8,128)(2,1)S(1)}, u32[]{:S(2)}, u32[]{:S(2)}) collective-permute-start(bf16[80,512]{1,0:T(8,128)(2,1)S(1)} %add_convert_fusion.8), channel_id=1, source_target_pairs={{0,3},{1,2},{2,1},{3,0},{4,7},{5,6},{6,5},{7,4},{8,11},{9,10},{10,... | collective-permute-start | bytes 245768 | tf_op jit(solution)/shard_map/ppermute | solution.py:776
  109.9 2.2 %collective-permute-start.27 = (bf16[80,512]{1,0:T(8,128)(2,1)S(1)}, bf16[80,512]{1,0:T(8,128)(2,1)S(1)}, u32[]{:S(2)}, u32[]{:S(2)}) collective-permute-start(bf16[80,512]{1,0:T(8,128)(2,1)S(1)} %add_convert_fusion.8), channel_id=1, source_target_pairs={{0,2},{1,3},{2,0},{3,1},{4,6},{5,7},{6,4},{7,5},{8,10},{9,11},{10,... | collective-permute-start | bytes 245768 | tf_op jit(solution)/shard_map/ppermute | solution.py:776
  114.2 2.5 %collective-permute-start.24 = (bf16[48,512]{1,0:T(8,128)(2,1)S(1)}, bf16[48,512]{1,0:T(8,128)(2,1)S(1)}, u32[]{:S(2)}, u32[]{:S(2)}) collective-permute-start(bf16[48,512]{1,0:T(8,128)(2,1)S(1)} %get-tuple-element.199), channel_id=1, source_target_pairs={{0,2},{1,3},{2,0},{3,1},{4,6},{5,7},{6,4},{7,5},{8,10},{9,11},{10,... | collective-permute-start | bytes 147464 | tf_op jit(solution)/shard_map/ppermute | solution.py:776
  119.5 3.7 %collective-permute-start.32 = (bf16[56,512]{1,0:T(8,128)(2,1)S(1)}, bf16[56,512]{1,0:T(8,128)(2,1)S(1)}, u32[]{:S(2)}, u32[]{:S(2)}) collective-permute-start(bf16[56,512]{1,0:T(8,128)(2,1)S(1)} %pad_maximum_fusion), channel_id=1, source_target_pairs={{0,3},{1,2},{2,1},{3,0},{4,7},{5,6},{6,5},{7,4},{8,11},{9,10},{10,... | collective-permute-start | bytes 172040 | tf_op jit(solution)/shard_map/ppermute | solution.py:776
  123.9 2.4 %collective-permute-start.39 = (bf16[320,512]{1,0:T(8,128)(2,1)S(1)}, bf16[320,512]{1,0:T(8,128)(2,1)S(1)}, u32[]{:S(2)}, u32[]{:S(2)}) collective-permute-start(bf16[320,512]{1,0:T(8,128)(2,1)S(1)} %constant_dynamic-update-slice_fusion.16), channel_id=1, source_target_pairs={{0,24},{1,25},{2,26},{3,27},{4,28},{5,29},{6,30},{7,31},{8,16},{9,... | collective-permute-start | bytes 983048 | tf_op jit(solution)/shard_map/ppermute | solution.py:776
  128.6 3.6 %ffn_out_grad.1 = f32[2048,512]{1,0:T(8,128)} custom-call(s32[1]{0:T(128)} %bitcast.where_ref.refs_0_, bf16[256,2048]{1,0:T(8,128)(2,1)S(1)} %constant_dynamic-update-slice_fusion.12.near_ref, bf16[256,2048]{1,0:T(8,128)(2,1)S(1)} %collective-permute-done.33.far_ref, bf16[512,512]{1,0:T(8,128)(2,1)S(1)} %get-tuple-element.162.dm_ref), custom_call_target="tpu_custom_call" | custom-call | tf_op jit(solution)/shard_map/ffn_out_grad/pallas_call | solution.py:363
  132.3 3.2 %collective-permute-done.39 = bf16[320,512]{1,0:T(8,128)(2,1)S(1)} collective-permute-done((bf16[320,512]{1,0:T(8,128)(2,1)S(1)}, bf16[320,512]{1,0:T(8,128)(2,1)S(1)}, u32[]{:S(2)}, u32[]{:S(2)}) %collective-permute-start.39) | collective-permute-done | bytes 327712 | tf_op jit(solution)/shard_map/ppermute | solution.py:776
  135.4 4.1 %collective-permute-done.38 = bf16[320,512]{1,0:T(8,128)(2,1)S(1)} collective-permute-done((bf16[320,512]{1,0:T(8,128)(2,1)S(1)}, bf16[320,512]{1,0:T(8,128)(2,1)S(1)}, u32[]{:S(2)}, u32[]{:S(2)}) %collective-permute-start.38) | collective-permute-done | bytes 327712 | tf_op jit(solution)/shard_map/ppermute | solution.py:776
  139.8 2.4 %collective-permute-start.36 = (bf16[224,512]{1,0:T(8,128)(2,1)S(1)}, bf16[224,512]{1,0:T(8,128)(2,1)S(1)}, u32[]{:S(2)}, u32[]{:S(2)}) collective-permute-start(bf16[224,512]{1,0:T(8,128)(2,1)S(1)} %constant_dynamic-update-slice_fusion.20), channel_id=1, source_target_pairs={{0,24},{1,25},{2,26},{3,27},{4,28},{5,29},{6,30},{7,31},{8,16},{9,... | collective-permute-start | bytes 688136 | tf_op jit(solution)/shard_map/ppermute | solution.py:776
  143.3 3.0 %unpack_ffn.1 = (f32[512,2048]{1,0:T(8,128)}, f32[512,512]{1,0:T(8,128)}) custom-call(s32[1]{0:T(128)} %bitcast.where_ref.refs_0_, bf16[1280,512]{1,0:T(8,128)(2,1)S(1)} %constant_dynamic-update-slice_fusion.24.near_ref, bf16[1280,512]{1,0:T(8,128)(2,1)S(1)} %collective-permute-done.40.far_ref), custom_call_target="tpu_custom_call" | custom-call | tf_op jit(solution)/shard_map/unpack_ffn/pallas_call | solution.py:702
  146.3 3.0 %collective-permute-done.36 = bf16[224,512]{1,0:T(8,128)(2,1)S(1)} collective-permute-done((bf16[224,512]{1,0:T(8,128)(2,1)S(1)}, bf16[224,512]{1,0:T(8,128)(2,1)S(1)}, u32[]{:S(2)}, u32[]{:S(2)}) %collective-permute-start.36) | collective-permute-done | bytes 229408 | tf_op jit(solution)/shard_map/ppermute | solution.py:776
  149.2 4.3 %collective-permute-done.35 = bf16[224,512]{1,0:T(8,128)(2,1)S(1)} collective-permute-done((bf16[224,512]{1,0:T(8,128)(2,1)S(1)}, bf16[224,512]{1,0:T(8,128)(2,1)S(1)}, u32[]{:S(2)}, u32[]{:S(2)}) %collective-permute-start.35) | collective-permute-done | bytes 229408 | tf_op jit(solution)/shard_map/ppermute | solution.py:776
  153.8 2.5 %collective-permute-done.41.far_ref = bf16[896,512]{1,0:T(8,128)(2,1)S(1)} collective-permute-done((bf16[896,512]{1,0:T(8,128)(2,1)S(1)}, bf16[896,512]{1,0:T(8,128)(2,1)S(1)}, u32[]{:S(2)}, u32[]{:S(2)}) %collective-permute-start.41) | collective-permute-done | bytes 917536 | tf_op jit(solution)/shard_map/ppermute | solution.py:776
  (154 shorter events, 45.1 us)
Async XLA Ops:
  21.7 9.6 %collective-permute-start.2 = (bf16[16,512]{1,0:T(8,128)(2,1)}, bf16[16,512]{1,0:T(8,128)(2,1)S(1)}, u32[]{:S(2)}, u32[]{:S(2)}) collective-permute-start(bf16[16,512]{1,0:T(8,128)(2,1)} %get-tuple-element.99), channel_id=1, source_target_pairs={{0,3},{1,2},{2,1},{3,0},{4,7},{5,6},{6,5},{7,4},{8,11},{9,10},{10,... | collective-permute-start | bytes 49160 | tf_op jit(solution)/shard_map/ppermute | solution.py:776
  27.5 8.6 %collective-permute-start.8 = (bf16[16,2048]{1,0:T(8,128)(2,1)}, bf16[16,2048]{1,0:T(8,128)(2,1)S(1)}, u32[]{:S(2)}, u32[]{:S(2)}) collective-permute-start(bf16[16,2048]{1,0:T(8,128)(2,1)} %get-tuple-element.122), channel_id=1, source_target_pairs={{0,3},{1,2},{2,1},{3,0},{4,7},{5,6},{6,5},{7,4},{8,11},{9,10},{10,... | collective-permute-start | bytes 196616 | tf_op jit(solution)/shard_map/ppermute | solution.py:776
  60.6 15.5 %collective-permute-start.10 = (bf16[1280,512]{1,0:T(8,128)(2,1)}, bf16[1280,512]{1,0:T(8,128)(2,1)S(1)}, u32[]{:S(2)}, u32[]{:S(2)}) collective-permute-start(bf16[1280,512]{1,0:T(8,128)(2,1)} %get-tuple-element.129), channel_id=1, source_target_pairs={{0,4},{1,5},{2,6},{3,7},{4,0},{5,1},{6,2},{7,3},{8,12},{9,13},{10,... | collective-permute-start | bytes 3932168 | tf_op jit(solution)/shard_map/ppermute | solution.py:776
  60.8 12.0 %collective-permute-start.13 = (bf16[64,2048]{1,0:T(8,128)(2,1)S(1)}, bf16[64,2048]{1,0:T(8,128)(2,1)S(1)}, u32[]{:S(2)}, u32[]{:S(2)}) collective-permute-start(bf16[64,2048]{1,0:T(8,128)(2,1)S(1)} %constant_dynamic-update-slice_fusion.8), channel_id=1, source_target_pairs={{0,24},{1,25},{2,26},{3,27},{4,28},{5,29},{6,30},{7,31},{8,16},{9,... | collective-permute-start | bytes 786440 | tf_op jit(solution)/shard_map/ppermute | solution.py:776
  62.3 12.8 %collective-permute-start.12 = (bf16[64,2048]{1,0:T(8,128)(2,1)S(1)}, bf16[64,2048]{1,0:T(8,128)(2,1)S(1)}, u32[]{:S(2)}, u32[]{:S(2)}) collective-permute-start(bf16[64,2048]{1,0:T(8,128)(2,1)S(1)} %constant_dynamic-update-slice_fusion.8), channel_id=1, source_target_pairs={{0,8},{1,9},{2,10},{3,11},{4,12},{5,13},{6,14},{7,15},{8,0},{9,1},... | collective-permute-start | bytes 786440 | tf_op jit(solution)/shard_map/ppermute | solution.py:776
  62.8 13.1 %collective-permute-start.11 = (bf16[64,2048]{1,0:T(8,128)(2,1)S(1)}, bf16[64,2048]{1,0:T(8,128)(2,1)S(1)}, u32[]{:S(2)}, u32[]{:S(2)}) collective-permute-start(bf16[64,2048]{1,0:T(8,128)(2,1)S(1)} %constant_dynamic-update-slice_fusion.8), channel_id=1, source_target_pairs={{0,16},{1,17},{2,18},{3,19},{4,20},{5,21},{6,22},{7,23},{8,24},{9,... | collective-permute-start | bytes 786440 | tf_op jit(solution)/shard_map/ppermute | solution.py:776
  76.5 15.1 %collective-permute-start.16 = (bf16[320,512]{1,0:T(8,128)(2,1)S(1)}, bf16[320,512]{1,0:T(8,128)(2,1)S(1)}, u32[]{:S(2)}, u32[]{:S(2)}) collective-permute-start(bf16[320,512]{1,0:T(8,128)(2,1)S(1)} %get-tuple-element.184), channel_id=1, source_target_pairs={{0,24},{1,25},{2,26},{3,27},{4,28},{5,29},{6,30},{7,31},{8,16},{9,... | collective-permute-start | bytes 983048 | tf_op jit(solution)/shard_map/ppermute | solution.py:776
  78.1 15.1 %collective-permute-start.15 = (bf16[320,512]{1,0:T(8,128)(2,1)S(1)}, bf16[320,512]{1,0:T(8,128)(2,1)S(1)}, u32[]{:S(2)}, u32[]{:S(2)}) collective-permute-start(bf16[320,512]{1,0:T(8,128)(2,1)S(1)} %get-tuple-element.185), channel_id=1, source_target_pairs={{0,8},{1,9},{2,10},{3,11},{4,12},{5,13},{6,14},{7,15},{8,0},{9,1},... | collective-permute-start | bytes 983048 | tf_op jit(solution)/shard_map/ppermute | solution.py:776
  78.6 15.5 %collective-permute-start.14 = (bf16[320,512]{1,0:T(8,128)(2,1)S(1)}, bf16[320,512]{1,0:T(8,128)(2,1)S(1)}, u32[]{:S(2)}, u32[]{:S(2)}) collective-permute-start(bf16[320,512]{1,0:T(8,128)(2,1)S(1)} %get-tuple-element.186), channel_id=1, source_target_pairs={{0,16},{1,17},{2,18},{3,19},{4,20},{5,21},{6,22},{7,23},{8,24},{9,... | collective-permute-start | bytes 983048 | tf_op jit(solution)/shard_map/ppermute | solution.py:776
  94.4 34.2 %collective-permute-start.33 = (bf16[256,2048]{1,0:T(8,128)(2,1)S(1)}, bf16[256,2048]{1,0:T(8,128)(2,1)S(1)}, u32[]{:S(2)}, u32[]{:S(2)}) collective-permute-start(bf16[256,2048]{1,0:T(8,128)(2,1)S(1)} %constant_dynamic-update-slice_fusion.12.near_ref), channel_id=1, source_target_pairs={{0,4},{1,5},{2,6},{3,7},{4,0},{5,1},{6,2},{7,3},{8,12},{9,13},{10,... | collective-permute-start | bytes 3145736 | tf_op jit(solution)/shard_map/ppermute | solution.py:776
  94.9 7.1 %collective-permute-start.23 = (bf16[80,512]{1,0:T(8,128)(2,1)S(1)}, bf16[80,512]{1,0:T(8,128)(2,1)S(1)}, u32[]{:S(2)}, u32[]{:S(2)}) collective-permute-start(bf16[80,512]{1,0:T(8,128)(2,1)S(1)} %get-tuple-element.192), channel_id=1, source_target_pairs={{0,3},{1,2},{2,1},{3,0},{4,7},{5,6},{6,5},{7,4},{8,11},{9,10},{10,... | collective-permute-start | bytes 245768 | tf_op jit(solution)/shard_map/ppermute | solution.py:776
  98.1 7.3 %collective-permute-start.21 = (bf16[80,512]{1,0:T(8,128)(2,1)S(1)}, bf16[80,512]{1,0:T(8,128)(2,1)S(1)}, u32[]{:S(2)}, u32[]{:S(2)}) collective-permute-start(bf16[80,512]{1,0:T(8,128)(2,1)S(1)} %get-tuple-element.194), channel_id=1, source_target_pairs={{0,2},{1,3},{2,0},{3,1},{4,6},{5,7},{6,4},{7,5},{8,10},{9,11},{10,... | collective-permute-start | bytes 245768 | tf_op jit(solution)/shard_map/ppermute | solution.py:776
  99.5 8.7 %collective-permute-start.20 = (bf16[192,512]{1,0:T(8,128)(2,1)S(1)}, bf16[192,512]{1,0:T(8,128)(2,1)S(1)}, u32[]{:S(2)}, u32[]{:S(2)}) collective-permute-start(bf16[192,512]{1,0:T(8,128)(2,1)S(1)} %get-tuple-element.188), channel_id=1, source_target_pairs={{0,24},{1,25},{2,26},{3,27},{4,28},{5,29},{6,30},{7,31},{8,16},{9,... | collective-permute-start | bytes 589832 | tf_op jit(solution)/shard_map/ppermute | solution.py:776
  102.0 7.9 %collective-permute-start.19 = (bf16[192,512]{1,0:T(8,128)(2,1)S(1)}, bf16[192,512]{1,0:T(8,128)(2,1)S(1)}, u32[]{:S(2)}, u32[]{:S(2)}) collective-permute-start(bf16[192,512]{1,0:T(8,128)(2,1)S(1)} %get-tuple-element.189), channel_id=1, source_target_pairs={{0,8},{1,9},{2,10},{3,11},{4,12},{5,13},{6,14},{7,15},{8,0},{9,1},... | collective-permute-start | bytes 589832 | tf_op jit(solution)/shard_map/ppermute | solution.py:776
  104.3 7.8 %collective-permute-start.18 = (bf16[192,512]{1,0:T(8,128)(2,1)S(1)}, bf16[192,512]{1,0:T(8,128)(2,1)S(1)}, u32[]{:S(2)}, u32[]{:S(2)}) collective-permute-start(bf16[192,512]{1,0:T(8,128)(2,1)S(1)} %get-tuple-element.190), channel_id=1, source_target_pairs={{0,16},{1,17},{2,18},{3,19},{4,20},{5,21},{6,22},{7,23},{8,24},{9,... | collective-permute-start | bytes 589832 | tf_op jit(solution)/shard_map/ppermute | solution.py:776
  105.5 8.7 %collective-permute-start.29 = (bf16[80,512]{1,0:T(8,128)(2,1)S(1)}, bf16[80,512]{1,0:T(8,128)(2,1)S(1)}, u32[]{:S(2)}, u32[]{:S(2)}) collective-permute-start(bf16[80,512]{1,0:T(8,128)(2,1)S(1)} %add_convert_fusion.8), channel_id=1, source_target_pairs={{0,3},{1,2},{2,1},{3,0},{4,7},{5,6},{6,5},{7,4},{8,11},{9,10},{10,... | collective-permute-start | bytes 245768 | tf_op jit(solution)/shard_map/ppermute | solution.py:776
  109.9 7.3 %collective-permute-start.27 = (bf16[80,512]{1,0:T(8,128)(2,1)S(1)}, bf16[80,512]{1,0:T(8,128)(2,1)S(1)}, u32[]{:S(2)}, u32[]{:S(2)}) collective-permute-start(bf16[80,512]{1,0:T(8,128)(2,1)S(1)} %add_convert_fusion.8), channel_id=1, source_target_pairs={{0,2},{1,3},{2,0},{3,1},{4,6},{5,7},{6,4},{7,5},{8,10},{9,11},{10,... | collective-permute-start | bytes 245768 | tf_op jit(solution)/shard_map/ppermute | solution.py:776
  119.5 6.8 %collective-permute-start.32 = (bf16[56,512]{1,0:T(8,128)(2,1)S(1)}, bf16[56,512]{1,0:T(8,128)(2,1)S(1)}, u32[]{:S(2)}, u32[]{:S(2)}) collective-permute-start(bf16[56,512]{1,0:T(8,128)(2,1)S(1)} %pad_maximum_fusion), channel_id=1, source_target_pairs={{0,3},{1,2},{2,1},{3,0},{4,7},{5,6},{6,5},{7,4},{8,11},{9,10},{10,... | collective-permute-start | bytes 172040 | tf_op jit(solution)/shard_map/ppermute | solution.py:776
  123.9 11.5 %collective-permute-start.39 = (bf16[320,512]{1,0:T(8,128)(2,1)S(1)}, bf16[320,512]{1,0:T(8,128)(2,1)S(1)}, u32[]{:S(2)}, u32[]{:S(2)}) collective-permute-start(bf16[320,512]{1,0:T(8,128)(2,1)S(1)} %constant_dynamic-update-slice_fusion.16), channel_id=1, source_target_pairs={{0,24},{1,25},{2,26},{3,27},{4,28},{5,29},{6,30},{7,31},{8,16},{9,... | collective-permute-start | bytes 983048 | tf_op jit(solution)/shard_map/ppermute | solution.py:776
  126.3 13.3 %collective-permute-start.38 = (bf16[320,512]{1,0:T(8,128)(2,1)S(1)}, bf16[320,512]{1,0:T(8,128)(2,1)S(1)}, u32[]{:S(2)}, u32[]{:S(2)}) collective-permute-start(bf16[320,512]{1,0:T(8,128)(2,1)S(1)} %constant_dynamic-update-slice_fusion.16), channel_id=1, source_target_pairs={{0,8},{1,9},{2,10},{3,11},{4,12},{5,13},{6,14},{7,15},{8,0},{9,1},... | collective-permute-start | bytes 983048 | tf_op jit(solution)/shard_map/ppermute | solution.py:776
  127.4 12.2 %collective-permute-start.37 = (bf16[320,512]{1,0:T(8,128)(2,1)S(1)}, bf16[320,512]{1,0:T(8,128)(2,1)S(1)}, u32[]{:S(2)}, u32[]{:S(2)}) collective-permute-start(bf16[320,512]{1,0:T(8,128)(2,1)S(1)} %constant_dynamic-update-slice_fusion.16), channel_id=1, source_target_pairs={{0,16},{1,17},{2,18},{3,19},{4,20},{5,21},{6,22},{7,23},{8,24},{9,... | collective-permute-start | bytes 983048 | tf_op jit(solution)/shard_map/ppermute | solution.py:776
  139.8 9.5 %collective-permute-start.36 = (bf16[224,512]{1,0:T(8,128)(2,1)S(1)}, bf16[224,512]{1,0:T(8,128)(2,1)S(1)}, u32[]{:S(2)}, u32[]{:S(2)}) collective-permute-start(bf16[224,512]{1,0:T(8,128)(2,1)S(1)} %constant_dynamic-update-slice_fusion.20), channel_id=1, source_target_pairs={{0,24},{1,25},{2,26},{3,27},{4,28},{5,29},{6,30},{7,31},{8,16},{9,... | collective-permute-start | bytes 688136 | tf_op jit(solution)/shard_map/ppermute | solution.py:776
  142.2 11.4 %collective-permute-start.35 = (bf16[224,512]{1,0:T(8,128)(2,1)S(1)}, bf16[224,512]{1,0:T(8,128)(2,1)S(1)}, u32[]{:S(2)}, u32[]{:S(2)}) collective-permute-start(bf16[224,512]{1,0:T(8,128)(2,1)S(1)} %constant_dynamic-update-slice_fusion.20), channel_id=1, source_target_pairs={{0,8},{1,9},{2,10},{3,11},{4,12},{5,13},{6,14},{7,15},{8,0},{9,1},... | collective-permute-start | bytes 688136 | tf_op jit(solution)/shard_map/ppermute | solution.py:776
  142.7 10.9 %collective-permute-start.34 = (bf16[224,512]{1,0:T(8,128)(2,1)S(1)}, bf16[224,512]{1,0:T(8,128)(2,1)S(1)}, u32[]{:S(2)}, u32[]{:S(2)}) collective-permute-start(bf16[224,512]{1,0:T(8,128)(2,1)S(1)} %constant_dynamic-update-slice_fusion.20), channel_id=1, source_target_pairs={{0,16},{1,17},{2,18},{3,19},{4,20},{5,21},{6,22},{7,23},{8,24},{9,... | collective-permute-start | bytes 688136 | tf_op jit(solution)/shard_map/ppermute | solution.py:776
  (41 other events, 397.3 us)
